TPU v7x, 32 devices: a whole 2x2x4 slice. The times are simulated.
32 devices in a mesh: ctx: 16 (over z, y, x), head: 2 (over core).
Axes of the slice: x: 2, y: 2, z: 4, core: 2. Of those that a mesh axis runs over, the one named last changes fastest.
Arguments:
- queries: bfloat16 [4096, 4096], P('ctx', 'head'), may hold values from -200 to 200
- span_keys: bfloat16 [4096, 4096], P('ctx', 'head'), may hold values from -6 to 6
- span_values: bfloat16 [4096, 4096], P('ctx', 'head'), may hold values from -96 to 96
- cache_keys: bfloat16 [16384, 4096], P('ctx', 'head'), may hold values from -6 to 6
- cache_values: bfloat16 [16384, 4096], P('ctx', 'head'), may hold values from -96 to 96
- land_keys: bfloat16 [256, 4096], P('ctx', 'head'), may hold values from -4.5 to 4.5
- land_values: bfloat16 [256, 4096], P('ctx', 'head'), may hold values from -96 to 96
- out_weight: bfloat16 [4096, 4096], P('head', 'ctx'), may hold values from -0.09375 to 0.09375
- selection: int32 [64, 32, 4], P('ctx', 'head'), may hold values from 0 to 255, as said below
Outputs:
- projected: bfloat16 [4096, 4096], P('ctx', 'head')
Inputs may be any that keep to these rules, and one draw needn't show every extreme that they name: `selection`: the 4 blocks of one query group and head are distinct. Count block b as owned by ctx index b // 16. Over all groups and heads of one device (one index of ctx and one of head), the selections within one owner's blocks number at most 32 and form at most 8 distinct pairs of block and head; some owner receives exactly that many of both from every device.
All inputs are finite; a program needn't handle non-finite values.
Results may differ from a plain program's by a relative error of at most 0.015.
Values may be sent and summed in bfloat16 or wider, within the bound.
No kernel may reach another device: no remote copies, remote signals or barrier semaphores. Data moves between devices by JAX's collectives and lax.ppermute only.
A program may use at most 128 MiB of HBM per device.

v0:
```python
import math

import jax
import jax.numpy as jnp
from jax import lax
from jax.sharding import PartitionSpec as P

BLOCK = 64


def local(
    queries,
    span_keys,
    span_values,
    cache_keys,
    cache_values,
    land_keys,
    land_values,
    out_weight,
    selection,
):
    query_rows, row_width = queries.shape
    groups, head_dev, pick_count = selection.shape
    head_size = row_width // head_dev
    blocks_dev = cache_keys.shape[0] // BLOCK
    devices = lax.axis_size("ctx")
    scaling = 1.0 / math.sqrt(head_size)
    query_heads = queries.reshape(query_rows, head_dev, head_size)
    run_max = jnp.full((head_dev, query_rows), -jnp.inf, jnp.float32)
    run_sum = jnp.zeros((head_dev, query_rows), jnp.float32)
    run_acc = jnp.zeros((head_dev, query_rows, head_size), jnp.float32)
    key_piece = lax.all_gather(land_keys, "ctx", axis=0, tiled=True).reshape(
        -1, head_dev, head_size
    )
    value_piece = lax.all_gather(land_values, "ctx", axis=0, tiled=True).reshape(
        -1, head_dev, head_size
    )
    scores = (
        jnp.einsum("qhd,nhd->hqn", query_heads, key_piece, preferred_element_type=jnp.float32)
        * scaling
    )
    new_max = jnp.max(scores, axis=2)
    weights = jnp.exp(scores - new_max[:, :, None])
    factor = jnp.exp(run_max - new_max)
    new_sum = run_sum * factor + jnp.sum(weights, axis=2)
    new_acc = run_acc * factor[:, :, None] + jnp.einsum(
        "hqn,nhd->hqd",
        weights.astype(jnp.bfloat16),
        value_piece,
        preferred_element_type=jnp.float32,
    )
    request_count = groups * head_dev * pick_count
    owners_flat = (selection // blocks_dev).reshape(request_count)
    block_flat = (selection % blocks_dev).reshape(request_count)
    head_flat = jnp.broadcast_to(
        jnp.arange(head_dev, dtype=jnp.int32)[None, :, None], selection.shape
    ).reshape(request_count)
    request_order = jnp.arange(request_count)
    earlier = request_order[None, :] < request_order[:, None]
    same_owner = owners_flat[:, None] == owners_flat[None, :]
    distinct_most = (head_dev * 2 * pick_count + devices - 1) // devices
    key_blocks = cache_keys.reshape(blocks_dev, BLOCK, head_dev, head_size)
    value_blocks = cache_values.reshape(blocks_dev, BLOCK, head_dev, head_size)
    asked_pairs = jnp.stack([block_flat, head_flat], axis=1)
    pair_ids = selection.reshape(request_count) * head_dev + head_flat
    same_pair = pair_ids[:, None] == pair_ids[None, :]
    is_first = jnp.logical_not(jnp.any(same_pair & earlier, axis=1))
    first_rank = jnp.sum(same_owner & earlier & is_first[None, :], axis=1)
    slot_ids = jnp.sum(jnp.where(same_pair & is_first[None, :], first_rank[None, :], 0), axis=1)
    wanted = (
        jnp.zeros((devices, distinct_most, 2), jnp.int32).at[owners_flat, slot_ids].set(asked_pairs)
    )
    asked_for = lax.all_to_all(wanted, "ctx", split_axis=0, concat_axis=0, tiled=True)
    sent_keys = key_blocks[asked_for[:, :, 0], :, asked_for[:, :, 1], :]
    sent_values = value_blocks[asked_for[:, :, 0], :, asked_for[:, :, 1], :]
    fetched_keys = lax.all_to_all(sent_keys, "ctx", split_axis=0, concat_axis=0, tiled=True)
    fetched_values = lax.all_to_all(sent_values, "ctx", split_axis=0, concat_axis=0, tiled=True)
    owner_grid = owners_flat.reshape(selection.shape)
    slot_grid = slot_ids.reshape(selection.shape)
    chosen_keys = fetched_keys[owner_grid, slot_grid]
    chosen_values = fetched_values[owner_grid, slot_grid].reshape(
        groups, head_dev, pick_count * BLOCK, head_size
    )
    query_groups = query_heads.reshape(groups, BLOCK, head_dev, head_size)
    chosen_scores = (
        jnp.einsum(
            "gqhd,ghpkd->ghqpk", query_groups, chosen_keys, preferred_element_type=jnp.float32
        )
        * scaling
    )
    chosen_scores = chosen_scores.reshape(groups, head_dev, BLOCK, pick_count * BLOCK)
    local_keys = span_keys.reshape(groups, BLOCK, head_dev, head_size)
    local_values = span_values.reshape(groups, BLOCK, head_dev, head_size)
    causal = jnp.arange(BLOCK)[:, None] >= jnp.arange(BLOCK)[None, :]
    local_scores = (
        jnp.einsum("gqhd,gkhd->ghqk", query_groups, local_keys, preferred_element_type=jnp.float32)
        * scaling
    )
    local_scores = jnp.where(causal[None, None], local_scores, -jnp.inf)
    land_top = jnp.transpose(new_max.reshape(head_dev, groups, BLOCK), (1, 0, 2))
    land_total = jnp.transpose(new_sum.reshape(head_dev, groups, BLOCK), (1, 0, 2))
    land_part = jnp.transpose(new_acc.reshape(head_dev, groups, BLOCK, head_size), (1, 0, 2, 3))
    overall_top = jnp.maximum(
        jnp.maximum(land_top, jnp.max(chosen_scores, axis=3)), jnp.max(local_scores, axis=3)
    )
    land_weight = jnp.exp(land_top - overall_top)
    chosen_weights = jnp.exp(chosen_scores - overall_top[..., None])
    local_weights = jnp.exp(local_scores - overall_top[..., None])
    denominator = (
        land_total * land_weight + jnp.sum(chosen_weights, axis=3) + jnp.sum(local_weights, axis=3)
    )
    numerator = land_part * land_weight[..., None]
    numerator = numerator + jnp.einsum(
        "ghqn,ghnd->ghqd",
        chosen_weights.astype(jnp.bfloat16),
        chosen_values,
        preferred_element_type=jnp.float32,
    )
    numerator = numerator + jnp.einsum(
        "ghqk,gkhd->ghqd",
        local_weights.astype(jnp.bfloat16),
        local_values,
        preferred_element_type=jnp.float32,
    )
    attended = (numerator / denominator[..., None]).astype(jnp.bfloat16)
    attended = jnp.transpose(attended, (0, 2, 1, 3)).reshape(query_rows, row_width)
    partial_out = jnp.dot(
        attended,
        lax.all_gather(out_weight, "ctx", axis=1, tiled=True),
        preferred_element_type=jnp.float32,
    )
    summed = lax.psum_scatter(
        partial_out.astype(jnp.bfloat16), "head", scatter_dimension=1, tiled=True
    )
    return summed


def solution(mesh):
    placed = (
        P("ctx", "head"),
        P("ctx", "head"),
        P("ctx", "head"),
        P("ctx", "head"),
        P("ctx", "head"),
        P("ctx", "head"),
        P("ctx", "head"),
        P("head", "ctx"),
        P("ctx", "head", None),
    )
    return jax.shard_map(
        local, mesh=mesh, in_specs=placed, out_specs=P("ctx", "head"), check_vma=False
    )
```

profile of v0, /device:TPU:0, one launch (start us, length us, event | category | flops | bytes accessed | tf_op | source)
XLA Modules:
  0.0 416.5 jit_solution(2511548139788343026)
XLA Ops:
  6.5 0.7 all-gather.4.cloned.1.call-update
  7.3 0.7 all-gather.6.cloned.1.call-update
  8.1 0.7 all-gather.8.cloned.1.call-update
  8.7 0.8 copy.133
  9.9 0.2 fusion.34
  10.1 0.1 stack_reshape.4
  10.3 0.1 copy.138
  10.5 0.2 convert_reduce_fusion
  10.7 0.2 select_reduce_fusion
  10.9 11.7 %scatter_fusion = s32[16,8,2]{2,1,0:T(8,128)S(1)} fusion(s32[16,8,2]{2,1,0:T(8,128)S(1)} %broadcast_in_dim.38, s32[256]{0:T(256)S(1)} %bitcast.109, s32[256,2]{1,0:T(8,128)S(1)} %copy.138), kind=kCustom, calls=%fused_computation.4 | custom fusion | bytes 8192 | tf_op jit(solution)/shard_map/scatter | solution.py:71
  22.6 0.8 copy.139
  23.3 8.4 %all-to-all-start = ((s32[16,8,2]{1,2,0:T(2,128)}), s32[16,8,2]{1,2,0:T(2,128)S(1)}, u32[]{:S(2)}, u32[]{:S(2)}) async-start(s32[16,8,2]{1,2,0:T(2,128)} %copy.139), calls=%async_computation | async-start | bytes 32768 | tf_op jit(solution)/shard_map/all_to_all | solution.py:73
  31.7 3.6 copy.160
  35.3 3.0 copy.140
  38.3 0.7 all-to-all-done
  39.2 4.5 %gather_fusion = bf16[128,64,128]{2,1,0:T(8,128)(2,1)} fusion(bf16[16,64,16,128]{3,1,2,0:T(8,128)(2,1)} %copy.140, s32[128]{0:T(128)S(1)} %reshape.182), kind=kCustom, calls=%fused_computation | custom fusion | bytes 4195328 | tf_op jit(solution)/shard_map/gather | solution.py:74
  43.7 6.2 %all-to-all-start.1 = ((bf16[16,8,64,128]{3,2,1,0:T(8,128)(2,1)}), bf16[16,8,64,128]{3,2,1,0:T(8,128)(2,1)S(1)}, u32[]{:S(2)}, u32[]{:S(2)}) async-start(bf16[16,8,64,128]{3,2,1,0:T(8,128)(2,1)} %bitcast.114), calls=%async_computation.1 | async-start | bytes 4194304 | tf_op jit(solution)/shard_map/all_to_all | solution.py:76
  49.9 3.6 copy.163
  53.5 3.0 copy.146
  56.5 4.6 %gather_fusion.2 = bf16[128,64,128]{2,1,0:T(8,128)(2,1)} fusion(bf16[16,64,16,128]{3,1,2,0:T(8,128)(2,1)} %copy.146, s32[128]{0:T(128)S(1)} %reshape.182), kind=kCustom, calls=%fused_computation.2 | custom fusion | bytes 4195328 | tf_op jit(solution)/shard_map/gather | solution.py:75
  61.1 37.9 %all-to-all-done.1 = bf16[16,8,64,128]{3,2,1,0:T(8,128)(2,1)S(1)} async-done(((bf16[16,8,64,128]{3,2,1,0:T(8,128)(2,1)}), bf16[16,8,64,128]{3,2,1,0:T(8,128)(2,1)S(1)}, u32[]{:S(2)}, u32[]{:S(2)}) %all-to-all-start.1) | async-done | bytes 2097184 | tf_op jit(solution)/shard_map/all_to_all | solution.py:76
  99.0 10.5 %all-to-all-start.2 = ((bf16[16,8,64,128]{3,2,1,0:T(8,128)(2,1)}), bf16[16,8,64,128]{3,2,1,0:T(8,128)(2,1)}, u32[]{:S(2)}, u32[]{:S(2)}) async-start(bf16[16,8,64,128]{3,2,1,0:T(8,128)(2,1)} %bitcast.113), calls=%async_computation.2 | async-start | bytes 4194304 | tf_op jit(solution)/shard_map/all_to_all | solution.py:77
  109.8 0.2 copy.161
  110.1 1.5 copy.162
  111.6 1.2 copy.164
  112.9 0.2 bitcast_bitcast_fusion
  113.0 2.1 fusion.12
  115.2 2.3 copy.125
  117.4 4.2 %multiply_reduce_fusion = (f32[16,256]{1,0:T(8,128)S(1)}, f32[16,256,256]{1,2,0:T(8,128)}) fusion(bf16[256,16,128]{0,2,1:T(8,128)(2,1)} %bitcast.121, bf16[256,2048]{1,0:T(8,128)(2,1)} %param.9), kind=kOutput, calls=%fused_computation.13 | convolution fusion | flops 270528512 | bytes 6307840 | tf_op jit(solution)/shard_map/qhd,nhd->hqn/dot_general | solution.py:39
  121.7 2.9 fusion.2
  124.7 27.3 %all-gather.6.cloned.1.call-done = bf16[256,2048]{1,0:T(8,128)(2,1)} async-done(((bf16[16,2048]{1,0:T(8,128)(2,1)}), bf16[256,2048]{1,0:T(8,128)(2,1)}) %all-gather.6.cloned.1.call-update) | async-done | bytes 1048592 | tf_op jit(solution)/shard_map/all_gather | solution.py:35
  152.0 2.3 copy.128
  154.3 5.2 %fusion.13 = f32[16,256,128]{2,1,0:T(8,128)} fusion(bf16[256,16,128]{0,2,1:T(8,128)(2,1)} %bitcast.115, f32[16,256,256]{1,2,0:T(8,128)} %get-tuple-element.15, f32[16,256]{1,0:T(8,128)S(1)} %get-tuple-element.14, f32[16,256]{1,0:T(8,128)S(1)} %exponential_multiply_fusion), kind=kOutput, calls=%fused_computation.29 | convolution fusion | flops 272105472 | bytes 7372800 | tf_op jit(solution)/shard_map/hqn,nhd->hqd/dot_general | solution.py:46
  159.5 3.4 gather_fusion.1
  162.9 7.2 %bitcast_reduce_fusion = (f32[4,16,64]{2,1,0:T(8,128)S(1)}, f32[4,16,4,64,64]{4,3,2,1,0:T(8,128)}) fusion(bf16[4,16,4,64,128]{4,3,2,1,0:T(8,128)(2,1)} %bitcast.108, bf16[4,64,16,128,1]{3,2,1,0,4:T(8,128)(2,1)S(1)} %bitcast_bitcast_fusion), kind=kOutput, calls=%fused_computation.6 | convolution fusion | flops 270528512 | bytes 9453568 | tf_op jit(solution)/shard_map/gqhd,ghpkd->ghqpk/dot_general | solution.py:86
  170.1 6.8 %copy.145 = f32[4,16,64,256]{3,2,1,0:T(8,128)} copy(f32[4,16,64,256]{2,3,1,0:T(8,128)} %bitcast.107) | data formatting | bytes 8388608 | tf_op jit(solution)/shard_map/reshape | solution.py:91
  176.9 5.1 %gather_fusion.3 = bf16[256,64,128]{2,1,0:T(8,128)(2,1)} fusion(bf16[16,8,64,128]{3,2,1,0:T(8,128)(2,1)} %all-to-all-done.2, s32[256]{0:T(256)S(1)} %reshape.188), kind=kCustom, calls=%fused_computation.3 | custom fusion | bytes 8390656 | tf_op jit(solution)/shard_map/gather | solution.py:81
  182.0 0.7 fusion.16
  182.7 5.5 %fusion.1 = f32[4,16,64]{2,1,0:T(8,128)S(1)} fusion(f32[4,16,4,64,64]{4,3,2,1,0:T(8,128)} %get-tuple-element.13, f32[4,16,64]{2,1,0:T(8,128)S(1)} %fusion.42), kind=kLoop, calls=%fused_computation.8 | loop fusion | flops 2093056 | bytes 4227072 | tf_op jit(solution)/shard_map/reduce_sum | solution.py:110
  188.2 0.4 copy-done.1
  188.6 1.2 fusion.6
  189.8 0.4 copy-done.3
  190.2 0.3 copy-done.6
  190.5 2.0 fusion.8
  192.5 0.7 copy.151
  193.2 197.3 %all-gather.8.cloned.1.call-done = bf16[2048,4096]{1,0:T(8,128)(2,1)} async-done(((bf16[2048,256]{1,0:T(8,128)(2,1)}), bf16[2048,4096]{1,0:T(8,128)(2,1)}) %all-gather.8.cloned.1.call-update) | async-done | bytes 16777232 | tf_op jit(solution)/shard_map/all_gather | solution.py:129
  390.4 11.5 %convolution_convert_fusion = bf16[256,4096]{1,0:T(8,128)(2,1)} fusion(bf16[2048,4096]{1,0:T(8,128)(2,1)} %all-gather.8.cloned.1.call-done, bf16[32,8,16,128]{3,2,1,0:T(8,128)(2,1)S(1)} %bitcast.127), kind=kOutput, calls=%fused_computation.9 | convolution fusion | flops 4296015872 | bytes 19922944 | tf_op jit(solution)/shard_map/dot_general | solution.py:127
  402.0 8.0 %reduce-scatter.2.cloned.1.call-done = bf16[256,2048]{1,0:T(8,128)(2,1)} async-done(((bf16[256,4096]{1,0:T(8,128)(2,1)}), bf16[256,2048]{1,0:T(8,128)(2,1)}) %reduce-scatter.2.cloned.1.call-update) | async-done | bytes 1048592 | tf_op jit(solution)/shard_map/reduce_scatter | solution.py:132
  (39 shorter events, 1.3 us)
Async XLA Ops:
  6.5 108.6 %all-gather.4.cloned.1.call-start = ((), (), s32[]{:S(2)}) async-start(), calls=%async_computation.4 | async-start | bytes 1114112 | tf_op jit(solution)/shard_map/all_gather | solution.py:32
  7.3 144.8 %all-gather.6.cloned.1.call-start = ((), (), s32[]{:S(2)}) async-start(), calls=%async_computation.5 | async-start | bytes 1114112 | tf_op jit(solution)/shard_map/all_gather | solution.py:35
  8.0 382.4 %all-gather.8.cloned.1.call-start = ((), (), s32[]{:S(2)}) async-start(), calls=%async_computation.6 | async-start | bytes 17825792 | tf_op jit(solution)/shard_map/all_gather | solution.py:129
  23.3 15.7 %all-to-all-start = ((s32[16,8,2]{1,2,0:T(2,128)}), s32[16,8,2]{1,2,0:T(2,128)S(1)}, u32[]{:S(2)}, u32[]{:S(2)}) async-start(s32[16,8,2]{1,2,0:T(2,128)} %copy.139), calls=%async_computation | async-start | bytes 32768 | tf_op jit(solution)/shard_map/all_to_all | solution.py:73
  43.7 55.3 %all-to-all-start.1 = ((bf16[16,8,64,128]{3,2,1,0:T(8,128)(2,1)}), bf16[16,8,64,128]{3,2,1,0:T(8,128)(2,1)S(1)}, u32[]{:S(2)}, u32[]{:S(2)}) async-start(bf16[16,8,64,128]{3,2,1,0:T(8,128)(2,1)} %bitcast.114), calls=%async_computation.1 | async-start | bytes 4194304 | tf_op jit(solution)/shard_map/all_to_all | solution.py:76
  56.5 53.3 %copy-start.2 = (bf16[256,2048]{1,0:T(8,128)(2,1)S(1)}, bf16[256,2048]{1,0:T(8,128)(2,1)}, u32[]{:S(2)}) copy-start(bf16[256,2048]{1,0:T(8,128)(2,1)} %param.9) | copy-start | bytes 3145732
  99.0 77.9 %all-to-all-start.2 = ((bf16[16,8,64,128]{3,2,1,0:T(8,128)(2,1)}), bf16[16,8,64,128]{3,2,1,0:T(8,128)(2,1)}, u32[]{:S(2)}, u32[]{:S(2)}) async-start(bf16[16,8,64,128]{3,2,1,0:T(8,128)(2,1)} %bitcast.113), calls=%async_computation.2 | async-start | bytes 4194304 | tf_op jit(solution)/shard_map/all_to_all | solution.py:77
  109.5 300.5 %reduce-scatter.2.cloned.1.call-start = ((), (), s32[]{:S(2)}) async-start(), calls=%async_computation.7 | async-start | bytes 3145728 | tf_op jit(solution)/shard_map/reduce_scatter | solution.py:132
  109.8 1.8 copy-start.5
  176.9 5.1 %copy-start.4 = (f32[4,16,64,64]{2,3,1,0:T(8,128)S(1)}, f32[4,16,64,64]{2,3,1,0:T(8,128)}, u32[]{:S(2)}) copy-start(f32[4,16,64,64]{2,3,1,0:T(8,128)} %get-tuple-element.11) | copy-start | bytes 3145732
  182.7 5.5 %copy-start = (f32[4,16,64,256]{3,2,1,0:T(8,128)S(1)}, f32[4,16,64,256]{3,2,1,0:T(8,128)}, u32[]{:S(2)}) copy-start(f32[4,16,64,256]{3,2,1,0:T(8,128)} %copy.145) | copy-start | bytes 12582916
  182.7 5.9 %copy-start.1 = (bf16[256,64,128]{2,1,0:T(8,128)(2,1)S(1)}, bf16[256,64,128]{2,1,0:T(8,128)(2,1)}, u32[]{:S(2)}) copy-start(bf16[256,64,128]{2,1,0:T(8,128)(2,1)} %gather_fusion.3) | copy-start | bytes 12582916
  188.6 1.6 copy-start.3
  188.6 1.9 copy-start.6
Sparse Core Ops, SparseCore 0:
  10.1 65.9 all-gather.3
  78.8 73.1 all-gather.5
  154.8 235.6 all-gather.7
  402.1 7.8 reduce-scatter.1
where the time goes:
time: 417 us
  waiting for transfers between devices  273 us (65%)
  local copies, waits for them, and re-layouts  61.3 us (15%)
  matrix products  33.5 us (8%)
  starting transfers between devices  25.2 us (6%)
  between operations  13.4 us (3%)
  other arithmetic  9.83 us (2%)
    all_gather x1, waiting for transfers between devices, local(): lax.all_gather(out_weight, 'ctx', axis=1, tiled=True)  197 us
    all_to_all x1, waiting for transfers between devices, local(): lax.all_to_all(sent_keys, 'ctx', split_axis=0, concat_axis=0, tiled=True)  37.9 us
    all_gather x1, waiting for transfers between devices, local(): lax.all_gather(land_values, 'ctx', axis=0, tiled=True)  27.3 us
    scatter x2, local copies, waits for them, and re-layouts, local(): jnp.zeros((devices, distinct_most, 2), jnp.int32).at[owners_flat, slot_ids]  12.4 us
    unnamed x20, local copies, waits for them, and re-layouts  12 us
    dot_general x1, matrix products, local(): jnp.dot(attended, lax.all_gather(out_weight, 'ctx', axis=1, tiled=True),...  11.5 us
    all_to_all x1, starting transfers between devices, local(): lax.all_to_all(sent_values, 'ctx', split_axis=0, concat_axis=0, tiled=True)  10.5 us
    all_to_all x1, starting transfers between devices, local(): lax.all_to_all(wanted, 'ctx', split_axis=0, concat_axis=0, tiled=True)  8.35 us
  transfers between devices with their start and end apart: 7, of which 5 were waited for; matrix products, arithmetic and copies ran while one was open for 22% of the time, Pallas kernels for 0%

commit v1 on v0

v1 whole, which is shorter than its diff:
```python
import functools
import math

import jax
import jax.numpy as jnp
from jax import lax
from jax.experimental import pallas as pl
from jax.experimental.pallas import tpu as pltpu
from jax.sharding import PartitionSpec as P

BLOCK = 64
ANY = pl.BlockSpec(memory_space=pl.ANY)
VMEM = pl.BlockSpec(memory_space=pltpu.VMEM)
SMEM = pl.BlockSpec(memory_space=pltpu.SMEM)
LIMIT = 60 * 1024 * 1024


def split_ctx(devices, head_devices):
    fast = 1
    while (
        (2 * fast) ** 2 <= devices
        and devices % (2 * fast) == 0
        and (devices // (2 * fast)) % head_devices == 0
    ):
        fast *= 2
    return devices // fast, fast


def exchange_tables(selection, blocks_dev, devices):
    groups, heads, picks = selection.shape
    count = groups * heads * picks
    most = (heads * 2 * picks + devices - 1) // devices
    head = lax.broadcasted_iota(jnp.int32, selection.shape, 1)
    owner = (selection // blocks_dev).reshape(count)
    code = ((selection % blocks_dev) * heads + head).reshape(count)
    pair = (selection * heads + head).reshape(count)
    order = jnp.arange(count)
    earlier = order[None, :] < order[:, None]
    same_pair = pair[:, None] == pair[None, :]
    same_owner = owner[:, None] == owner[None, :]
    first = jnp.logical_not(jnp.any(same_pair & earlier, axis=1))
    rank = jnp.sum((same_owner & earlier & first[None, :]).astype(jnp.int32), axis=1)
    slot = jnp.sum(jnp.where(same_pair & first[None, :], rank[None, :], 0), axis=1)
    cell = owner * most + slot
    cells = jnp.arange(devices * most)
    asked = jnp.sum(
        jnp.where((cells[:, None] == cell[None, :]) & first[None, :], code[None, :], 0), axis=1
    )
    return cell, asked.reshape(devices, most)


def gather_kernel(heads, asked_ref, source_ref, out_ref, sem):
    size = out_ref.shape[2]

    def start(cell, carry):
        code = asked_ref[cell]
        row = pl.multiple_of(lax.div(code, heads) * BLOCK, BLOCK)
        column = pl.multiple_of(lax.rem(code, heads) * size, size)
        pltpu.make_async_copy(
            source_ref.at[pl.ds(row, BLOCK), pl.ds(column, size)], out_ref.at[cell], sem
        ).start()
        return carry

    lax.fori_loop(0, out_ref.shape[0], start, 0)
    pltpu.make_async_copy(out_ref, out_ref, sem).wait()


def gather_blocks(asked, source, heads):
    cells = asked.shape[0]
    size = source.shape[1] // heads
    return pl.pallas_call(
        functools.partial(gather_kernel, heads),
        out_shape=jax.ShapeDtypeStruct((cells, BLOCK, size), source.dtype),
        in_specs=[SMEM, ANY],
        out_specs=VMEM,
        scratch_shapes=[pltpu.SemaphoreType.DMA],
        cost_estimate=pl.CostEstimate(
            flops=cells * BLOCK * size * 64,
            bytes_accessed=4 * cells * BLOCK * size,
            transcendentals=0,
        ),
        name="gather_blocks",
    )(asked, source)


def nt_dot(a, b):
    return lax.dot_general(a, b, (((1,), (1,)), ((), ())), preferred_element_type=jnp.float32)


def score_kernel(
    groups, heads, picks, step_heads, cell_ref, q_ref, land_ref, lk_ref, lv_ref, fk_ref,
    weight_ref, acc_ref,
):
    size = q_ref.shape[1] // step_heads
    scaling = 1.0 / math.sqrt(size)
    first_head = pl.program_id(0) * step_heads
    row = lax.broadcasted_iota(jnp.int32, (BLOCK, BLOCK), 0)
    column = lax.broadcasted_iota(jnp.int32, (BLOCK, BLOCK), 1)
    causal = row >= column
    pieces, _, land_rows, _ = land_ref.shape
    chosen = picks * BLOCK
    for hh in range(step_heads):
        cols = slice(hh * size, (hh + 1) * size)
        land_k = land_ref[:, 0, :, cols].reshape(pieces * land_rows, size)
        land_v = land_ref[:, 1, :, cols].reshape(pieces * land_rows, size)
        for g in range(groups):
            rows = slice(g * BLOCK, (g + 1) * BLOCK)
            q = q_ref[rows, cols]
            base = (g * heads + first_head + hh) * picks
            keys = jnp.concatenate([fk_ref[cell_ref[base + p]] for p in range(picks)], axis=0)
            s_land = nt_dot(q, land_k) * scaling
            s_chosen = nt_dot(q, keys) * scaling
            s_local = jnp.where(causal, nt_dot(q, lk_ref[rows, cols]) * scaling, -jnp.inf)
            top = jnp.maximum(
                jnp.maximum(
                    jnp.max(s_land, axis=1, keepdims=True),
                    jnp.max(s_chosen, axis=1, keepdims=True),
                ),
                jnp.max(s_local, axis=1, keepdims=True),
            )
            w_land = jnp.exp(s_land - top)
            w_chosen = jnp.exp(s_chosen - top)
            w_local = jnp.exp(s_local - top)
            total = (
                jnp.sum(w_land, axis=1, keepdims=True)
                + jnp.sum(w_chosen, axis=1, keepdims=True)
                + jnp.sum(w_local, axis=1, keepdims=True)
            )
            inverse = 1.0 / total
            part = jnp.dot(
                w_land.astype(jnp.bfloat16), land_v, preferred_element_type=jnp.float32
            ) + jnp.dot(
                w_local.astype(jnp.bfloat16), lv_ref[rows, cols], preferred_element_type=jnp.float32
            )
            acc_ref[rows, cols] = part * inverse
            weight_ref[rows, hh * chosen : (hh + 1) * chosen] = (w_chosen * inverse).astype(
                jnp.bfloat16
            )


def value_kernel(groups, heads, picks, step_heads, cell_ref, weight_ref, acc_ref, fv_ref, out_ref):
    size = acc_ref.shape[1] // step_heads
    first_head = pl.program_id(0) * step_heads
    chosen = picks * BLOCK
    for hh in range(step_heads):
        cols = slice(hh * size, (hh + 1) * size)
        for g in range(groups):
            rows = slice(g * BLOCK, (g + 1) * BLOCK)
            base = (g * heads + first_head + hh) * picks
            values = jnp.concatenate([fv_ref[cell_ref[base + p]] for p in range(picks)], axis=0)
            out_ref[rows, cols] = (
                acc_ref[rows, cols]
                + jnp.dot(
                    weight_ref[rows, hh * chosen : (hh + 1) * chosen],
                    values,
                    preferred_element_type=jnp.float32,
                )
            ).astype(out_ref.dtype)


def attention_scores(cell, queries, land, span_keys, span_values, fetched_keys, dims):
    groups, heads, picks = dims
    rows, width = queries.shape
    size = width // heads
    step = math.gcd(heads, 4)
    wide = step * size
    chosen = picks * BLOCK
    by_head = lambda i, c: (0, i)
    keys = land.shape[0] * land.shape[2] + chosen + BLOCK
    return pl.pallas_call(
        functools.partial(score_kernel, groups, heads, picks, step),
        grid_spec=pltpu.PrefetchScalarGridSpec(
            num_scalar_prefetch=1,
            grid=(heads // step,),
            in_specs=[
                pl.BlockSpec((rows, wide), by_head),
                pl.BlockSpec(land.shape[:3] + (wide,), lambda i, c: (0, 0, 0, i)),
                pl.BlockSpec((rows, wide), by_head),
                pl.BlockSpec((rows, wide), by_head),
                pl.BlockSpec(fetched_keys.shape, lambda i, c: (0, 0, 0)),
            ],
            out_specs=[
                pl.BlockSpec((rows, step * chosen), by_head),
                pl.BlockSpec((rows, wide), by_head),
            ],
        ),
        out_shape=[
            jax.ShapeDtypeStruct((rows, heads * chosen), jnp.bfloat16),
            jax.ShapeDtypeStruct((rows, width), jnp.float32),
        ],
        compiler_params=pltpu.CompilerParams(vmem_limit_bytes=LIMIT),
        cost_estimate=pl.CostEstimate(
            flops=16 * rows * keys * width,
            bytes_accessed=16 * rows * width,
            transcendentals=rows * keys * heads,
        ),
        name="attention_scores",
    )(cell, queries, land, span_keys, span_values, fetched_keys)


def attention_values(cell, weights, part, fetched_values, dims):
    groups, heads, picks = dims
    rows, width = part.shape
    size = width // heads
    step = math.gcd(heads, 4)
    wide = step * size
    chosen = picks * BLOCK
    by_head = lambda i, c: (0, i)
    return pl.pallas_call(
        functools.partial(value_kernel, groups, heads, picks, step),
        grid_spec=pltpu.PrefetchScalarGridSpec(
            num_scalar_prefetch=1,
            grid=(heads // step,),
            in_specs=[
                pl.BlockSpec((rows, step * chosen), by_head),
                pl.BlockSpec((rows, wide), by_head),
                pl.BlockSpec(fetched_values.shape, lambda i, c: (0, 0, 0)),
            ],
            out_specs=pl.BlockSpec((rows, wide), by_head),
        ),
        out_shape=jax.ShapeDtypeStruct((rows, width), jnp.bfloat16),
        compiler_params=pltpu.CompilerParams(vmem_limit_bytes=LIMIT),
        cost_estimate=pl.CostEstimate(
            flops=4 * rows * chosen * width,
            bytes_accessed=12 * rows * width,
            transcendentals=0,
        ),
        name="attention_values",
    )(cell, weights, part, fetched_values)


def project_kernel(slow_count, head_devices, pieces, place_ref, *refs):
    a_refs, b_refs = refs[:pieces], refs[pieces : pieces + 2 * slow_count - 1]
    mine_ref, send_ref, b_buf, sem = refs[pieces + 2 * slow_count - 1 :]
    slow, head = place_ref[0], place_ref[1]
    share = slow_count // head_devices
    width = b_buf.shape[2]
    for slot in range(slow_count):
        target = lax.rem(head + slot // share, head_devices) * share + slot % share
        for index in range(2 * slow_count - 1):

            @pl.when(target - slow == index - (slow_count - 1))
            def _():
                pltpu.make_async_copy(b_refs[index], b_buf.at[slot], sem.at[slot]).start()

    for slot in range(slow_count):
        pltpu.make_async_copy(b_refs[0], b_buf.at[slot], sem.at[slot]).wait()
        row = 0
        for a_ref in a_refs:
            rows = slice(row, row + a_ref.shape[0])
            row += a_ref.shape[0]
            product = jnp.dot(a_ref[...], b_buf[slot], preferred_element_type=jnp.float32)
            if slot < share:
                mine_ref[rows, slot * width : (slot + 1) * width] = product
            else:
                other = slot - share
                send_ref[
                    other // share, rows, (other % share) * width : (other % share + 1) * width
                ] = product.astype(send_ref.dtype)


def project(place, a_pieces, b_blocks, slow_count, head_devices):
    rows = sum(a.shape[0] for a in a_pieces)
    depth, width = b_blocks[0].shape
    share = slow_count // head_devices
    return pl.pallas_call(
        functools.partial(project_kernel, slow_count, head_devices, len(a_pieces)),
        out_shape=[
            jax.ShapeDtypeStruct((rows, share * width), jnp.float32),
            jax.ShapeDtypeStruct((head_devices - 1, rows, share * width), jnp.bfloat16),
        ],
        in_specs=[SMEM] + [VMEM] * len(a_pieces) + [ANY] * len(b_blocks),
        out_specs=[VMEM, VMEM],
        scratch_shapes=[
            pltpu.VMEM((slow_count, depth, width), jnp.bfloat16),
            pltpu.SemaphoreType.DMA((slow_count,)),
        ],
        compiler_params=pltpu.CompilerParams(vmem_limit_bytes=LIMIT),
        cost_estimate=pl.CostEstimate(
            flops=2 * rows * depth * width * slow_count,
            bytes_accessed=2 * depth * width * slow_count,
            transcendentals=0,
        ),
        name="project",
    )(place, *a_pieces, *b_blocks)


def assemble_kernel(fast_count, share, others, place_ref, mine_ref, *refs):
    received, tiles, out_ref = refs[:others], refs[others:-1], refs[-1]
    width = mine_ref.shape[1] // share
    for fast in range(fast_count):

        @pl.when(place_ref[2] == fast)
        def _():
            for mask in range(fast_count):
                for block in range(share):
                    cols = slice(block * width, (block + 1) * width)
                    if mask == 0:
                        total = mine_ref[:, cols]
                        for other in received:
                            total = total + other[:, cols].astype(jnp.float32)
                        tile = total.astype(out_ref.dtype)
                    else:
                        tile = tiles[mask - 1][:, cols]
                    start = (block * fast_count + (fast ^ mask)) * width
                    out_ref[:, start : start + width] = tile


def assemble(place, mine, received, tiles, share):
    fast_count = len(tiles) + 1
    rows, wide = mine.shape
    return pl.pallas_call(
        functools.partial(assemble_kernel, fast_count, share, len(received)),
        out_shape=jax.ShapeDtypeStruct((rows, wide * fast_count), jnp.bfloat16),
        in_specs=[SMEM] + [VMEM] * (1 + len(received) + len(tiles)),
        out_specs=VMEM,
        name="assemble",
    )(place, mine, *received, *tiles)


def local(
    queries,
    span_keys,
    span_values,
    cache_keys,
    cache_values,
    land_keys,
    land_values,
    out_weight,
    selection,
):
    rows, width = queries.shape
    groups, heads, picks = selection.shape
    size = width // heads
    devices = lax.axis_size("ctx")
    head_devices = lax.axis_size("head")
    slow_count, fast_count = split_ctx(devices, head_devices)
    share = slow_count // head_devices
    bits = [1 << k for k in range(fast_count.bit_length() - 1)]
    index = lax.axis_index("ctx")
    place = jnp.stack([index // fast_count, lax.axis_index("head"), index % fast_count])
    place = place.astype(jnp.int32)

    def across(value, mask):
        return lax.ppermute(value, "ctx", [(i, i ^ mask) for i in range(devices)])

    def along(value, shift, low=0, high=None):
        high = slow_count if high is None else high
        pairs = [
            (s * fast_count + f, (s + shift) * fast_count + f)
            for s in range(low, high)
            for f in range(fast_count)
            if 0 <= s + shift < slow_count
        ]
        return lax.ppermute(value, "ctx", pairs)

    blocks_dev = cache_keys.shape[0] // BLOCK
    cell, asked = exchange_tables(selection, blocks_dev, devices)
    asked_for = lax.all_to_all(asked, "ctx", split_axis=0, concat_axis=0, tiled=True)
    asked_for = asked_for.reshape(-1)

    below, above = [out_weight], [out_weight]
    if slow_count > 1:
        below.append(along(out_weight, 1))
        above.append(along(out_weight, -1))
    land = jnp.stack([land_keys, land_values])[None]
    land_parts = [land]
    for shift in range(1, slow_count):
        pairs = [
            (s * fast_count + f, (s + shift) % slow_count * fast_count + f)
            for s in range(slow_count)
            for f in range(fast_count)
        ]
        land_parts.append(lax.ppermute(land, "ctx", pairs))
    land = jnp.concatenate(land_parts, axis=0)
    for bit in bits:
        land = jnp.concatenate([land, across(land, bit)], axis=0)

    def fetch(source):
        sent = gather_blocks(asked_for, source, heads).reshape(devices, -1, BLOCK, size)
        got = lax.all_to_all(sent, "ctx", split_axis=0, concat_axis=0, tiled=True)
        return got.reshape(-1, BLOCK, size)

    fetched_keys = fetch(cache_keys)
    fetched_values = fetch(cache_values)

    dims = (groups, heads, picks)
    weights, part = attention_scores(
        cell, queries, land, span_keys, span_values, fetched_keys, dims
    )
    attended = attention_values(cell, weights, part, fetched_values, dims)

    for hop in range(2, slow_count):
        low, high = below[-1], above[-1]
        if hop == 2:
            low, high, _ = lax.optimization_barrier((low, high, fetched_values))
        below.append(along(low, 1, hop - 1, slow_count))
        above.append(along(high, -1, 0, slow_count - hop + 1))
    b_blocks = below[:0:-1] + [out_weight] + above[1:]

    pieces = {0: [attended]}
    for mask in sorted(range(1, fast_count), key=lambda m: (m.bit_count(), m)):
        own = [b for b in bits if b & mask]
        if len(own) == 1:
            pieces[mask] = [across(attended, mask)]
            continue
        edges = [rows * k // len(own) for k in range(len(own) + 1)]
        pieces[mask] = []
        for k, bit in enumerate(own):
            whole = pieces[mask ^ bit]
            whole = whole[0] if len(whole) == 1 else jnp.concatenate(whole, axis=0)
            pieces[mask].append(across(whole[edges[k] : edges[k + 1]], bit))

    tiles = {}
    for mask in [*range(1, fast_count), 0]:
        mine, send = project(place, pieces[mask], b_blocks, slow_count, head_devices)
        received = [
            lax.ppermute(
                send[r - 1], "head", [(h, (h + r) % head_devices) for h in range(head_devices)]
            )
            for r in range(1, head_devices)
        ]
        if mask == 0:
            break
        total = mine
        for other in received:
            total = total + other.astype(jnp.float32)
        tiles[mask] = across(total.astype(jnp.bfloat16), mask)
    return assemble(place, mine, received, [tiles[m] for m in range(1, fast_count)], share)


def solution(mesh):
    placed = (
        P("ctx", "head"),
        P("ctx", "head"),
        P("ctx", "head"),
        P("ctx", "head"),
        P("ctx", "head"),
        P("ctx", "head"),
        P("ctx", "head"),
        P("head", "ctx"),
        P("ctx", "head", None),
    )
    return jax.shard_map(
        local, mesh=mesh, in_specs=placed, out_specs=P("ctx", "head"), check_vma=False
    )
```

time: 417 us -> 277 us (0.66)
  waiting for transfers between devices: 273 us -> 140 us
  Pallas kernels: 0 us -> 61.5 us
  local copies, waits for them, and re-layouts: 61.3 us -> 13.7 us
  matrix products: 33.5 us -> 0 us
  starting transfers between devices: 25.2 us -> 41.7 us
  blocking collectives: 0 us -> 15.5 us
  between operations: 13.4 us -> 0.33 us
  other arithmetic: 9.83 us -> 3.65 us
    all_gather x3 -> x0, waiting for transfers between devices: 225 us -> none  [the longest x1 197 us: local(): lax.all_gather(out_weight, 'ctx', axis=1, tiled=True)]
    ppermute x0 -> x22, waiting for transfers between devices: none -> 101 us  [the longest x9 55 us: across(): return lax.ppermute(value, 'ctx', [(i, i ^ mask) for i in range(devices)])]
    pallas_call x0 -> x9, Pallas kernels: none -> 61.5 us  [the longest x4 23 us: project(): pl.pallas_call(functools.partial(project_kernel, slow_count, head_devices...]
    dot_general x7 -> x0, matrix products: 33.5 us -> none  [the longest x1 11.5 us: local(): jnp.dot(attended, lax.all_gather(out_weight, 'ctx', axis=1, tiled=True),...]
    ppermute x0 -> x22, starting transfers between devices: none -> 28 us  [the longest x9 13 us: across(): return lax.ppermute(value, 'ctx', [(i, i ^ mask) for i in range(devices)])]
    gather x4 -> x0, local copies, waits for them, and re-layouts: 17.5 us -> none  [the longest x1 5.07 us: local(): fetched_values[owner_grid, slot_grid]]
    all_to_all x0 -> x1, blocking collectives: none -> 15.5 us  [local(): lax.all_to_all(asked, 'ctx', split_axis=0, concat_axis=0, tiled=True)]
    reshape x7 -> x2, local copies, waits for them, and re-layouts: 13.3 us -> 0.7 us  [the longest x1 0.6 us: local(): asked_for = asked_for.reshape(-1)]
  transfers between devices with their start and end apart: 7 -> 24, of which waited for: 5 -> 8; matrix products, arithmetic and copies ran while one was open for 22% -> 3% of each run, Pallas kernels for 0% -> 20%
where the time goes in v1:
time: 277 us; the launch traced here: 276 us
  waiting for transfers between devices  140 us (51%)
  Pallas kernels  61.5 us (22%)
  starting transfers between devices  41.7 us (15%)
  blocking collectives  15.5 us (6%)
  local copies, waits for them, and re-layouts  13.7 us (5%)
  other arithmetic  3.65 us (1%)
    ppermute x9, waiting for transfers between devices, across(): return lax.ppermute(value, 'ctx', [(i, i ^ mask) for i in range(devices)])  55 us
    ppermute x3, waiting for transfers between devices, local(): land_parts.append(lax.ppermute(land, 'ctx', pairs))  46.5 us
    all_to_all x2, waiting for transfers between devices, fetch(): got = lax.all_to_all(sent, 'ctx', split_axis=0, concat_axis=0, tiled=True)  38.1 us
    pallas_call x4, Pallas kernels, project(): pl.pallas_call(functools.partial(project_kernel, slow_count, head_devices...  23 us
    pallas_call x1, Pallas kernels, attention_scores(): pl.pallas_call(functools.partial(score_kernel, groups, heads, picks, step...  21.6 us
    all_to_all x1, blocking collectives, local(): lax.all_to_all(asked, 'ctx', split_axis=0, concat_axis=0, tiled=True)  15.5 us
    all_to_all x2, starting transfers between devices, fetch(): got = lax.all_to_all(sent, 'ctx', split_axis=0, concat_axis=0, tiled=True)  13.7 us
    ppermute x9, starting transfers between devices, across(): return lax.ppermute(value, 'ctx', [(i, i ^ mask) for i in range(devices)])  13 us
  transfers between devices with their start and end apart: 24, of which 8 were waited for; matrix products, arithmetic and copies ran while one was open for 3% of the time, Pallas kernels for 20%

profile of v1, /device:TPU:0, one launch (start us, length us, event | category | flops | bytes accessed | tf_op | source)
XLA Modules:
  0.0 275.9 jit_solution(9956010302907523474)
XLA Ops:
  0.0 0.7 fusion.5
  2.2 15.5 %all_to_all.19 = s32[16,1,8]{2,1,0:T(1,128)S(1)} all-to-all(s32[16,1,8]{2,1,0:T(1,128)S(1)} %bitcast.27), channel_id=1, replica_groups=mesh['ctx'=16,'head'=2] {'ctx'}, dimensions={0} | all-to-all | bytes 1024 | tf_op jit(solution)/shard_map/all_to_all | solution.py:359
  19.4 4.2 %gather_blocks.3 = bf16[128,64,128]{2,1,0:T(8,128)(2,1)} custom-call(s32[128]{0:T(128)} %reshape.41.asked_ref, bf16[1024,2048]{1,0:T(8,128)(2,1)} %source_ref.3), custom_call_target="tpu_custom_call" | custom-call | flops 67108864 | bytes 4194304 | tf_op jit(solution)/shard_map/gather_blocks/pallas_call | solution.py:71
  23.6 3.7 %all-to-all-start.2 = ((bf16[16,8,64,128]{3,2,1,0:T(8,128)(2,1)}), bf16[16,8,64,128]{3,2,1,0:T(8,128)(2,1)S(1)}, u32[]{:S(2)}, u32[]{:S(2)}) async-start(bf16[16,8,64,128]{3,2,1,0:T(8,128)(2,1)} %bitcast.21), calls=%async_computation.2 | async-start | bytes 4194304 | tf_op jit(solution)/shard_map/all_to_all | solution.py:381
  27.4 4.2 %gather_blocks.2 = bf16[128,64,128]{2,1,0:T(8,128)(2,1)} custom-call(s32[128]{0:T(128)} %reshape.41.asked_ref, bf16[1024,2048]{1,0:T(8,128)(2,1)} %source_ref.2), custom_call_target="tpu_custom_call" | custom-call | flops 67108864 | bytes 4194304 | tf_op jit(solution)/shard_map/gather_blocks/pallas_call | solution.py:71
  31.6 38.1 %all-to-all-done.2 = bf16[16,8,64,128]{3,2,1,0:T(8,128)(2,1)S(1)} async-done(((bf16[16,8,64,128]{3,2,1,0:T(8,128)(2,1)}), bf16[16,8,64,128]{3,2,1,0:T(8,128)(2,1)S(1)}, u32[]{:S(2)}, u32[]{:S(2)}) %all-to-all-start.2) | async-done | bytes 2097184 | tf_op jit(solution)/shard_map/all_to_all | solution.py:381
  69.7 1.4 copy-done.6
  71.1 10.0 %all-to-all-start.1 = ((bf16[16,8,64,128]{3,2,1,0:T(8,128)(2,1)}), bf16[16,8,64,128]{3,2,1,0:T(8,128)(2,1)}, u32[]{:S(2)}, u32[]{:S(2)}) async-start(bf16[16,8,64,128]{3,2,1,0:T(8,128)(2,1)} %bitcast.20), calls=%async_computation.1 | async-start | bytes 4194304 | tf_op jit(solution)/shard_map/all_to_all | solution.py:381
  81.1 1.9 collective-permute-start
  83.0 2.4 collective-permute-start.1
  85.4 1.5 collective-permute-start.2
  86.8 2.5 collective-permute-start.5
  89.4 1.3 collective-permute-start.6
  91.3 31.7 %collective-permute-done = bf16[1,2,16,2048]{3,2,1,0:T(8,128)(2,1)S(1)} collective-permute-done((bf16[1,2,16,2048]{3,2,1,0:T(8,128)(2,1)S(1)}, bf16[1,2,16,2048]{3,2,1,0:T(8,128)(2,1)S(1)}, u32[]{:S(2)}, u32[]{:S(2)}) %collective-permute-start) | collective-permute-done | bytes 131104 | tf_op jit(solution)/shard_map/ppermute | solution.py:374
  123.1 14.8 %collective-permute-done.1 = bf16[1,2,16,2048]{3,2,1,0:T(8,128)(2,1)S(1)} collective-permute-done((bf16[1,2,16,2048]{3,2,1,0:T(8,128)(2,1)S(1)}, bf16[1,2,16,2048]{3,2,1,0:T(8,128)(2,1)S(1)}, u32[]{:S(2)}, u32[]{:S(2)}) %collective-permute-start.1) | collective-permute-done | bytes 131104 | tf_op jit(solution)/shard_map/ppermute | solution.py:374
  137.9 1.5 collective-permute-start.3
  141.5 8.5 %collective-permute-done.3 = bf16[4,2,16,2048]{3,2,1,0:T(8,128)(2,1)S(1)} collective-permute-done((bf16[4,2,16,2048]{3,2,1,0:T(8,128)(2,1)S(1)}, bf16[4,2,16,2048]{3,2,1,0:T(8,128)(2,1)S(1)}, u32[]{:S(2)}, u32[]{:S(2)}) %collective-permute-start.3) | collective-permute-done | bytes 524320 | tf_op jit(solution)/shard_map/ppermute | solution.py:345
  149.9 0.9 constant_dynamic-update-slice_fusion
  150.9 2.4 collective-permute-start.4
  153.3 0.7 collective-permute-start.7
  154.0 1.3 collective-permute-start.9
  155.3 18.5 %collective-permute-done.4 = bf16[8,2,16,2048]{3,2,1,0:T(8,128)(2,1)S(1)} collective-permute-done((bf16[8,2,16,2048]{3,2,1,0:T(8,128)(2,1)S(1)}, bf16[8,2,16,2048]{3,2,1,0:T(8,128)(2,1)S(1)}, u32[]{:S(2)}, u32[]{:S(2)}) %collective-permute-start.4) | collective-permute-done | bytes 1048608 | tf_op jit(solution)/shard_map/ppermute | solution.py:345
  173.9 1.1 constant_dynamic-update-slice_fusion.5.land_ref
  174.9 21.6 %attention_scores.1 = (bf16[256,4096]{1,0:T(8,128)(2,1)}, f32[256,2048]{1,0:T(8,128)}) custom-call(s32[256]{0:T(256)} %copy-done.18, bf16[256,2048]{1,0:T(8,128)(2,1)} %q_ref.1, bf16[16,2,16,2048]{3,2,1,0:T(8,128)(2,1)} %constant_dynamic-update-slice_fusion.5.land_ref, bf16[256,2048]{1,0:T(8,128)(2,1)} %lk_ref.1, bf16[256,2048]{1,0:T(8,128)(2,1)} %lv_ref.1, ...), custom_call_target="tpu_custom_call" | custom-call | flops 4831838208 | bytes 8388608 | tf_op jit(solution)/shard_map/attention_scores/pallas_call | solution.py:170
  196.6 5.9 %attention_values.1.refs_0_ = bf16[256,2048]{1,0:T(8,128)(2,1)} custom-call(s32[256]{0:T(256)} %copy-done.18, bf16[256,4096]{1,0:T(8,128)(2,1)} %get-tuple-element.17.weight_ref, f32[256,2048]{1,0:T(8,128)} %get-tuple-element.18.acc_ref, bf16[128,64,128]{2,1,0:T(8,128)(2,1)} %bitcast.22), custom_call_target="tpu_custom_call" | custom-call | flops 536870912 | bytes 6291456 | tf_op jit(solution)/shard_map/attention_values/pallas_call | solution.py:209
  202.5 1.7 collective-permute-start.15
  204.3 1.1 collective-permute-start.12
  205.4 0.7 collective-permute-start.8
  206.1 1.5 collective-permute-start.10
  207.6 17.0 %collective-permute-done.15.refs_0_ = bf16[256,2048]{1,0:T(8,128)(2,1)S(1)} collective-permute-done((bf16[256,2048]{1,0:T(8,128)(2,1)}, bf16[256,2048]{1,0:T(8,128)(2,1)S(1)}, u32[]{:S(2)}, u32[]{:S(2)}) %collective-permute-start.15) | collective-permute-done | bytes 1048608 | tf_op jit(solution)/shard_map/ppermute | solution.py:345
  224.6 1.0 copy-done.7
  225.5 0.8 slice.8
  226.4 1.1 collective-permute-start.18
  227.5 1.0 copy-done.8
  228.5 0.9 slice.9
  229.4 1.5 collective-permute-start.19
  231.4 1.0 copy-done.4
  232.4 1.0 copy-done.5
  233.4 6.0 %project.5 = (f32[256,512]{1,0:T(8,128)}, bf16[1,256,512]{2,1,0:T(8,128)(2,1)}) custom-call(s32[3]{0:T(128)} %pad_add_fusion.place_ref, bf16[256,2048]{1,0:T(8,128)(2,1)} %copy-done.8, bf16[2048,256]{1,0:T(8,128)(2,1)} %copy-done.4, bf16[2048,256]{1,0:T(8,128)(2,1)} %copy-done.3, bf16[2048,256]{1,0:T(8,128)(2,1)} %copy-done.1, bf16[2048,256]{1,0:T(8,128)(2,1)} %refs_5_.1, ...), custom_call_target="tpu_custom_call" | custom-call | flops 1073741824 | bytes 4194304 | tf_op jit(solution)/shard_map/project/pallas_call | solution.py:266
  239.5 6.0 %project.4 = (f32[256,512]{1,0:T(8,128)}, bf16[1,256,512]{2,1,0:T(8,128)(2,1)}) custom-call(s32[3]{0:T(128)} %pad_add_fusion.place_ref, bf16[256,2048]{1,0:T(8,128)(2,1)} %attention_values.1.refs_0_, bf16[2048,256]{1,0:T(8,128)(2,1)} %copy-done.4, bf16[2048,256]{1,0:T(8,128)(2,1)} %copy-done.3, bf16[2048,256]{1,0:T(8,128)(2,1)} %copy-done.1, ...), custom_call_target="tpu_custom_call" | custom-call | flops 1073741824 | bytes 4194304 | tf_op jit(solution)/shard_map/project/pallas_call | solution.py:266
  246.0 6.0 %project.6 = (f32[256,512]{1,0:T(8,128)}, bf16[1,256,512]{2,1,0:T(8,128)(2,1)}) custom-call(s32[3]{0:T(128)} %pad_add_fusion.place_ref, bf16[256,2048]{1,0:T(8,128)(2,1)} %copy-done.7, bf16[2048,256]{1,0:T(8,128)(2,1)} %copy-done.4, bf16[2048,256]{1,0:T(8,128)(2,1)} %copy-done.3, bf16[2048,256]{1,0:T(8,128)(2,1)} %copy-done.1, bf16[2048,256]{1,0:T(8,128)(2,1)} %refs_5_.1, ...), custom_call_target="tpu_custom_call" | custom-call | flops 1073741824 | bytes 4194304 | tf_op jit(solution)/shard_map/project/pallas_call | solution.py:266
  252.2 5.1 %project.7 = (f32[256,512]{1,0:T(8,128)}, bf16[1,256,512]{2,1,0:T(8,128)(2,1)}) custom-call(s32[3]{0:T(128)} %pad_add_fusion.place_ref, bf16[128,2048]{1,0:T(8,128)(2,1)} %collective-permute-done.18.refs_0_, bf16[128,2048]{1,0:T(8,128)(2,1)} %collective-permute-done.19.refs_1_, bf16[2048,256]{1,0:T(8,128)(2,1)} %copy-done.4, bf16[2048,256]{1,0:T(8,128)(2,1)} %copy-done.3, ...), custom_call_target="tpu_custom_call" | custom-call | flops 1073741824 | bytes 4194304 | tf_op jit(solution)/shard_map/project/pallas_call | solution.py:266
  257.8 1.0 collective-permute-start.14
  259.6 2.0 collective-permute-start.21
  261.7 5.4 %collective-permute-done.14.refs_1_ = bf16[256,512]{1,0:T(8,128)(2,1)S(1)} collective-permute-done((bf16[256,512]{1,0:T(8,128)(2,1)S(1)}, bf16[256,512]{1,0:T(8,128)(2,1)S(1)}, u32[]{:S(2)}, u32[]{:S(2)}) %collective-permute-start.14) | collective-permute-done | bytes 262176 | tf_op jit(solution)/shard_map/ppermute | solution.py:345
  267.0 5.5 %collective-permute-done.17.refs_2_ = bf16[256,512]{1,0:T(8,128)(2,1)S(1)} collective-permute-done((bf16[256,512]{1,0:T(8,128)(2,1)S(1)}, bf16[256,512]{1,0:T(8,128)(2,1)S(1)}, u32[]{:S(2)}, u32[]{:S(2)}) %collective-permute-start.17) | collective-permute-done | bytes 262176 | tf_op jit(solution)/shard_map/ppermute | solution.py:345
  272.6 0.7 copy-done.16
  273.4 2.5 assemble.1
  (79 shorter events, 8.8 us)
Async XLA Ops:
  1.7 21.9 %copy-start.18 = (s32[256]{0:T(256)}, s32[256]{0:T(256)S(1)}, u32[]{:S(2)}) copy-start(s32[256]{0:T(256)S(1)} %multiply_add_fusion.cell_ref) | copy-start | bytes 3076
  23.6 46.1 %all-to-all-start.2 = ((bf16[16,8,64,128]{3,2,1,0:T(8,128)(2,1)}), bf16[16,8,64,128]{3,2,1,0:T(8,128)(2,1)S(1)}, u32[]{:S(2)}, u32[]{:S(2)}) async-start(bf16[16,8,64,128]{3,2,1,0:T(8,128)(2,1)} %bitcast.21), calls=%async_computation.2 | async-start | bytes 4194304 | tf_op jit(solution)/shard_map/all_to_all | solution.py:381
  69.7 1.4 copy-start.6
  71.1 10.0 %copy-start.12 = (bf16[16,2048]{1,0:T(8,128)(2,1)S(1)}, bf16[16,2048]{1,0:T(8,128)(2,1)}, u32[]{:S(2)}) copy-start(bf16[16,2048]{1,0:T(8,128)(2,1)} %param.15) | copy-start | bytes 196612
  71.1 10.0 %copy-start.13 = (bf16[16,2048]{1,0:T(8,128)(2,1)S(1)}, bf16[16,2048]{1,0:T(8,128)(2,1)}, u32[]{:S(2)}) copy-start(bf16[16,2048]{1,0:T(8,128)(2,1)} %param.14) | copy-start | bytes 196612
  71.1 15.8 %copy-start = (bf16[2048,256]{1,0:T(8,128)(2,1)S(1)}, bf16[2048,256]{1,0:T(8,128)(2,1)}, u32[]{:S(2)}) copy-start(bf16[2048,256]{1,0:T(8,128)(2,1)} %refs_5_.1) | copy-start | bytes 3145732
  71.1 103.9 %all-to-all-start.1 = ((bf16[16,8,64,128]{3,2,1,0:T(8,128)(2,1)}), bf16[16,8,64,128]{3,2,1,0:T(8,128)(2,1)}, u32[]{:S(2)}, u32[]{:S(2)}) async-start(bf16[16,8,64,128]{3,2,1,0:T(8,128)(2,1)} %bitcast.20), calls=%async_computation.1 | async-start | bytes 4194304 | tf_op jit(solution)/shard_map/all_to_all | solution.py:381
  81.1 42.0 %collective-permute-start = (bf16[1,2,16,2048]{3,2,1,0:T(8,128)(2,1)S(1)}, bf16[1,2,16,2048]{3,2,1,0:T(8,128)(2,1)S(1)}, u32[]{:S(2)}, u32[]{:S(2)}) collective-permute-start(bf16[1,2,16,2048]{3,2,1,0:T(8,128)(2,1)S(1)} %maximum_bitcast_fusion), channel_id=1, source_target_pairs={{0,8},{2,10},{4,12},{6,14},{8,16},{10,18},{12,20},{14,22},{16,24},... | collective-permute-start | bytes 393224 | tf_op jit(solution)/shard_map/ppermute | solution.py:374
  83.0 54.8 %collective-permute-start.1 = (bf16[1,2,16,2048]{3,2,1,0:T(8,128)(2,1)S(1)}, bf16[1,2,16,2048]{3,2,1,0:T(8,128)(2,1)S(1)}, u32[]{:S(2)}, u32[]{:S(2)}) collective-permute-start(bf16[1,2,16,2048]{3,2,1,0:T(8,128)(2,1)S(1)} %maximum_bitcast_fusion), channel_id=1, source_target_pairs={{0,16},{2,18},{4,20},{6,22},{8,24},{10,26},{12,28},{14,30},{16,0},... | collective-permute-start | bytes 393224 | tf_op jit(solution)/shard_map/ppermute | solution.py:374
  85.4 52.5 %collective-permute-start.2 = (bf16[1,2,16,2048]{3,2,1,0:T(8,128)(2,1)S(1)}, bf16[1,2,16,2048]{3,2,1,0:T(8,128)(2,1)S(1)}, u32[]{:S(2)}, u32[]{:S(2)}) collective-permute-start(bf16[1,2,16,2048]{3,2,1,0:T(8,128)(2,1)S(1)} %maximum_bitcast_fusion), channel_id=1, source_target_pairs={{0,24},{2,26},{4,28},{6,30},{8,0},{10,2},{12,4},{14,6},{16,8},{18,... | collective-permute-start | bytes 393224 | tf_op jit(solution)/shard_map/ppermute | solution.py:374
  86.8 66.5 %collective-permute-start.5 = (bf16[2048,256]{1,0:T(8,128)(2,1)S(1)}, bf16[2048,256]{1,0:T(8,128)(2,1)S(1)}, u32[]{:S(2)}, u32[]{:S(2)}) collective-permute-start(bf16[2048,256]{1,0:T(8,128)(2,1)S(1)} %copy-done), channel_id=1, source_target_pairs={{0,8},{2,10},{4,12},{6,14},{8,16},{10,18},{12,20},{14,22},{16,24},... | collective-permute-start | bytes 3145736 | tf_op jit(solution)/shard_map/ppermute | solution.py:355
  89.4 63.9 %collective-permute-start.6 = (bf16[2048,256]{1,0:T(8,128)(2,1)S(1)}, bf16[2048,256]{1,0:T(8,128)(2,1)S(1)}, u32[]{:S(2)}, u32[]{:S(2)}) collective-permute-start(bf16[2048,256]{1,0:T(8,128)(2,1)S(1)} %copy-done), channel_id=1, source_target_pairs={{8,0},{10,2},{12,4},{14,6},{16,8},{18,10},{20,12},{22,14},{24,16},... | collective-permute-start | bytes 3145736 | tf_op jit(solution)/shard_map/ppermute | solution.py:355
  137.9 12.0 %collective-permute-start.3 = (bf16[4,2,16,2048]{3,2,1,0:T(8,128)(2,1)S(1)}, bf16[4,2,16,2048]{3,2,1,0:T(8,128)(2,1)S(1)}, u32[]{:S(2)}, u32[]{:S(2)}) collective-permute-start(bf16[4,2,16,2048]{3,2,1,0:T(8,128)(2,1)S(1)} %pad_maximum_fusion), channel_id=1, source_target_pairs={{0,2},{2,0},{4,6},{6,4},{8,10},{10,8},{12,14},{14,12},{16,18},{18,... | collective-permute-start | bytes 1572872 | tf_op jit(solution)/shard_map/ppermute | solution.py:345
  150.9 23.0 %collective-permute-start.4 = (bf16[8,2,16,2048]{3,2,1,0:T(8,128)(2,1)S(1)}, bf16[8,2,16,2048]{3,2,1,0:T(8,128)(2,1)S(1)}, u32[]{:S(2)}, u32[]{:S(2)}) collective-permute-start(bf16[8,2,16,2048]{3,2,1,0:T(8,128)(2,1)S(1)} %get-tuple-element.29), channel_id=1, source_target_pairs={{0,4},{2,6},{4,0},{6,2},{8,12},{10,14},{12,8},{14,10},{16,20},{18,... | collective-permute-start | bytes 3145736 | tf_op jit(solution)/shard_map/ppermute | solution.py:345
  153.3 43.3 %copy-start.1 = (bf16[2048,256]{1,0:T(8,128)(2,1)}, bf16[2048,256]{1,0:T(8,128)(2,1)S(1)}, u32[]{:S(2)}) copy-start(bf16[2048,256]{1,0:T(8,128)(2,1)S(1)} %collective-permute-done.5.refs_3_.refs_4_) | copy-start | bytes 3145732
  153.3 43.3 %copy-start.2 = (bf16[2048,256]{1,0:T(8,128)(2,1)}, bf16[2048,256]{1,0:T(8,128)(2,1)S(1)}, u32[]{:S(2)}) copy-start(bf16[2048,256]{1,0:T(8,128)(2,1)S(1)} %collective-permute-done.6.refs_5_.refs_6_) | copy-start | bytes 3145732
  153.3 52.0 %collective-permute-start.7 = (bf16[2048,256]{1,0:T(8,128)(2,1)S(1)}, bf16[2048,256]{1,0:T(8,128)(2,1)S(1)}, u32[]{:S(2)}, u32[]{:S(2)}) collective-permute-start(bf16[2048,256]{1,0:T(8,128)(2,1)S(1)} %collective-permute-done.5.refs_3_.refs_4_), channel_id=1, source_target_pairs={{8,16},{10,18},{12,20},{14,22},{16,24},{18,26},{20,28},{22,30},{9,... | collective-permute-start | bytes 3145736 | tf_op jit(solution)/shard_map/ppermute | solution.py:355
  154.0 52.0 %collective-permute-start.9 = (bf16[2048,256]{1,0:T(8,128)(2,1)S(1)}, bf16[2048,256]{1,0:T(8,128)(2,1)}, u32[]{:S(2)}, u32[]{:S(2)}) collective-permute-start(bf16[2048,256]{1,0:T(8,128)(2,1)S(1)} %collective-permute-done.6.refs_5_.refs_6_), channel_id=1, source_target_pairs={{8,0},{10,2},{12,4},{14,6},{16,8},{18,10},{20,12},{22,14},{9,1},{1... | collective-permute-start | bytes 3145736 | tf_op jit(solution)/shard_map/ppermute | solution.py:355
  202.5 22.1 %collective-permute-start.15 = (bf16[256,2048]{1,0:T(8,128)(2,1)}, bf16[256,2048]{1,0:T(8,128)(2,1)S(1)}, u32[]{:S(2)}, u32[]{:S(2)}) collective-permute-start(bf16[256,2048]{1,0:T(8,128)(2,1)} %attention_values.1.refs_0_), channel_id=1, source_target_pairs={{0,4},{2,6},{4,0},{6,2},{8,12},{10,14},{12,8},{14,10},{16,20},{18,... | collective-permute-start | bytes 3145736 | tf_op jit(solution)/shard_map/ppermute | solution.py:345
  204.3 23.2 %collective-permute-start.12 = (bf16[256,2048]{1,0:T(8,128)(2,1)}, bf16[256,2048]{1,0:T(8,128)(2,1)S(1)}, u32[]{:S(2)}, u32[]{:S(2)}) collective-permute-start(bf16[256,2048]{1,0:T(8,128)(2,1)} %attention_values.1.refs_0_), channel_id=1, source_target_pairs={{0,2},{2,0},{4,6},{6,4},{8,10},{10,8},{12,14},{14,12},{16,18},{18,... | collective-permute-start | bytes 3145736 | tf_op jit(solution)/shard_map/ppermute | solution.py:345
  205.4 26.1 %copy-start.3 = (bf16[2048,256]{1,0:T(8,128)(2,1)}, bf16[2048,256]{1,0:T(8,128)(2,1)S(1)}, u32[]{:S(2)}) copy-start(bf16[2048,256]{1,0:T(8,128)(2,1)S(1)} %collective-permute-done.7.refs_2_.refs_3_) | copy-start | bytes 3145732
  205.4 26.1 %collective-permute-start.8 = (bf16[2048,256]{1,0:T(8,128)(2,1)S(1)}, bf16[2048,256]{1,0:T(8,128)(2,1)S(1)}, u32[]{:S(2)}, u32[]{:S(2)}) collective-permute-start(bf16[2048,256]{1,0:T(8,128)(2,1)S(1)} %collective-permute-done.7.refs_2_.refs_3_), channel_id=1, source_target_pairs={{16,24},{18,26},{20,28},{22,30},{17,25},{19,27},{21,29},{23,31}} | collective-permute-start | bytes 3145736 | tf_op jit(solution)/shard_map/ppermute | solution.py:355
  206.1 25.3 %collective-permute-start.10 = (bf16[2048,256]{1,0:T(8,128)(2,1)}, bf16[2048,256]{1,0:T(8,128)(2,1)S(1)}, u32[]{:S(2)}, u32[]{:S(2)}) collective-permute-start(bf16[2048,256]{1,0:T(8,128)(2,1)} %collective-permute-done.9.refs_6_.refs_7_), channel_id=1, source_target_pairs={{8,0},{10,2},{12,4},{14,6},{9,1},{11,3},{13,5},{15,7}} | collective-permute-start | bytes 3145736 | tf_op jit(solution)/shard_map/ppermute | solution.py:355
  224.6 1.0 copy-start.7
  226.4 25.8 %collective-permute-start.18 = (bf16[128,2048]{1,0:T(8,128)(2,1)}, bf16[128,2048]{1,0:T(8,128)(2,1)}, u32[]{:S(2)}, u32[]{:S(2)}) collective-permute-start(bf16[128,2048]{1,0:T(8,128)(2,1)} %slice.8), channel_id=1, source_target_pairs={{0,2},{2,0},{4,6},{6,4},{8,10},{10,8},{12,14},{14,12},{16,18},{18,... | collective-permute-start | bytes 1572872 | tf_op jit(solution)/shard_map/ppermute | solution.py:345
  227.5 1.0 copy-start.8
  229.4 22.8 %collective-permute-start.19 = (bf16[128,2048]{1,0:T(8,128)(2,1)}, bf16[128,2048]{1,0:T(8,128)(2,1)}, u32[]{:S(2)}, u32[]{:S(2)}) collective-permute-start(bf16[128,2048]{1,0:T(8,128)(2,1)} %slice.9), channel_id=1, source_target_pairs={{0,4},{2,6},{4,0},{6,2},{8,12},{10,14},{12,8},{14,10},{16,20},{18,... | collective-permute-start | bytes 1572872 | tf_op jit(solution)/shard_map/ppermute | solution.py:345
  231.4 1.0 copy-start.4
  232.4 1.0 copy-start.5
  239.4 18.3 %collective-permute-start.13 = (bf16[256,512]{1,0:T(8,128)(2,1)}, bf16[256,512]{1,0:T(8,128)(2,1)S(1)}, u32[]{:S(2)}, u32[]{:S(2)}) collective-permute-start(bf16[256,512]{1,0:T(8,128)(2,1)} %bitcast.29), channel_id=1, source_target_pairs={{0,1},{1,0},{2,3},{3,2},{4,5},{5,4},{6,7},{7,6},{8,9},{9,8},{10,11... | collective-permute-start | bytes 786440 | tf_op jit(solution)/shard_map/ppermute | solution.py:418
  245.5 16.2 %collective-permute-start.11 = (bf16[256,512]{1,0:T(8,128)(2,1)}, bf16[256,512]{1,0:T(8,128)(2,1)S(1)}, u32[]{:S(2)}, u32[]{:S(2)}) collective-permute-start(bf16[256,512]{1,0:T(8,128)(2,1)} %bitcast.28), channel_id=1, source_target_pairs={{0,1},{1,0},{2,3},{3,2},{4,5},{5,4},{6,7},{7,6},{8,9},{9,8},{10,11... | collective-permute-start | bytes 786440 | tf_op jit(solution)/shard_map/ppermute | solution.py:418
  252.0 5.7 %copy-start.9 = (f32[256,512]{1,0:T(8,128)S(1)}, f32[256,512]{1,0:T(8,128)}, u32[]{:S(2)}) copy-start(f32[256,512]{1,0:T(8,128)} %get-tuple-element.23) | copy-start | bytes 1572868
  252.0 6.8 %copy-start.10 = (f32[256,512]{1,0:T(8,128)S(1)}, f32[256,512]{1,0:T(8,128)}, u32[]{:S(2)}) copy-start(f32[256,512]{1,0:T(8,128)} %get-tuple-element.25) | copy-start | bytes 1572868
  252.1 6.7 %collective-permute-start.16 = (bf16[256,512]{1,0:T(8,128)(2,1)}, bf16[256,512]{1,0:T(8,128)(2,1)S(1)}, u32[]{:S(2)}, u32[]{:S(2)}) collective-permute-start(bf16[256,512]{1,0:T(8,128)(2,1)} %bitcast.30), channel_id=1, source_target_pairs={{0,1},{1,0},{2,3},{3,2},{4,5},{5,4},{6,7},{7,6},{8,9},{9,8},{10,11... | collective-permute-start | bytes 786440 | tf_op jit(solution)/shard_map/ppermute | solution.py:418
  257.2 2.3 copy-start.11
  257.2 2.3 collective-permute-start.20
  257.8 9.2 %collective-permute-start.14 = (bf16[256,512]{1,0:T(8,128)(2,1)S(1)}, bf16[256,512]{1,0:T(8,128)(2,1)S(1)}, u32[]{:S(2)}, u32[]{:S(2)}) collective-permute-start(bf16[256,512]{1,0:T(8,128)(2,1)S(1)} %add_convert_fusion.2), channel_id=1, source_target_pairs={{0,2},{2,0},{4,6},{6,4},{8,10},{10,8},{12,14},{14,12},{16,18},{18,... | collective-permute-start | bytes 786440 | tf_op jit(solution)/shard_map/ppermute | solution.py:345
  258.9 13.7 %collective-permute-start.17 = (bf16[256,512]{1,0:T(8,128)(2,1)S(1)}, bf16[256,512]{1,0:T(8,128)(2,1)S(1)}, u32[]{:S(2)}, u32[]{:S(2)}) collective-permute-start(bf16[256,512]{1,0:T(8,128)(2,1)S(1)} %add_convert_fusion.1), channel_id=1, source_target_pairs={{0,4},{2,6},{4,0},{6,2},{8,12},{10,14},{12,8},{14,10},{16,20},{18,... | collective-permute-start | bytes 786440 | tf_op jit(solution)/shard_map/ppermute | solution.py:345
  259.6 13.0 %collective-permute-start.21 = (bf16[256,512]{1,0:T(8,128)(2,1)S(1)}, bf16[256,512]{1,0:T(8,128)(2,1)S(1)}, u32[]{:S(2)}, u32[]{:S(2)}) collective-permute-start(bf16[256,512]{1,0:T(8,128)(2,1)S(1)} %add_convert_fusion), channel_id=1, source_target_pairs={{0,6},{2,4},{4,2},{6,0},{8,14},{10,12},{12,10},{14,8},{16,22},{18,... | collective-permute-start | bytes 786440 | tf_op jit(solution)/shard_map/ppermute | solution.py:345
  261.6 10.9 %copy-start.14 = (bf16[256,512]{1,0:T(8,128)(2,1)}, bf16[256,512]{1,0:T(8,128)(2,1)S(1)}, u32[]{:S(2)}) copy-start(bf16[256,512]{1,0:T(8,128)(2,1)S(1)} %collective-permute-done.11.refs_0_) | copy-start | bytes 786436
  267.0 5.6 %copy-start.15 = (bf16[256,512]{1,0:T(8,128)(2,1)}, bf16[256,512]{1,0:T(8,128)(2,1)S(1)}, u32[]{:S(2)}) copy-start(bf16[256,512]{1,0:T(8,128)(2,1)S(1)} %collective-permute-done.14.refs_1_) | copy-start | bytes 786436
  272.6 0.7 copy-start.16
  272.6 0.8 copy-start.17

commit v2 on v1

--- a/solution.py
+++ b/solution.py
@@ -8,11 +8,12 @@
 from jax.experimental.pallas import tpu as pltpu
 from jax.sharding import PartitionSpec as P
 
+
 BLOCK = 64
-ANY = pl.BlockSpec(memory_space=pl.ANY)
+HBM = pl.BlockSpec(memory_space=pltpu.HBM)
 VMEM = pl.BlockSpec(memory_space=pltpu.VMEM)
 SMEM = pl.BlockSpec(memory_space=pltpu.SMEM)
-LIMIT = 60 * 1024 * 1024
+LIMIT = 24 * 1024 * 1024
 
 
 def split_ctx(devices, head_devices):
@@ -71,7 +72,7 @@
     return pl.pallas_call(
         functools.partial(gather_kernel, heads),
         out_shape=jax.ShapeDtypeStruct((cells, BLOCK, size), source.dtype),
-        in_specs=[SMEM, ANY],
+        in_specs=[SMEM, HBM],
         out_specs=VMEM,
         scratch_shapes=[pltpu.SemaphoreType.DMA],
         cost_estimate=pl.CostEstimate(
@@ -138,7 +139,7 @@
             )
 
 
-def value_kernel(groups, heads, picks, step_heads, cell_ref, weight_ref, acc_ref, fv_ref, out_ref):
+def value_kernel(groups, heads, picks, step_heads, cell_ref, weight_ref, acc_ref, fv_ref, *outs):
     size = acc_ref.shape[1] // step_heads
     first_head = pl.program_id(0) * step_heads
     chosen = picks * BLOCK
@@ -146,16 +147,17 @@
         cols = slice(hh * size, (hh + 1) * size)
         for g in range(groups):
             rows = slice(g * BLOCK, (g + 1) * BLOCK)
+            chunk, inner = divmod(g, groups // len(outs))
             base = (g * heads + first_head + hh) * picks
             values = jnp.concatenate([fv_ref[cell_ref[base + p]] for p in range(picks)], axis=0)
-            out_ref[rows, cols] = (
+            outs[chunk][inner * BLOCK : (inner + 1) * BLOCK, cols] = (
                 acc_ref[rows, cols]
                 + jnp.dot(
                     weight_ref[rows, hh * chosen : (hh + 1) * chosen],
                     values,
                     preferred_element_type=jnp.float32,
                 )
-            ).astype(out_ref.dtype)
+            ).astype(jnp.bfloat16)
 
 
 def attention_scores(cell, queries, land, span_keys, span_values, fetched_keys, dims):
@@ -205,6 +207,7 @@
     step = math.gcd(heads, 4)
     wide = step * size
     chosen = picks * BLOCK
+    chunks = math.gcd(groups, 2)
     by_head = lambda i, c: (0, i)
     return pl.pallas_call(
         functools.partial(value_kernel, groups, heads, picks, step),
@@ -216,9 +219,9 @@
                 pl.BlockSpec((rows, wide), by_head),
                 pl.BlockSpec(fetched_values.shape, lambda i, c: (0, 0, 0)),
             ],
-            out_specs=pl.BlockSpec((rows, wide), by_head),
-        ),
-        out_shape=jax.ShapeDtypeStruct((rows, width), jnp.bfloat16),
+            out_specs=[pl.BlockSpec((rows // chunks, wide), by_head)] * chunks,
+        ),
+        out_shape=[jax.ShapeDtypeStruct((rows // chunks, width), jnp.bfloat16)] * chunks,
         compiler_params=pltpu.CompilerParams(vmem_limit_bytes=LIMIT),
         cost_estimate=pl.CostEstimate(
             flops=4 * rows * chosen * width,
@@ -229,60 +232,84 @@
     )(cell, weights, part, fetched_values)
 
 
-def project_kernel(slow_count, head_devices, pieces, place_ref, *refs):
-    a_refs, b_refs = refs[:pieces], refs[pieces : pieces + 2 * slow_count - 1]
-    mine_ref, send_ref, b_buf, sem = refs[pieces + 2 * slow_count - 1 :]
+def pick_kernel(slow_count, head_devices, table, place_ref, *refs):
+    b_refs, out_ref, sem = refs[:-2], refs[-2], refs[-1]
     slow, head = place_ref[0], place_ref[1]
     share = slow_count // head_devices
-    width = b_buf.shape[2]
     for slot in range(slow_count):
         target = lax.rem(head + slot // share, head_devices) * share + slot % share
-        for index in range(2 * slow_count - 1):
-
-            @pl.when(target - slow == index - (slow_count - 1))
+        for step, low, high, members in table:
+
+            @pl.when((target - slow == step) & (slow >= low) & (slow <= high))
             def _():
-                pltpu.make_async_copy(b_refs[index], b_buf.at[slot], sem.at[slot]).start()
+                row = 0
+                for member in members:
+                    ref = b_refs[member]
+                    rows = pl.ds(row, ref.shape[0])
+                    row += ref.shape[0]
+                    pltpu.make_async_copy(ref, out_ref.at[slot, rows], sem.at[slot]).start()
 
     for slot in range(slow_count):
-        pltpu.make_async_copy(b_refs[0], b_buf.at[slot], sem.at[slot]).wait()
+        pltpu.make_async_copy(out_ref.at[slot], out_ref.at[slot], sem.at[slot]).wait()
+
+
+def pick(place, blocks, slow_count, head_devices):
+    arrays, table = [], []
+    for step, low, high, chunks in blocks:
+        table.append((step, low, high, range(len(arrays), len(arrays) + len(chunks))))
+        arrays += chunks
+    depth, width = sum(c.shape[0] for c in blocks[0][3]), arrays[0].shape[1]
+    return pl.pallas_call(
+        functools.partial(pick_kernel, slow_count, head_devices, table),
+        out_shape=jax.ShapeDtypeStruct((slow_count, depth, width), jnp.bfloat16),
+        in_specs=[SMEM] + [HBM] * len(arrays),
+        out_specs=VMEM,
+        scratch_shapes=[pltpu.SemaphoreType.DMA((slow_count,))],
+        compiler_params=pltpu.CompilerParams(vmem_limit_bytes=60 * 1024 * 1024),
+        cost_estimate=pl.CostEstimate(
+            flops=64 * depth * width * slow_count,
+            bytes_accessed=4 * depth * width * slow_count,
+            transcendentals=0,
+        ),
+        name="pick",
+    )(place, *arrays)
+
+
+def project_kernel(share, a_count, *refs):
+    a_refs, (b_ref, mine_ref, send_ref) = refs[:a_count], refs[a_count:]
+    slots, _, width = b_ref.shape
+    for slot in range(slots):
         row = 0
         for a_ref in a_refs:
             rows = slice(row, row + a_ref.shape[0])
             row += a_ref.shape[0]
-            product = jnp.dot(a_ref[...], b_buf[slot], preferred_element_type=jnp.float32)
+            product = jnp.dot(a_ref[...], b_ref[slot], preferred_element_type=jnp.float32)
+            cols = slice(slot % share * width, (slot % share + 1) * width)
             if slot < share:
-                mine_ref[rows, slot * width : (slot + 1) * width] = product
+                mine_ref[rows, cols] = product
             else:
-                other = slot - share
-                send_ref[
-                    other // share, rows, (other % share) * width : (other % share + 1) * width
-                ] = product.astype(send_ref.dtype)
-
-
-def project(place, a_pieces, b_blocks, slow_count, head_devices):
+                send_ref[slot // share - 1, rows, cols] = product.astype(send_ref.dtype)
+
+
+def project(a_pieces, b_all, share):
     rows = sum(a.shape[0] for a in a_pieces)
-    depth, width = b_blocks[0].shape
-    share = slow_count // head_devices
-    return pl.pallas_call(
-        functools.partial(project_kernel, slow_count, head_devices, len(a_pieces)),
+    slots, depth, width = b_all.shape
+    return pl.pallas_call(
+        functools.partial(project_kernel, share, len(a_pieces)),
         out_shape=[
             jax.ShapeDtypeStruct((rows, share * width), jnp.float32),
-            jax.ShapeDtypeStruct((head_devices - 1, rows, share * width), jnp.bfloat16),
+            jax.ShapeDtypeStruct((slots // share - 1, rows, share * width), jnp.bfloat16),
         ],
-        in_specs=[SMEM] + [VMEM] * len(a_pieces) + [ANY] * len(b_blocks),
+        in_specs=[VMEM] * (len(a_pieces) + 1),
         out_specs=[VMEM, VMEM],
-        scratch_shapes=[
-            pltpu.VMEM((slow_count, depth, width), jnp.bfloat16),
-            pltpu.SemaphoreType.DMA((slow_count,)),
-        ],
-        compiler_params=pltpu.CompilerParams(vmem_limit_bytes=LIMIT),
+        compiler_params=pltpu.CompilerParams(vmem_limit_bytes=LIMIT // 2),
         cost_estimate=pl.CostEstimate(
-            flops=2 * rows * depth * width * slow_count,
-            bytes_accessed=2 * depth * width * slow_count,
+            flops=2 * rows * depth * width * slots,
+            bytes_accessed=2 * depth * width * slots,
             transcendentals=0,
         ),
         name="project",
-    )(place, *a_pieces, *b_blocks)
+    )(*a_pieces, b_all)
 
 
 def assemble_kernel(fast_count, share, others, place_ref, mine_ref, *refs):
@@ -329,7 +356,7 @@
     out_weight,
     selection,
 ):
-    rows, width = queries.shape
+    _, width = queries.shape
     groups, heads, picks = selection.shape
     size = width // heads
     devices = lax.axis_size("ctx")
@@ -359,10 +386,17 @@
     asked_for = lax.all_to_all(asked, "ctx", split_axis=0, concat_axis=0, tiled=True)
     asked_for = asked_for.reshape(-1)
 
-    below, above = [out_weight], [out_weight]
+    last = slow_count - 1
+    blocks = [(0, 0, last, [out_weight])]
+    low_parts = high_parts = None
     if slow_count > 1:
-        below.append(along(out_weight, 1))
-        above.append(along(out_weight, -1))
+        low, high = along(out_weight, 1), along(out_weight, -1)
+        blocks += [(-1, 1, last, [low]), (1, 0, last - 1, [high])]
+    if slow_count > 2:
+        blocks.append((-2, last, last, [along(low, 1, last - 1, last)]))
+        blocks.append((2, 0, 0, [along(high, -1, 1, 2)]))
+        cut = low.shape[0] // 2
+        low_parts, high_parts = [low[:cut], low[cut:]], [high[:cut], high[cut:]]
     land = jnp.stack([land_keys, land_values])[None]
     land_parts = [land]
     for shift in range(1, slow_count):
@@ -390,30 +424,35 @@
     )
     attended = attention_values(cell, weights, part, fetched_values, dims)
 
+    if slow_count > 3:
+        low_parts, high_parts, _ = lax.optimization_barrier(
+            (low_parts, high_parts, fetched_values)
+        )
     for hop in range(2, slow_count):
-        low, high = below[-1], above[-1]
-        if hop == 2:
-            low, high, _ = lax.optimization_barrier((low, high, fetched_values))
-        below.append(along(low, 1, hop - 1, slow_count))
-        above.append(along(high, -1, 0, slow_count - hop + 1))
-    b_blocks = below[:0:-1] + [out_weight] + above[1:]
-
-    pieces = {0: [attended]}
-    for mask in sorted(range(1, fast_count), key=lambda m: (m.bit_count(), m)):
+        top = last - 1 if hop == 2 else last
+        if hop > top:
+            break
+        for j in range(2):
+            low_parts[j] = along(low_parts[j], 1, hop - 1, top)
+            high_parts[j] = along(high_parts[j], -1, last - top + 1, last - hop + 2)
+        low_parts, high_parts = list(low_parts), list(high_parts)
+        blocks.append((-hop, hop, top, list(low_parts)))
+        blocks.append((hop, last - top, last - hop, list(high_parts)))
+
+    chunks = len(attended)
+    pieces = {0: attended}
+    masks = sorted(range(1, fast_count), key=lambda m: (m.bit_count(), m))
+    for mask in masks:
         own = [b for b in bits if b & mask]
-        if len(own) == 1:
-            pieces[mask] = [across(attended, mask)]
-            continue
-        edges = [rows * k // len(own) for k in range(len(own) + 1)]
-        pieces[mask] = []
-        for k, bit in enumerate(own):
-            whole = pieces[mask ^ bit]
-            whole = whole[0] if len(whole) == 1 else jnp.concatenate(whole, axis=0)
-            pieces[mask].append(across(whole[edges[k] : edges[k + 1]], bit))
-
+        pieces[mask] = [None] * chunks
+        for j in reversed(range(chunks)) if mask == 1 else range(chunks):
+            bit = own[j % len(own)]
+            pieces[mask][j] = across(pieces[mask ^ bit][j], bit)
+
+    b_all = pick(place, blocks, slow_count, head_devices)
     tiles = {}
-    for mask in [*range(1, fast_count), 0]:
-        mine, send = project(place, pieces[mask], b_blocks, slow_count, head_devices)
+    for mask in [*reversed(masks), 0]:
+        mine, send = project(pieces[mask], b_all, share)
         received = [
             lax.ppermute(
                 send[r - 1], "head", [(h, (h + r) % head_devices) for h in range(head_devices)]
@@ -441,6 +480,9 @@
         P("head", "ctx"),
         P("ctx", "head", None),
     )
-    return jax.shard_map(
+
+    step = jax.shard_map(
         local, mesh=mesh, in_specs=placed, out_specs=P("ctx", "head"), check_vma=False
     )
+    _, _ = split_ctx(mesh.shape["ctx"], mesh.shape["head"])
+    return step

time: 277 us -> 276 us (level)
  the two profiles are of different devices: /device:TPU:0 before, /device:TPU:28 now
where the time goes in v2:
time: 276 us; the launch traced here: 275 us
  waiting for transfers between devices  149 us (54%)
  starting transfers between devices  50.7 us (18%)
  Pallas kernels  45.6 us (17%)
  local copies, waits for them, and re-layouts  16.5 us (6%)
  blocking collectives  10 us (4%)
  other arithmetic  3.02 us (1%)
    ppermute x3, waiting for transfers between devices, local(): land_parts.append(lax.ppermute(land, 'ctx', pairs))  48.7 us
    all_to_all x2, waiting for transfers between devices, fetch(): got = lax.all_to_all(sent, 'ctx', split_axis=0, concat_axis=0, tiled=True)  41.4 us
    ppermute x11, waiting for transfers between devices, across(): return lax.ppermute(value, 'ctx', [(i, i ^ mask) for i in range(devices)])  41 us
    ppermute x12, starting transfers between devices, along(): return lax.ppermute(value, 'ctx', pairs)  20.4 us
    pallas_call x1, Pallas kernels, attention_scores(): pl.pallas_call(functools.partial(score_kernel, groups, heads, picks, step...  20.4 us
    ppermute x12, waiting for transfers between devices, along(): return lax.ppermute(value, 'ctx', pairs)  17.9 us
    all_to_all x2, starting transfers between devices, fetch(): got = lax.all_to_all(sent, 'ctx', split_axis=0, concat_axis=0, tiled=True)  14.3 us
    ppermute x11, starting transfers between devices, across(): return lax.ppermute(value, 'ctx', [(i, i ^ mask) for i in range(devices)])  12.2 us
  transfers between devices with their start and end apart: 32, of which 11 were waited for; matrix products, arithmetic and copies ran while one was open for 2% of the time, Pallas kernels for 14%

profile of v2, /device:TPU:28, one launch (start us, length us, event | category | flops | bytes accessed | tf_op | source)
XLA Modules:
  0.0 275.2 jit_solution(12323128538584021527)
XLA Ops:
  2.2 10.0 %all_to_all.19 = s32[16,1,8]{2,1,0:T(1,128)S(1)} all-to-all(s32[16,1,8]{2,1,0:T(1,128)S(1)} %bitcast.31), channel_id=1, replica_groups=mesh['ctx'=16,'head'=2] {'ctx'}, dimensions={0} | all-to-all | bytes 1024 | tf_op jit(solution)/shard_map/all_to_all | solution.py:386
  14.0 4.2 %gather_blocks.3 = bf16[128,64,128]{2,1,0:T(8,128)(2,1)} custom-call(s32[128]{0:T(128)} %reshape.41.asked_ref, bf16[1024,2048]{1,0:T(8,128)(2,1)} %source_ref.3), custom_call_target="tpu_custom_call" | custom-call | flops 67108864 | bytes 4194304 | tf_op jit(solution)/shard_map/gather_blocks/pallas_call | solution.py:72
  18.2 7.8 %all-to-all-start.2 = ((bf16[16,8,64,128]{3,2,1,0:T(8,128)(2,1)}), bf16[16,8,64,128]{3,2,1,0:T(8,128)(2,1)S(1)}, u32[]{:S(2)}, u32[]{:S(2)}) async-start(bf16[16,8,64,128]{3,2,1,0:T(8,128)(2,1)} %bitcast.26), calls=%async_computation.2 | async-start | bytes 4194304 | tf_op jit(solution)/shard_map/all_to_all | solution.py:415
  25.9 4.2 %gather_blocks.2 = bf16[128,64,128]{2,1,0:T(8,128)(2,1)} custom-call(s32[128]{0:T(128)} %reshape.41.asked_ref, bf16[1024,2048]{1,0:T(8,128)(2,1)} %source_ref.2), custom_call_target="tpu_custom_call" | custom-call | flops 67108864 | bytes 4194304 | tf_op jit(solution)/shard_map/gather_blocks/pallas_call | solution.py:72
  30.1 41.4 %all-to-all-done.2 = bf16[16,8,64,128]{3,2,1,0:T(8,128)(2,1)S(1)} async-done(((bf16[16,8,64,128]{3,2,1,0:T(8,128)(2,1)}), bf16[16,8,64,128]{3,2,1,0:T(8,128)(2,1)S(1)}, u32[]{:S(2)}, u32[]{:S(2)}) %all-to-all-start.2) | async-done | bytes 2097184 | tf_op jit(solution)/shard_map/all_to_all | solution.py:415
  71.5 6.5 %all-to-all-start.1 = ((bf16[16,8,64,128]{3,2,1,0:T(8,128)(2,1)}), bf16[16,8,64,128]{3,2,1,0:T(8,128)(2,1)}, u32[]{:S(2)}, u32[]{:S(2)}) async-start(bf16[16,8,64,128]{3,2,1,0:T(8,128)(2,1)} %bitcast.25), calls=%async_computation.1 | async-start | bytes 4194304 | tf_op jit(solution)/shard_map/all_to_all | solution.py:415
  78.7 1.5 collective-permute-start.1
  80.7 1.3 collective-permute-start.5
  82.0 5.5 %collective-permute-start.6 = (bf16[2048,256]{1,0:T(8,128)(2,1)S(1)}, bf16[2048,256]{1,0:T(8,128)(2,1)}, u32[]{:S(2)}, u32[]{:S(2)}) collective-permute-start(bf16[2048,256]{1,0:T(8,128)(2,1)S(1)} %copy-done.9), channel_id=1, source_target_pairs={{8,0},{10,2},{12,4},{14,6},{16,8},{18,10},{20,12},{22,14},{24,16},... | collective-permute-start | bytes 3145736 | tf_op jit(solution)/shard_map/ppermute | solution.py:382
  87.6 29.0 %collective-permute-done = bf16[1,2,16,2048]{3,2,1,0:T(8,128)(2,1)S(1)} collective-permute-done((bf16[1,2,16,2048]{3,2,1,0:T(8,128)(2,1)S(1)}, bf16[1,2,16,2048]{3,2,1,0:T(8,128)(2,1)S(1)}, u32[]{:S(2)}, u32[]{:S(2)}) %collective-permute-start) | collective-permute-done | bytes 131104 | tf_op jit(solution)/shard_map/ppermute | solution.py:408
  116.6 19.6 %collective-permute-done.1 = bf16[1,2,16,2048]{3,2,1,0:T(8,128)(2,1)S(1)} collective-permute-done((bf16[1,2,16,2048]{3,2,1,0:T(8,128)(2,1)S(1)}, bf16[1,2,16,2048]{3,2,1,0:T(8,128)(2,1)S(1)}, u32[]{:S(2)}, u32[]{:S(2)}) %collective-permute-start.1) | collective-permute-done | bytes 131104 | tf_op jit(solution)/shard_map/ppermute | solution.py:408
  136.3 1.4 collective-permute-start.3
  137.8 9.3 %collective-permute-done.3 = bf16[4,2,16,2048]{3,2,1,0:T(8,128)(2,1)S(1)} collective-permute-done((bf16[4,2,16,2048]{3,2,1,0:T(8,128)(2,1)S(1)}, bf16[4,2,16,2048]{3,2,1,0:T(8,128)(2,1)S(1)}, u32[]{:S(2)}, u32[]{:S(2)}) %collective-permute-start.3) | collective-permute-done | bytes 524320 | tf_op jit(solution)/shard_map/ppermute | solution.py:372
  147.4 1.3 collective-permute-start.7
  148.7 1.7 collective-permute-start.8
  151.5 2.3 fusion.7
  153.8 1.5 collective-permute-start.9
  155.3 13.2 %collective-permute-done.4 = bf16[8,2,16,2048]{3,2,1,0:T(8,128)(2,1)S(1)} collective-permute-done((bf16[8,2,16,2048]{3,2,1,0:T(8,128)(2,1)S(1)}, bf16[8,2,16,2048]{3,2,1,0:T(8,128)(2,1)S(1)}, u32[]{:S(2)}, u32[]{:S(2)}) %collective-permute-start.4) | collective-permute-done | bytes 1048608 | tf_op jit(solution)/shard_map/ppermute | solution.py:372
  168.6 1.4 copy-done.3
  169.9 1.5 collective-permute-start.10
  171.4 1.4 collective-permute-start.11
  172.8 8.2 %collective-permute-done.7.refs_3_ = bf16[2048,256]{1,0:T(8,128)(2,1)S(1)} collective-permute-done((bf16[2048,256]{1,0:T(8,128)(2,1)S(1)}, bf16[2048,256]{1,0:T(8,128)(2,1)S(1)}, u32[]{:S(2)}, u32[]{:S(2)}) %collective-permute-start.7) | collective-permute-done | bytes 1048608 | tf_op jit(solution)/shard_map/ppermute | solution.py:382
  182.1 1.4 collective-permute-start.12
  183.5 1.6 copy-done.4
  185.1 1.2 copy-done.6
  186.3 1.2 copy-done.7
  187.6 20.4 %attention_scores.1 = (bf16[256,4096]{1,0:T(8,128)(2,1)S(1)}, f32[256,2048]{1,0:T(8,128)S(1)}) custom-call(s32[256]{0:T(256)S(1)} %multiply_add_fusion.cell_ref, bf16[256,2048]{1,0:T(8,128)(2,1)S(1)} %copy-done.5, bf16[16,2,16,2048]{3,2,1,0:T(8,128)(2,1)S(1)} %copy-done.4, bf16[256,2048]{1,0:T(8,128)(2,1)S(1)} %copy-done.6, bf16[256,2048]{1,0:T(8,128)(2,1)S(1)} %copy-done.7, ...), custom_call_target="tpu_custom_call" | custom-call | flops 4831838208 | bytes 8388608 | tf_op jit(solution)/shard_map/attention_scores/pallas_call | solution.py:172
  207.9 2.2 attention_values.1
  210.1 1.3 collective-permute-start.19
  211.5 1.3 collective-permute-start.13
  212.8 1.3 collective-permute-start.14
  214.8 7.3 %collective-permute-done.19.refs_1_ = bf16[128,2048]{1,0:T(8,128)(2,1)S(1)} collective-permute-done((bf16[128,2048]{1,0:T(8,128)(2,1)S(1)}, bf16[128,2048]{1,0:T(8,128)(2,1)S(1)}, u32[]{:S(2)}, u32[]{:S(2)}) %collective-permute-start.19) | collective-permute-done | bytes 524320 | tf_op jit(solution)/shard_map/ppermute | solution.py:372
  222.1 1.5 collective-permute-start.16
  224.8 3.6 %collective-permute-done.13.refs_9_ = bf16[1024,256]{1,0:T(8,128)(2,1)S(1)} collective-permute-done((bf16[1024,256]{1,0:T(8,128)(2,1)}, bf16[1024,256]{1,0:T(8,128)(2,1)S(1)}, u32[]{:S(2)}, u32[]{:S(2)}) %collective-permute-start.13) | collective-permute-done | bytes 524320 | tf_op jit(solution)/shard_map/ppermute | solution.py:382
  228.4 2.0 collective-permute-start.23
  230.4 6.0 %collective-permute-done.14.refs_10_ = bf16[1024,256]{1,0:T(8,128)(2,1)S(1)} collective-permute-done((bf16[1024,256]{1,0:T(8,128)(2,1)}, bf16[1024,256]{1,0:T(8,128)(2,1)S(1)}, u32[]{:S(2)}, u32[]{:S(2)}) %collective-permute-start.14) | collective-permute-done | bytes 524320 | tf_op jit(solution)/shard_map/ppermute | solution.py:382
  238.1 1.7 collective-permute-start.27
  240.4 4.9 %pick.1.refs_2_ = bf16[4,2048,256]{2,1,0:T(8,128)(2,1)} custom-call(s32[3]{0:T(128)} %pad_add_fusion.place_ref, bf16[2048,256]{1,0:T(8,128)(2,1)} %refs_0_.1, bf16[2048,256]{1,0:T(8,128)(2,1)} %copy-done.8, bf16[2048,256]{1,0:T(8,128)(2,1)} %collective-permute-done.6.refs_2_, bf16[2048,256]{1,0:T(8,128)(2,1)} %copy-done.10, ...), custom_call_target="tpu_custom_call" | custom-call | flops 134217728 | bytes 8388608 | tf_op jit(solution)/shard_map/pick/pallas_call | solution.py:262
  245.3 2.2 copy-done
  247.5 2.4 project.5
  250.1 1.3 project.4
  252.6 2.3 project.6
  255.0 1.3 project.7
  256.9 1.2 collective-permute-start.21
  258.7 2.1 collective-permute-start.29
  260.8 5.4 %collective-permute-done.21.refs_1_ = bf16[256,512]{1,0:T(8,128)(2,1)S(1)} collective-permute-done((bf16[256,512]{1,0:T(8,128)(2,1)S(1)}, bf16[256,512]{1,0:T(8,128)(2,1)S(1)}, u32[]{:S(2)}, u32[]{:S(2)}) %collective-permute-start.21) | collective-permute-done | bytes 262176 | tf_op jit(solution)/shard_map/ppermute | solution.py:372
  266.2 5.7 %collective-permute-done.25.refs_2_ = bf16[256,512]{1,0:T(8,128)(2,1)S(1)} collective-permute-done((bf16[256,512]{1,0:T(8,128)(2,1)S(1)}, bf16[256,512]{1,0:T(8,128)(2,1)S(1)}, u32[]{:S(2)}, u32[]{:S(2)}) %collective-permute-start.25) | collective-permute-done | bytes 262176 | tf_op jit(solution)/shard_map/ppermute | solution.py:372
  272.7 2.5 assemble.1
  (98 shorter events, 15.2 us)
Async XLA Ops:
  18.2 53.4 %all-to-all-start.2 = ((bf16[16,8,64,128]{3,2,1,0:T(8,128)(2,1)}), bf16[16,8,64,128]{3,2,1,0:T(8,128)(2,1)S(1)}, u32[]{:S(2)}, u32[]{:S(2)}) async-start(bf16[16,8,64,128]{3,2,1,0:T(8,128)(2,1)} %bitcast.26), calls=%async_computation.2 | async-start | bytes 4194304 | tf_op jit(solution)/shard_map/all_to_all | solution.py:415
  71.5 6.5 %copy-start.14 = (bf16[16,2048]{1,0:T(8,128)(2,1)S(1)}, bf16[16,2048]{1,0:T(8,128)(2,1)}, u32[]{:S(2)}) copy-start(bf16[16,2048]{1,0:T(8,128)(2,1)} %param.15) | copy-start | bytes 196612
  71.5 6.5 %copy-start.15 = (bf16[16,2048]{1,0:T(8,128)(2,1)S(1)}, bf16[16,2048]{1,0:T(8,128)(2,1)}, u32[]{:S(2)}) copy-start(bf16[16,2048]{1,0:T(8,128)(2,1)} %param.14) | copy-start | bytes 196612
  71.5 9.2 %copy-start.9 = (bf16[2048,256]{1,0:T(8,128)(2,1)S(1)}, bf16[2048,256]{1,0:T(8,128)(2,1)}, u32[]{:S(2)}) copy-start(bf16[2048,256]{1,0:T(8,128)(2,1)} %refs_0_.1) | copy-start | bytes 3145732
  71.5 112.0 %all-to-all-start.1 = ((bf16[16,8,64,128]{3,2,1,0:T(8,128)(2,1)}), bf16[16,8,64,128]{3,2,1,0:T(8,128)(2,1)}, u32[]{:S(2)}, u32[]{:S(2)}) async-start(bf16[16,8,64,128]{3,2,1,0:T(8,128)(2,1)} %bitcast.25), calls=%async_computation.1 | async-start | bytes 4194304 | tf_op jit(solution)/shard_map/all_to_all | solution.py:415
  78.1 38.5 %collective-permute-start = (bf16[1,2,16,2048]{3,2,1,0:T(8,128)(2,1)S(1)}, bf16[1,2,16,2048]{3,2,1,0:T(8,128)(2,1)S(1)}, u32[]{:S(2)}, u32[]{:S(2)}) collective-permute-start(bf16[1,2,16,2048]{3,2,1,0:T(8,128)(2,1)S(1)} %maximum_bitcast_fusion), channel_id=1, source_target_pairs={{0,8},{2,10},{4,12},{6,14},{8,16},{10,18},{12,20},{14,22},{16,24},... | collective-permute-start | bytes 393224 | tf_op jit(solution)/shard_map/ppermute | solution.py:408
  78.7 57.5 %collective-permute-start.1 = (bf16[1,2,16,2048]{3,2,1,0:T(8,128)(2,1)S(1)}, bf16[1,2,16,2048]{3,2,1,0:T(8,128)(2,1)S(1)}, u32[]{:S(2)}, u32[]{:S(2)}) collective-permute-start(bf16[1,2,16,2048]{3,2,1,0:T(8,128)(2,1)S(1)} %maximum_bitcast_fusion), channel_id=1, source_target_pairs={{0,16},{2,18},{4,20},{6,22},{8,24},{10,26},{12,28},{14,30},{16,0},... | collective-permute-start | bytes 393224 | tf_op jit(solution)/shard_map/ppermute | solution.py:408
  80.2 56.1 %collective-permute-start.2 = (bf16[1,2,16,2048]{3,2,1,0:T(8,128)(2,1)S(1)}, bf16[1,2,16,2048]{3,2,1,0:T(8,128)(2,1)S(1)}, u32[]{:S(2)}, u32[]{:S(2)}) collective-permute-start(bf16[1,2,16,2048]{3,2,1,0:T(8,128)(2,1)S(1)} %maximum_bitcast_fusion), channel_id=1, source_target_pairs={{0,24},{2,26},{4,28},{6,30},{8,0},{10,2},{12,4},{14,6},{16,8},{18,... | collective-permute-start | bytes 393224 | tf_op jit(solution)/shard_map/ppermute | solution.py:408
  80.7 66.6 %collective-permute-start.5 = (bf16[2048,256]{1,0:T(8,128)(2,1)S(1)}, bf16[2048,256]{1,0:T(8,128)(2,1)S(1)}, u32[]{:S(2)}, u32[]{:S(2)}) collective-permute-start(bf16[2048,256]{1,0:T(8,128)(2,1)S(1)} %copy-done.9), channel_id=1, source_target_pairs={{0,8},{2,10},{4,12},{6,14},{8,16},{10,18},{12,20},{14,22},{16,24},... | collective-permute-start | bytes 3145736 | tf_op jit(solution)/shard_map/ppermute | solution.py:382
  82.0 66.6 %collective-permute-start.6 = (bf16[2048,256]{1,0:T(8,128)(2,1)S(1)}, bf16[2048,256]{1,0:T(8,128)(2,1)}, u32[]{:S(2)}, u32[]{:S(2)}) collective-permute-start(bf16[2048,256]{1,0:T(8,128)(2,1)S(1)} %copy-done.9), channel_id=1, source_target_pairs={{8,0},{10,2},{12,4},{14,6},{16,8},{18,10},{20,12},{22,14},{24,16},... | collective-permute-start | bytes 3145736 | tf_op jit(solution)/shard_map/ppermute | solution.py:382
  136.3 10.8 %collective-permute-start.3 = (bf16[4,2,16,2048]{3,2,1,0:T(8,128)(2,1)S(1)}, bf16[4,2,16,2048]{3,2,1,0:T(8,128)(2,1)S(1)}, u32[]{:S(2)}, u32[]{:S(2)}) collective-permute-start(bf16[4,2,16,2048]{3,2,1,0:T(8,128)(2,1)S(1)} %pad_maximum_fusion), channel_id=1, source_target_pairs={{0,2},{2,0},{4,6},{6,4},{8,10},{10,8},{12,14},{14,12},{16,18},{18,... | collective-permute-start | bytes 1572872 | tf_op jit(solution)/shard_map/ppermute | solution.py:372
  147.3 21.2 %collective-permute-start.4 = (bf16[8,2,16,2048]{3,2,1,0:T(8,128)(2,1)S(1)}, bf16[8,2,16,2048]{3,2,1,0:T(8,128)(2,1)S(1)}, u32[]{:S(2)}, u32[]{:S(2)}) collective-permute-start(bf16[8,2,16,2048]{3,2,1,0:T(8,128)(2,1)S(1)} %get-tuple-element.41), channel_id=1, source_target_pairs={{0,4},{2,6},{4,0},{6,2},{8,12},{10,14},{12,8},{14,10},{16,20},{18,... | collective-permute-start | bytes 3145736 | tf_op jit(solution)/shard_map/ppermute | solution.py:372
  147.4 6.5 %copy-start.8 = (bf16[2048,256]{1,0:T(8,128)(2,1)}, bf16[2048,256]{1,0:T(8,128)(2,1)S(1)}, u32[]{:S(2)}) copy-start(bf16[2048,256]{1,0:T(8,128)(2,1)S(1)} %collective-permute-done.5.refs_1_) | copy-start | bytes 3145732
  147.4 33.7 %collective-permute-start.7 = (bf16[2048,256]{1,0:T(8,128)(2,1)S(1)}, bf16[2048,256]{1,0:T(8,128)(2,1)S(1)}, u32[]{:S(2)}, u32[]{:S(2)}) collective-permute-start(bf16[2048,256]{1,0:T(8,128)(2,1)S(1)} %collective-permute-done.5.refs_1_), channel_id=1, source_target_pairs={{16,24},{18,26},{20,28},{22,30},{17,25},{19,27},{21,29},{23,31}} | collective-permute-start | bytes 3145736 | tf_op jit(solution)/shard_map/ppermute | solution.py:382
  148.7 61.5 %collective-permute-start.8 = (bf16[2048,256]{1,0:T(8,128)(2,1)}, bf16[2048,256]{1,0:T(8,128)(2,1)}, u32[]{:S(2)}, u32[]{:S(2)}) collective-permute-start(bf16[2048,256]{1,0:T(8,128)(2,1)} %collective-permute-done.6.refs_2_), channel_id=1, source_target_pairs={{8,0},{10,2},{12,4},{14,6},{9,1},{11,3},{13,5},{15,7}} | collective-permute-start | bytes 3145736 | tf_op jit(solution)/shard_map/ppermute | solution.py:382
  151.5 32.0 %copy-start.5 = (bf16[256,2048]{1,0:T(8,128)(2,1)S(1)}, bf16[256,2048]{1,0:T(8,128)(2,1)}, u32[]{:S(2)}) copy-start(bf16[256,2048]{1,0:T(8,128)(2,1)} %q_ref.1) | copy-start | bytes 3145732
  153.8 57.6 %collective-permute-start.9 = (bf16[1024,256]{1,0:T(8,128)(2,1)}, bf16[1024,256]{1,0:T(8,128)(2,1)}, u32[]{:S(2)}, u32[]{:S(2)}) collective-permute-start(bf16[1024,256]{1,0:T(8,128)(2,1)} %get-tuple-element.25), channel_id=1, source_target_pairs={{8,16},{10,18},{12,20},{14,22},{9,17},{11,19},{13,21},{15,23}} | collective-permute-start | bytes 1572872 | tf_op jit(solution)/shard_map/ppermute | solution.py:382
  168.6 1.4 copy-start.3
  169.9 41.5 %collective-permute-start.10 = (bf16[1024,256]{1,0:T(8,128)(2,1)}, bf16[1024,256]{1,0:T(8,128)(2,1)}, u32[]{:S(2)}, u32[]{:S(2)}) collective-permute-start(bf16[1024,256]{1,0:T(8,128)(2,1)} %get-tuple-element.26), channel_id=1, source_target_pairs={{8,16},{10,18},{12,20},{14,22},{9,17},{11,19},{13,21},{15,23}} | collective-permute-start | bytes 1572872 | tf_op jit(solution)/shard_map/ppermute | solution.py:382
  171.4 41.4 %collective-permute-start.11 = (bf16[1024,256]{1,0:T(8,128)(2,1)}, bf16[1024,256]{1,0:T(8,128)(2,1)}, u32[]{:S(2)}, u32[]{:S(2)}) collective-permute-start(bf16[1024,256]{1,0:T(8,128)(2,1)} %get-tuple-element.27), channel_id=1, source_target_pairs={{16,8},{18,10},{20,12},{22,14},{17,9},{19,11},{21,13},{23,15}} | collective-permute-start | bytes 1572872 | tf_op jit(solution)/shard_map/ppermute | solution.py:382
  181.1 1.0 copy-start.10
  182.1 32.0 %collective-permute-start.12 = (bf16[1024,256]{1,0:T(8,128)(2,1)}, bf16[1024,256]{1,0:T(8,128)(2,1)}, u32[]{:S(2)}, u32[]{:S(2)}) collective-permute-start(bf16[1024,256]{1,0:T(8,128)(2,1)} %get-tuple-element.28), channel_id=1, source_target_pairs={{16,8},{18,10},{20,12},{22,14},{17,9},{19,11},{21,13},{23,15}} | collective-permute-start | bytes 1572872 | tf_op jit(solution)/shard_map/ppermute | solution.py:382
  183.5 1.6 copy-start.4
  185.1 1.2 copy-start.6
  186.3 1.2 copy-start.7
  210.1 12.0 %collective-permute-start.19 = (bf16[128,2048]{1,0:T(8,128)(2,1)S(1)}, bf16[128,2048]{1,0:T(8,128)(2,1)S(1)}, u32[]{:S(2)}, u32[]{:S(2)}) collective-permute-start(bf16[128,2048]{1,0:T(8,128)(2,1)S(1)} %get-tuple-element.24.refs_1_), channel_id=1, source_target_pairs={{0,2},{2,0},{4,6},{6,4},{8,10},{10,8},{12,14},{14,12},{16,18},{18,... | collective-permute-start | bytes 1572872 | tf_op jit(solution)/shard_map/ppermute | solution.py:372
  211.4 12.2 %collective-permute-start.22 = (bf16[128,2048]{1,0:T(8,128)(2,1)S(1)}, bf16[128,2048]{1,0:T(8,128)(2,1)S(1)}, u32[]{:S(2)}, u32[]{:S(2)}) collective-permute-start(bf16[128,2048]{1,0:T(8,128)(2,1)S(1)} %get-tuple-element.23.refs_0_), channel_id=1, source_target_pairs={{0,4},{2,6},{4,0},{6,2},{8,12},{10,14},{12,8},{14,10},{16,20},{18,... | collective-permute-start | bytes 1572872 | tf_op jit(solution)/shard_map/ppermute | solution.py:372
  211.5 16.9 %collective-permute-start.13 = (bf16[1024,256]{1,0:T(8,128)(2,1)}, bf16[1024,256]{1,0:T(8,128)(2,1)S(1)}, u32[]{:S(2)}, u32[]{:S(2)}) collective-permute-start(bf16[1024,256]{1,0:T(8,128)(2,1)} %collective-permute-done.9.refs_5_), channel_id=1, source_target_pairs={{16,24},{18,26},{20,28},{22,30},{17,25},{19,27},{21,29},{23,31}} | collective-permute-start | bytes 1572872 | tf_op jit(solution)/shard_map/ppermute | solution.py:382
  212.8 23.6 %collective-permute-start.14 = (bf16[1024,256]{1,0:T(8,128)(2,1)}, bf16[1024,256]{1,0:T(8,128)(2,1)S(1)}, u32[]{:S(2)}, u32[]{:S(2)}) collective-permute-start(bf16[1024,256]{1,0:T(8,128)(2,1)} %collective-permute-done.10.refs_6_), channel_id=1, source_target_pairs={{16,24},{18,26},{20,28},{22,30},{17,25},{19,27},{21,29},{23,31}} | collective-permute-start | bytes 1572872 | tf_op jit(solution)/shard_map/ppermute | solution.py:382
  214.1 23.2 %collective-permute-start.15 = (bf16[1024,256]{1,0:T(8,128)(2,1)}, bf16[1024,256]{1,0:T(8,128)(2,1)S(1)}, u32[]{:S(2)}, u32[]{:S(2)}) collective-permute-start(bf16[1024,256]{1,0:T(8,128)(2,1)} %collective-permute-done.11.refs_7_), channel_id=1, source_target_pairs={{8,0},{10,2},{12,4},{14,6},{9,1},{11,3},{13,5},{15,7}} | collective-permute-start | bytes 1572872 | tf_op jit(solution)/shard_map/ppermute | solution.py:382
  222.1 18.3 %collective-permute-start.16 = (bf16[1024,256]{1,0:T(8,128)(2,1)}, bf16[1024,256]{1,0:T(8,128)(2,1)}, u32[]{:S(2)}, u32[]{:S(2)}) collective-permute-start(bf16[1024,256]{1,0:T(8,128)(2,1)} %collective-permute-done.12.refs_8_), channel_id=1, source_target_pairs={{8,0},{10,2},{12,4},{14,6},{9,1},{11,3},{13,5},{15,7}} | collective-permute-start | bytes 1572872 | tf_op jit(solution)/shard_map/ppermute | solution.py:382
  223.6 21.7 %collective-permute-start.18 = (bf16[128,2048]{1,0:T(8,128)(2,1)S(1)}, bf16[128,2048]{1,0:T(8,128)(2,1)}, u32[]{:S(2)}, u32[]{:S(2)}) collective-permute-start(bf16[128,2048]{1,0:T(8,128)(2,1)S(1)} %get-tuple-element.23.refs_0_), channel_id=1, source_target_pairs={{0,2},{2,0},{4,6},{6,4},{8,10},{10,8},{12,14},{14,12},{16,18},{18,... | collective-permute-start | bytes 1572872 | tf_op jit(solution)/shard_map/ppermute | solution.py:372
  228.4 2.0 copy-start.11
  228.4 24.3 %collective-permute-start.23 = (bf16[128,2048]{1,0:T(8,128)(2,1)S(1)}, bf16[128,2048]{1,0:T(8,128)(2,1)}, u32[]{:S(2)}, u32[]{:S(2)}) collective-permute-start(bf16[128,2048]{1,0:T(8,128)(2,1)S(1)} %get-tuple-element.24.refs_1_), channel_id=1, source_target_pairs={{0,4},{2,6},{4,0},{6,2},{8,12},{10,14},{12,8},{14,10},{16,20},{18,... | collective-permute-start | bytes 1572872 | tf_op jit(solution)/shard_map/ppermute | solution.py:372
  236.4 0.9 copy-start.12
  236.4 18.6 %collective-permute-start.26 = (bf16[128,2048]{1,0:T(8,128)(2,1)S(1)}, bf16[128,2048]{1,0:T(8,128)(2,1)S(1)}, u32[]{:S(2)}, u32[]{:S(2)}) collective-permute-start(bf16[128,2048]{1,0:T(8,128)(2,1)S(1)} %collective-permute-done.22.refs_0_), channel_id=1, source_target_pairs={{0,2},{2,0},{4,6},{6,4},{8,10},{10,8},{12,14},{14,12},{16,18},{18,... | collective-permute-start | bytes 1572872 | tf_op jit(solution)/shard_map/ppermute | solution.py:372
  238.1 16.9 %collective-permute-start.27 = (bf16[128,2048]{1,0:T(8,128)(2,1)S(1)}, bf16[128,2048]{1,0:T(8,128)(2,1)S(1)}, u32[]{:S(2)}, u32[]{:S(2)}) collective-permute-start(bf16[128,2048]{1,0:T(8,128)(2,1)S(1)} %collective-permute-done.19.refs_1_), channel_id=1, source_target_pairs={{0,4},{2,6},{4,0},{6,2},{8,12},{10,14},{12,8},{14,10},{16,20},{18,... | collective-permute-start | bytes 1572872 | tf_op jit(solution)/shard_map/ppermute | solution.py:372
  245.3 2.2 copy-start
  247.5 2.5 copy-start.1
  250.0 6.9 %collective-permute-start.20 = (bf16[256,512]{1,0:T(8,128)(2,1)S(1)}, bf16[256,512]{1,0:T(8,128)(2,1)S(1)}, u32[]{:S(2)}, u32[]{:S(2)}) collective-permute-start(bf16[256,512]{1,0:T(8,128)(2,1)S(1)} %bitcast.22), channel_id=1, source_target_pairs={{0,1},{1,0},{2,3},{3,2},{4,5},{5,4},{6,7},{7,6},{8,9},{9,8},{10,11... | collective-permute-start | bytes 786440 | tf_op jit(solution)/shard_map/ppermute | solution.py:457
  252.1 8.7 %collective-permute-start.17 = (bf16[256,512]{1,0:T(8,128)(2,1)S(1)}, bf16[256,512]{1,0:T(8,128)(2,1)S(1)}, u32[]{:S(2)}, u32[]{:S(2)}) collective-permute-start(bf16[256,512]{1,0:T(8,128)(2,1)S(1)} %bitcast.21), channel_id=1, source_target_pairs={{0,1},{1,0},{2,3},{3,2},{4,5},{5,4},{6,7},{7,6},{8,9},{9,8},{10,11... | collective-permute-start | bytes 786440 | tf_op jit(solution)/shard_map/ppermute | solution.py:457
  254.9 3.3 %collective-permute-start.24 = (bf16[256,512]{1,0:T(8,128)(2,1)S(1)}, bf16[256,512]{1,0:T(8,128)(2,1)S(1)}, u32[]{:S(2)}, u32[]{:S(2)}) collective-permute-start(bf16[256,512]{1,0:T(8,128)(2,1)S(1)} %bitcast.23), channel_id=1, source_target_pairs={{0,1},{1,0},{2,3},{3,2},{4,5},{5,4},{6,7},{7,6},{8,9},{9,8},{10,11... | collective-permute-start | bytes 786440 | tf_op jit(solution)/shard_map/ppermute | solution.py:457
  256.3 2.3 collective-permute-start.28
  256.9 9.2 %collective-permute-start.21 = (bf16[256,512]{1,0:T(8,128)(2,1)S(1)}, bf16[256,512]{1,0:T(8,128)(2,1)S(1)}, u32[]{:S(2)}, u32[]{:S(2)}) collective-permute-start(bf16[256,512]{1,0:T(8,128)(2,1)S(1)} %add_convert_fusion.2), channel_id=1, source_target_pairs={{0,2},{2,0},{4,6},{6,4},{8,10},{10,8},{12,14},{14,12},{16,18},{18,... | collective-permute-start | bytes 786440 | tf_op jit(solution)/shard_map/ppermute | solution.py:372
  258.2 13.6 %collective-permute-start.25 = (bf16[256,512]{1,0:T(8,128)(2,1)S(1)}, bf16[256,512]{1,0:T(8,128)(2,1)S(1)}, u32[]{:S(2)}, u32[]{:S(2)}) collective-permute-start(bf16[256,512]{1,0:T(8,128)(2,1)S(1)} %add_convert_fusion.1), channel_id=1, source_target_pairs={{0,4},{2,6},{4,0},{6,2},{8,12},{10,14},{12,8},{14,10},{16,20},{18,... | collective-permute-start | bytes 786440 | tf_op jit(solution)/shard_map/ppermute | solution.py:372
  258.7 13.2 %collective-permute-start.29 = (bf16[256,512]{1,0:T(8,128)(2,1)S(1)}, bf16[256,512]{1,0:T(8,128)(2,1)S(1)}, u32[]{:S(2)}, u32[]{:S(2)}) collective-permute-start(bf16[256,512]{1,0:T(8,128)(2,1)S(1)} %add_convert_fusion), channel_id=1, source_target_pairs={{0,6},{2,4},{4,2},{6,0},{8,14},{10,12},{12,10},{14,8},{16,22},{18,... | collective-permute-start | bytes 786440 | tf_op jit(solution)/shard_map/ppermute | solution.py:372
  260.8 11.1 %copy-start.16 = (bf16[256,512]{1,0:T(8,128)(2,1)}, bf16[256,512]{1,0:T(8,128)(2,1)S(1)}, u32[]{:S(2)}) copy-start(bf16[256,512]{1,0:T(8,128)(2,1)S(1)} %collective-permute-done.17.refs_0_) | copy-start | bytes 786436
  266.2 5.7 %copy-start.17 = (bf16[256,512]{1,0:T(8,128)(2,1)}, bf16[256,512]{1,0:T(8,128)(2,1)S(1)}, u32[]{:S(2)}) copy-start(bf16[256,512]{1,0:T(8,128)(2,1)S(1)} %collective-permute-done.21.refs_1_) | copy-start | bytes 786436
  (4 other events, 3.1 us)

commit v3 on v2

--- a/solution.py
+++ b/solution.py
@@ -82,6 +82,60 @@
         ),
         name="gather_blocks",
     )(asked, source)
+
+
+def spread_kernel(heads, asked_ref, place_ref, source_ref, *refs):
+    outs, sem = refs[:-1], refs[-1]
+    most, _, size = outs[0].shape
+    for mask, out_ref in enumerate(outs):
+        base = (place_ref[3] ^ mask) * most
+        for slot in range(most):
+            code = asked_ref[base + slot]
+            row = pl.multiple_of(lax.div(code, heads) * BLOCK, BLOCK)
+            column = pl.multiple_of(lax.rem(code, heads) * size, size)
+            pltpu.make_async_copy(
+                source_ref.at[pl.ds(row, BLOCK), pl.ds(column, size)],
+                out_ref.at[slot],
+                sem.at[mask],
+            ).start()
+    for mask, out_ref in enumerate(outs):
+        pltpu.make_async_copy(out_ref, out_ref, sem.at[mask]).wait()
+
+
+def spread_blocks(asked, place, source, heads, devices):
+    most = asked.shape[0] // devices
+    size = source.shape[1] // heads
+    return pl.pallas_call(
+        functools.partial(spread_kernel, heads),
+        out_shape=[jax.ShapeDtypeStruct((most, BLOCK, size), source.dtype)] * devices,
+        in_specs=[SMEM, SMEM, HBM],
+        out_specs=[VMEM] * devices,
+        scratch_shapes=[pltpu.SemaphoreType.DMA((devices,))],
+        cost_estimate=pl.CostEstimate(
+            flops=asked.shape[0] * BLOCK * size * 64,
+            bytes_accessed=4 * asked.shape[0] * BLOCK * size,
+            transcendentals=0,
+        ),
+        name="spread_blocks",
+    )(asked, place, source)
+
+
+def fence_kernel(in_ref, out_ref):
+    def move(i, carry):
+        out_ref[i] = in_ref[i]
+        return carry
+
+    lax.fori_loop(0, in_ref.shape[0], move, 0)
+
+
+def fence(table):
+    return pl.pallas_call(
+        fence_kernel,
+        out_shape=jax.ShapeDtypeStruct(table.shape, table.dtype),
+        in_specs=[SMEM],
+        out_specs=SMEM,
+        name="fence",
+    )(table)
 
 
 def nt_dot(a, b):
@@ -139,8 +193,22 @@
             )
 
 
-def value_kernel(groups, heads, picks, step_heads, cell_ref, weight_ref, acc_ref, fv_ref, *outs):
+def value_kernel(groups, heads, picks, step_heads, devices, cell_ref, weight_ref, acc_ref, *refs):
+    sources, outs, (fv_ref, sem) = refs[:devices], refs[devices:-2], refs[-2:]
     size = acc_ref.shape[1] // step_heads
+    most = sources[0].shape[0]
+
+    @pl.when(pl.program_id(0) == 0)
+    def _():
+        copies = [
+            pltpu.make_async_copy(source, fv_ref.at[pl.ds(k * most, most)], sem.at[k])
+            for k, source in enumerate(sources)
+        ]
+        for copy in copies:
+            copy.start()
+        for copy in copies:
+            copy.wait()
+
     first_head = pl.program_id(0) * step_heads
     chosen = picks * BLOCK
     for hh in range(step_heads):
@@ -203,6 +271,8 @@
 def attention_values(cell, weights, part, fetched_values, dims):
     groups, heads, picks = dims
     rows, width = part.shape
+    devices = len(fetched_values)
+    most = fetched_values[0].shape[0]
     size = width // heads
     step = math.gcd(heads, 4)
     wide = step * size
@@ -210,14 +280,18 @@
     chunks = math.gcd(groups, 2)
     by_head = lambda i, c: (0, i)
     return pl.pallas_call(
-        functools.partial(value_kernel, groups, heads, picks, step),
+        functools.partial(value_kernel, groups, heads, picks, step, devices),
         grid_spec=pltpu.PrefetchScalarGridSpec(
             num_scalar_prefetch=1,
             grid=(heads // step,),
             in_specs=[
                 pl.BlockSpec((rows, step * chosen), by_head),
                 pl.BlockSpec((rows, wide), by_head),
-                pl.BlockSpec(fetched_values.shape, lambda i, c: (0, 0, 0)),
+                *[HBM] * devices,
+            ],
+            scratch_shapes=[
+                pltpu.VMEM((devices * most,) + fetched_values[0].shape[1:], jnp.bfloat16),
+                pltpu.SemaphoreType.DMA((devices,)),
             ],
             out_specs=[pl.BlockSpec((rows // chunks, wide), by_head)] * chunks,
         ),
@@ -229,7 +303,7 @@
             transcendentals=0,
         ),
         name="attention_values",
-    )(cell, weights, part, fetched_values)
+    )(cell, weights, part, *fetched_values)
 
 
 def pick_kernel(slow_count, head_devices, table, place_ref, *refs):
@@ -261,18 +335,18 @@
     depth, width = sum(c.shape[0] for c in blocks[0][3]), arrays[0].shape[1]
     return pl.pallas_call(
         functools.partial(pick_kernel, slow_count, head_devices, table),
-        out_shape=jax.ShapeDtypeStruct((slow_count, depth, width), jnp.bfloat16),
+        out_shape=pltpu.VMEM((slow_count, depth, width), jnp.bfloat16),
         in_specs=[SMEM] + [HBM] * len(arrays),
         out_specs=VMEM,
         scratch_shapes=[pltpu.SemaphoreType.DMA((slow_count,))],
-        compiler_params=pltpu.CompilerParams(vmem_limit_bytes=60 * 1024 * 1024),
+        compiler_params=pltpu.CompilerParams(vmem_limit_bytes=LIMIT // 2),
         cost_estimate=pl.CostEstimate(
             flops=64 * depth * width * slow_count,
             bytes_accessed=4 * depth * width * slow_count,
             transcendentals=0,
         ),
         name="pick",
-    )(place, *arrays)
+    )(place, *[pltpu.with_memory_space_constraint(a, pltpu.HBM) for a in arrays])
 
 
 def project_kernel(share, a_count, *refs):
@@ -365,7 +439,9 @@
     share = slow_count // head_devices
     bits = [1 << k for k in range(fast_count.bit_length() - 1)]
     index = lax.axis_index("ctx")
-    place = jnp.stack([index // fast_count, lax.axis_index("head"), index % fast_count])
+    place = jnp.stack(
+        [index // fast_count, lax.axis_index("head"), index % fast_count, index]
+    )
     place = place.astype(jnp.int32)
 
     def across(value, mask):
@@ -410,19 +486,20 @@
     for bit in bits:
         land = jnp.concatenate([land, across(land, bit)], axis=0)
 
-    def fetch(source):
-        sent = gather_blocks(asked_for, source, heads).reshape(devices, -1, BLOCK, size)
-        got = lax.all_to_all(sent, "ctx", split_axis=0, concat_axis=0, tiled=True)
-        return got.reshape(-1, BLOCK, size)
-
-    fetched_keys = fetch(cache_keys)
-    fetched_values = fetch(cache_values)
+    sent = gather_blocks(asked_for, cache_keys, heads).reshape(devices, -1, BLOCK, size)
+    got = lax.all_to_all(sent, "ctx", split_axis=0, concat_axis=0, tiled=True)
+    fetched_keys = got.reshape(-1, BLOCK, size)
+    sent = spread_blocks(asked_for, place, cache_values, heads, devices)
+    fetched_values = [sent[0]] + [across(sent[m], m) for m in range(1, devices)]
+    cell = fence(cell)
+    most = asked.shape[1]
+    partner_cell = (cell // most ^ index) * most + cell % most
 
     dims = (groups, heads, picks)
     weights, part = attention_scores(
         cell, queries, land, span_keys, span_values, fetched_keys, dims
     )
-    attended = attention_values(cell, weights, part, fetched_values, dims)
+    attended = attention_values(partner_cell, weights, part, fetched_values, dims)
 
     if slow_count > 3:
         low_parts, high_parts, _ = lax.optimization_barrier(
@@ -451,7 +528,7 @@
 
     b_all = pick(place, blocks, slow_count, head_devices)
     tiles = {}
-    for mask in [*reversed(masks), 0]:
+    for mask in [*masks, 0]:
         mine, send = project(pieces[mask], b_all, share)
         received = [
             lax.ppermute(

time: 276 us -> 277 us (level)
  the two profiles are of different devices: /device:TPU:28 before, /device:TPU:8 now
where the time goes in v3:
time: 277 us; the launch traced here: 276 us
  waiting for transfers between devices  112 us (40%)
  starting transfers between devices  77.9 us (28%)
  Pallas kernels  45.4 us (16%)
  local copies, waits for them, and re-layouts  22 us (8%)
  blocking collectives  13 us (5%)
  other arithmetic  4.49 us (2%)
    ppermute x26, waiting for transfers between devices, across(): return lax.ppermute(value, 'ctx', [(i, i ^ mask) for i in range(devices)])  62.6 us
    ppermute x26, starting transfers between devices, across(): return lax.ppermute(value, 'ctx', [(i, i ^ mask) for i in range(devices)])  40.2 us
    ppermute x3, waiting for transfers between devices, local(): land_parts.append(lax.ppermute(land, 'ctx', pairs))  39.5 us
    ppermute x12, starting transfers between devices, along(): return lax.ppermute(value, 'ctx', pairs)  27.1 us
    pallas_call x1, Pallas kernels, attention_scores(): pl.pallas_call(functools.partial(score_kernel, groups, heads, picks, step...  18.9 us
    all_to_all x1, blocking collectives, local(): lax.all_to_all(asked, 'ctx', split_axis=0, concat_axis=0, tiled=True)  13 us
    unnamed x71, local copies, waits for them, and re-layouts  12.4 us
    ppermute x12, waiting for transfers between devices, along(): return lax.ppermute(value, 'ctx', pairs)  10.3 us
  transfers between devices with their start and end apart: 46, of which 22 were waited for; matrix products, arithmetic and copies ran while one was open for 4% of the time, Pallas kernels for 14%

profile of v3, /device:TPU:8, one launch (start us, length us, event | category | flops | bytes accessed | tf_op | source)
XLA Modules:
  0.0 275.6 jit_solution(9369401802537949925)
XLA Ops:
  2.2 13.0 %all_to_all.14 = s32[16,1,8]{2,1,0:T(1,128)S(1)} all-to-all(s32[16,1,8]{2,1,0:T(1,128)S(1)} %bitcast.29), channel_id=1, replica_groups=mesh['ctx'=16,'head'=2] {'ctx'}, dimensions={0} | all-to-all | bytes 1024 | tf_op jit(solution)/shard_map/all_to_all | solution.py:462
  17.0 4.2 %gather_blocks.1 = bf16[128,64,128]{2,1,0:T(8,128)(2,1)} custom-call(s32[128]{0:T(128)} %reshape.35.asked_ref, bf16[1024,2048]{1,0:T(8,128)(2,1)} %source_ref.2), custom_call_target="tpu_custom_call" | custom-call | flops 67108864 | bytes 4194304 | tf_op jit(solution)/shard_map/gather_blocks/pallas_call | solution.py:72
  21.2 5.2 %all-to-all-start.1 = ((bf16[16,8,64,128]{3,2,1,0:T(8,128)(2,1)}), bf16[16,8,64,128]{3,2,1,0:T(8,128)(2,1)S(1)}, u32[]{:S(2)}, u32[]{:S(2)}) async-start(bf16[16,8,64,128]{3,2,1,0:T(8,128)(2,1)} %bitcast.24), calls=%async_computation.1 | async-start | bytes 4194304 | tf_op jit(solution)/shard_map/all_to_all | solution.py:490
  26.4 1.5 collective-permute-start
  29.0 1.9 collective-permute-start.2
  30.9 2.0 collective-permute-start.20
  32.9 4.8 %collective-permute-start.21 = (bf16[2048,256]{1,0:T(8,128)(2,1)}, bf16[2048,256]{1,0:T(8,128)(2,1)}, u32[]{:S(2)}, u32[]{:S(2)}) collective-permute-start(bf16[2048,256]{1,0:T(8,128)(2,1)} %refs_0_.1), channel_id=1, source_target_pairs={{8,0},{10,2},{12,4},{14,6},{16,8},{18,10},{20,12},{22,14},{24,16},... | collective-permute-start | bytes 3145736 | tf_op jit(solution)/shard_map/ppermute | solution.py:458
  39.1 3.9 %spread_blocks.1 = (bf16[8,64,128]{2,1,0:T(8,128)(2,1)}, bf16[8,64,128]{2,1,0:T(8,128)(2,1)}, bf16[8,64,128]{2,1,0:T(8,128)(2,1)}, bf16[8,64,128]{2,1,0:T(8,128)...) custom-call(s32[128]{0:T(128)} %reshape.35.asked_ref, ...), custom_call_target="tpu_custom_call" | custom-call | flops 67108864 | bytes 4194304 | tf_op jit(solution)/shard_map/spread_blocks/pallas_call | solution.py:108
  43.0 38.1 %collective-permute-done = bf16[1,2,16,2048]{3,2,1,0:T(8,128)(2,1)S(1)} collective-permute-done((bf16[1,2,16,2048]{3,2,1,0:T(8,128)(2,1)S(1)}, bf16[1,2,16,2048]{3,2,1,0:T(8,128)(2,1)S(1)}, u32[]{:S(2)}, u32[]{:S(2)}) %collective-permute-start) | collective-permute-done | bytes 131104 | tf_op jit(solution)/shard_map/ppermute | solution.py:484
  84.3 1.5 collective-permute-start.3
  87.3 1.8 collective-permute-start.7
  89.9 11.3 %collective-permute-done.7.refs_3_ = bf16[8,64,128]{2,1,0:T(8,128)(2,1)S(1)} collective-permute-done((bf16[8,64,128]{2,1,0:T(8,128)(2,1)}, bf16[8,64,128]{2,1,0:T(8,128)(2,1)S(1)}, u32[]{:S(2)}, u32[]{:S(2)}) %collective-permute-start.7) | collective-permute-done | bytes 131104 | tf_op jit(solution)/shard_map/ppermute | solution.py:448
  101.9 2.8 %collective-permute-start.10 = (bf16[8,64,128]{2,1,0:T(8,128)(2,1)S(1)}, bf16[8,64,128]{2,1,0:T(8,128)(2,1)S(1)}, u32[]{:S(2)}, u32[]{:S(2)}) collective-permute-start(bf16[8,64,128]{2,1,0:T(8,128)(2,1)S(1)} %copy-done.33), channel_id=1, source_target_pairs={{0,12},{2,14},{4,8},{6,10},{8,4},{10,6},{12,0},{14,2},{16,28},{18,... | collective-permute-start | bytes 393224 | tf_op jit(solution)/shard_map/ppermute | solution.py:448
  104.7 2.5 collective-permute-done.9.refs_5_
  110.5 2.5 collective-permute-start.13
  113.0 2.4 collective-permute-done.11.refs_7_
  115.4 2.0 collective-permute-start.14
  117.5 3.9 %collective-permute-done.12.refs_8_ = bf16[8,64,128]{2,1,0:T(8,128)(2,1)S(1)} collective-permute-done((bf16[8,64,128]{2,1,0:T(8,128)(2,1)S(1)}, bf16[8,64,128]{2,1,0:T(8,128)(2,1)S(1)}, u32[]{:S(2)}, u32[]{:S(2)}) %collective-permute-start.12) | collective-permute-done | bytes 131104 | tf_op jit(solution)/shard_map/ppermute | solution.py:448
  121.4 5.0 %collective-permute-start.15 = (bf16[8,64,128]{2,1,0:T(8,128)(2,1)S(1)}, bf16[8,64,128]{2,1,0:T(8,128)(2,1)S(1)}, u32[]{:S(2)}, u32[]{:S(2)}) collective-permute-start(bf16[8,64,128]{2,1,0:T(8,128)(2,1)S(1)} %copy-done.28), channel_id=1, source_target_pairs={{0,22},{2,20},{4,18},{6,16},{8,30},{10,28},{12,26},{14,24},{16,6},... | collective-permute-start | bytes 393224 | tf_op jit(solution)/shard_map/ppermute | solution.py:448
  126.7 2.1 fusion.9
  130.3 2.2 collective-permute-done.14.refs_10_
  133.2 2.2 collective-permute-done.15.refs_11_
  135.4 3.1 %collective-permute-start.18 = (bf16[8,64,128]{2,1,0:T(8,128)(2,1)S(1)}, bf16[8,64,128]{2,1,0:T(8,128)(2,1)S(1)}, u32[]{:S(2)}, u32[]{:S(2)}) collective-permute-start(bf16[8,64,128]{2,1,0:T(8,128)(2,1)S(1)} %copy-done.25), channel_id=1, source_target_pairs={{0,28},{2,30},{4,24},{6,26},{8,20},{10,22},{12,16},{14,18},{16,12}... | collective-permute-start | bytes 393224 | tf_op jit(solution)/shard_map/ppermute | solution.py:448
  138.8 2.2 fusion.8
  141.1 3.7 %collective-permute-done.16.refs_12_ = bf16[8,64,128]{2,1,0:T(8,128)(2,1)S(1)} collective-permute-done((bf16[8,64,128]{2,1,0:T(8,128)(2,1)S(1)}, bf16[8,64,128]{2,1,0:T(8,128)(2,1)S(1)}, u32[]{:S(2)}, u32[]{:S(2)}) %collective-permute-start.16) | collective-permute-done | bytes 131104 | tf_op jit(solution)/shard_map/ppermute | solution.py:448
  145.4 2.3 collective-permute-done.17.refs_13_
  148.4 3.8 %collective-permute-done.18.refs_14_ = bf16[8,64,128]{2,1,0:T(8,128)(2,1)S(1)} collective-permute-done((bf16[8,64,128]{2,1,0:T(8,128)(2,1)S(1)}, bf16[8,64,128]{2,1,0:T(8,128)(2,1)S(1)}, u32[]{:S(2)}, u32[]{:S(2)}) %collective-permute-start.18) | collective-permute-done | bytes 131104 | tf_op jit(solution)/shard_map/ppermute | solution.py:448
  154.4 4.2 %collective-permute-start.24 = (bf16[1024,256]{1,0:T(8,128)(2,1)S(1)}, bf16[1024,256]{1,0:T(8,128)(2,1)}, u32[]{:S(2)}, u32[]{:S(2)}) collective-permute-start(bf16[1024,256]{1,0:T(8,128)(2,1)S(1)} %get-tuple-element.57), channel_id=1, source_target_pairs={{8,16},{10,18},{12,20},{14,22},{9,17},{11,19},{13,21},{15,23}} | collective-permute-start | bytes 1572872 | tf_op jit(solution)/shard_map/ppermute | solution.py:458
  158.6 1.7 collective-permute-start.22
  160.3 2.3 collective-permute-start.23
  162.7 2.9 %collective-permute-start.25 = (bf16[1024,256]{1,0:T(8,128)(2,1)}, bf16[1024,256]{1,0:T(8,128)(2,1)}, u32[]{:S(2)}, u32[]{:S(2)}) collective-permute-start(bf16[1024,256]{1,0:T(8,128)(2,1)} %get-tuple-element.58), channel_id=1, source_target_pairs={{8,16},{10,18},{12,20},{14,22},{9,17},{11,19},{13,21},{15,23}} | collective-permute-start | bytes 1572872 | tf_op jit(solution)/shard_map/ppermute | solution.py:458
  165.5 4.2 %collective-permute-done.24.refs_5_ = bf16[1024,256]{1,0:T(8,128)(2,1)} collective-permute-done((bf16[1024,256]{1,0:T(8,128)(2,1)S(1)}, bf16[1024,256]{1,0:T(8,128)(2,1)}, u32[]{:S(2)}, u32[]{:S(2)}) %collective-permute-start.24) | collective-permute-done | bytes 524320 | tf_op jit(solution)/shard_map/ppermute | solution.py:458
  172.3 2.9 %fence.1.cell_ref = s32[256]{0:T(256)} custom-call(s32[256]{0:T(256)} %copy-done.23), custom_call_target="tpu_custom_call" | custom-call | tf_op jit(solution)/shard_map/fence/pallas_call | solution.py:132
  175.9 2.3 constant_dynamic-update-slice_fusion.5.land_ref
  179.7 2.0 collective-permute-done.26.refs_7_
  183.2 4.1 %collective-permute-done.27.refs_8_ = bf16[1024,256]{1,0:T(8,128)(2,1)} collective-permute-done((bf16[1024,256]{1,0:T(8,128)(2,1)}, bf16[1024,256]{1,0:T(8,128)(2,1)}, u32[]{:S(2)}, u32[]{:S(2)}) %collective-permute-start.27) | collective-permute-done | bytes 524320 | tf_op jit(solution)/shard_map/ppermute | solution.py:458
  187.4 2.1 collective-permute-start.30
  189.5 1.6 copy-done.10
  194.8 18.9 %attention_scores.1 = (bf16[256,4096]{1,0:T(8,128)(2,1)S(1)}, f32[256,2048]{1,0:T(8,128)S(1)}) custom-call(s32[256]{0:T(256)S(1)} %copy-done.12, bf16[256,2048]{1,0:T(8,128)(2,1)S(1)} %copy-done.13, bf16[16,2,16,2048]{3,2,1,0:T(8,128)(2,1)S(1)} %copy-done.10, bf16[256,2048]{1,0:T(8,128)(2,1)S(1)} %copy-done.14, bf16[256,2048]{1,0:T(8,128)(2,1)S(1)} %copy-done.15, ...), custom_call_target="tpu_custom_call" | custom-call | flops 4831838208 | bytes 8388608 | tf_op jit(solution)/shard_map/attention_scores/pallas_call | solution.py:240
  213.7 5.3 %attention_values.1 = (bf16[128,2048]{1,0:T(8,128)(2,1)S(1)}, bf16[128,2048]{1,0:T(8,128)(2,1)S(1)}) custom-call(s32[256]{0:T(256)S(1)} %fusion.7.cell_ref, bf16[256,4096]{1,0:T(8,128)(2,1)S(1)} %get-tuple-element.37.weight_ref, f32[256,2048]{1,0:T(8,128)S(1)} %get-tuple-element.38.acc_ref, bf16[8,64,128]{2,1,0:T(8,128)(2,1)S(1)} %copy-done.1, ...), custom_call_target="tpu_custom_call" | custom-call | flops 536870912 | bytes 6291456 | tf_op jit(solution)/shard_map/attention_values/pallas_call | solution.py:282
  219.0 6.1 %collective-permute-start.37 = (bf16[128,2048]{1,0:T(8,128)(2,1)S(1)}, bf16[128,2048]{1,0:T(8,128)(2,1)S(1)}, u32[]{:S(2)}, u32[]{:S(2)}) collective-permute-start(bf16[128,2048]{1,0:T(8,128)(2,1)S(1)} %get-tuple-element.55.refs_0_), channel_id=1, source_target_pairs={{0,4},{2,6},{4,0},{6,2},{8,12},{10,14},{12,8},{14,10},{16,20},{18,... | collective-permute-start | bytes 1572872 | tf_op jit(solution)/shard_map/ppermute | solution.py:448
  228.8 9.1 %collective-permute-done.37.refs_0_ = bf16[128,2048]{1,0:T(8,128)(2,1)S(1)} collective-permute-done((bf16[128,2048]{1,0:T(8,128)(2,1)S(1)}, bf16[128,2048]{1,0:T(8,128)(2,1)S(1)}, u32[]{:S(2)}, u32[]{:S(2)}) %collective-permute-start.37) | collective-permute-done | bytes 524320 | tf_op jit(solution)/shard_map/ppermute | solution.py:448
  242.1 2.7 pick.1.refs_2_
  244.8 4.6 %collective-permute-done.33.refs_0_ = bf16[128,2048]{1,0:T(8,128)(2,1)S(1)} collective-permute-done((bf16[128,2048]{1,0:T(8,128)(2,1)S(1)}, bf16[128,2048]{1,0:T(8,128)(2,1)S(1)}, u32[]{:S(2)}, u32[]{:S(2)}) %collective-permute-start.33) | collective-permute-done | bytes 524320 | tf_op jit(solution)/shard_map/ppermute | solution.py:448
  256.6 1.7 collective-permute-start.36
  260.5 5.4 %collective-permute-done.36.refs_1_ = bf16[256,512]{1,0:T(8,128)(2,1)S(1)} collective-permute-done((bf16[256,512]{1,0:T(8,128)(2,1)S(1)}, bf16[256,512]{1,0:T(8,128)(2,1)S(1)}, u32[]{:S(2)}, u32[]{:S(2)}) %collective-permute-start.36) | collective-permute-done | bytes 262176 | tf_op jit(solution)/shard_map/ppermute | solution.py:448
  265.8 6.5 %collective-permute-done.40.refs_2_ = bf16[256,512]{1,0:T(8,128)(2,1)S(1)} collective-permute-done((bf16[256,512]{1,0:T(8,128)(2,1)S(1)}, bf16[256,512]{1,0:T(8,128)(2,1)S(1)}, u32[]{:S(2)}, u32[]{:S(2)}) %collective-permute-start.40) | collective-permute-done | bytes 262176 | tf_op jit(solution)/shard_map/ppermute | solution.py:448
  273.2 2.5 assemble.1
  (156 shorter events, 50.2 us)
Async XLA Ops:
  21.2 168.3 %all-to-all-start.1 = ((bf16[16,8,64,128]{3,2,1,0:T(8,128)(2,1)}), bf16[16,8,64,128]{3,2,1,0:T(8,128)(2,1)S(1)}, u32[]{:S(2)}, u32[]{:S(2)}) async-start(bf16[16,8,64,128]{3,2,1,0:T(8,128)(2,1)} %bitcast.24), calls=%async_computation.1 | async-start | bytes 4194304 | tf_op jit(solution)/shard_map/all_to_all | solution.py:490
  26.4 54.7 %collective-permute-start = (bf16[1,2,16,2048]{3,2,1,0:T(8,128)(2,1)S(1)}, bf16[1,2,16,2048]{3,2,1,0:T(8,128)(2,1)S(1)}, u32[]{:S(2)}, u32[]{:S(2)}) collective-permute-start(bf16[1,2,16,2048]{3,2,1,0:T(8,128)(2,1)S(1)} %maximum_bitcast_fusion), channel_id=1, source_target_pairs={{0,8},{2,10},{4,12},{6,14},{8,16},{10,18},{12,20},{14,22},{16,24},... | collective-permute-start | bytes 393224 | tf_op jit(solution)/shard_map/ppermute | solution.py:484
  27.9 56.0 %collective-permute-start.1 = (bf16[1,2,16,2048]{3,2,1,0:T(8,128)(2,1)S(1)}, bf16[1,2,16,2048]{3,2,1,0:T(8,128)(2,1)S(1)}, u32[]{:S(2)}, u32[]{:S(2)}) collective-permute-start(bf16[1,2,16,2048]{3,2,1,0:T(8,128)(2,1)S(1)} %maximum_bitcast_fusion), channel_id=1, source_target_pairs={{0,16},{2,18},{4,20},{6,22},{8,24},{10,26},{12,28},{14,30},{16,0},... | collective-permute-start | bytes 393224 | tf_op jit(solution)/shard_map/ppermute | solution.py:484
  29.0 55.3 %collective-permute-start.2 = (bf16[1,2,16,2048]{3,2,1,0:T(8,128)(2,1)S(1)}, bf16[1,2,16,2048]{3,2,1,0:T(8,128)(2,1)S(1)}, u32[]{:S(2)}, u32[]{:S(2)}) collective-permute-start(bf16[1,2,16,2048]{3,2,1,0:T(8,128)(2,1)S(1)} %maximum_bitcast_fusion), channel_id=1, source_target_pairs={{0,24},{2,26},{4,28},{6,30},{8,0},{10,2},{12,4},{14,6},{16,8},{18,... | collective-permute-start | bytes 393224 | tf_op jit(solution)/shard_map/ppermute | solution.py:484
  30.9 95.5 %collective-permute-start.20 = (bf16[2048,256]{1,0:T(8,128)(2,1)}, bf16[2048,256]{1,0:T(8,128)(2,1)}, u32[]{:S(2)}, u32[]{:S(2)}) collective-permute-start(bf16[2048,256]{1,0:T(8,128)(2,1)} %refs_0_.1), channel_id=1, source_target_pairs={{0,8},{2,10},{4,12},{6,14},{8,16},{10,18},{12,20},{14,22},{16,24},... | collective-permute-start | bytes 3145736 | tf_op jit(solution)/shard_map/ppermute | solution.py:458
  32.9 105.6 %collective-permute-start.21 = (bf16[2048,256]{1,0:T(8,128)(2,1)}, bf16[2048,256]{1,0:T(8,128)(2,1)}, u32[]{:S(2)}, u32[]{:S(2)}) collective-permute-start(bf16[2048,256]{1,0:T(8,128)(2,1)} %refs_0_.1), channel_id=1, source_target_pairs={{8,0},{10,2},{12,4},{14,6},{16,8},{18,10},{20,12},{22,14},{24,16},... | collective-permute-start | bytes 3145736 | tf_op jit(solution)/shard_map/ppermute | solution.py:458
  43.0 72.4 %copy-start.29 = (bf16[8,64,128]{2,1,0:T(8,128)(2,1)S(1)}, bf16[8,64,128]{2,1,0:T(8,128)(2,1)}, u32[]{:S(2)}) copy-start(bf16[8,64,128]{2,1,0:T(8,128)(2,1)} %get-tuple-element.49) | copy-start | bytes 393220
  43.0 78.4 %copy-start.28 = (bf16[8,64,128]{2,1,0:T(8,128)(2,1)S(1)}, bf16[8,64,128]{2,1,0:T(8,128)(2,1)}, u32[]{:S(2)}) copy-start(bf16[8,64,128]{2,1,0:T(8,128)(2,1)} %get-tuple-element.50) | copy-start | bytes 393220
  81.1 6.2 %collective-permute-start.5 = (bf16[8,64,128]{2,1,0:T(8,128)(2,1)}, bf16[8,64,128]{2,1,0:T(8,128)(2,1)S(1)}, u32[]{:S(2)}, u32[]{:S(2)}) collective-permute-start(bf16[8,64,128]{2,1,0:T(8,128)(2,1)} %get-tuple-element.40), channel_id=1, source_target_pairs={{0,2},{2,0},{4,6},{6,4},{8,10},{10,8},{12,14},{14,12},{16,18},{18,... | collective-permute-start | bytes 393224 | tf_op jit(solution)/shard_map/ppermute | solution.py:448
  83.9 6.0 %collective-permute-start.6 = (bf16[8,64,128]{2,1,0:T(8,128)(2,1)}, bf16[8,64,128]{2,1,0:T(8,128)(2,1)S(1)}, u32[]{:S(2)}, u32[]{:S(2)}) collective-permute-start(bf16[8,64,128]{2,1,0:T(8,128)(2,1)} %get-tuple-element.41), channel_id=1, source_target_pairs={{0,4},{2,6},{4,0},{6,2},{8,12},{10,14},{12,8},{14,10},{16,20},{18,... | collective-permute-start | bytes 393224 | tf_op jit(solution)/shard_map/ppermute | solution.py:448
  84.3 24.4 %collective-permute-start.3 = (bf16[4,2,16,2048]{3,2,1,0:T(8,128)(2,1)S(1)}, bf16[4,2,16,2048]{3,2,1,0:T(8,128)(2,1)S(1)}, u32[]{:S(2)}, u32[]{:S(2)}) collective-permute-start(bf16[4,2,16,2048]{3,2,1,0:T(8,128)(2,1)S(1)} %pad_maximum_fusion), channel_id=1, source_target_pairs={{0,2},{2,0},{4,6},{6,4},{8,10},{10,8},{12,14},{14,12},{16,18},{18,... | collective-permute-start | bytes 1572872 | tf_op jit(solution)/shard_map/ppermute | solution.py:448
  87.3 13.9 %collective-permute-start.7 = (bf16[8,64,128]{2,1,0:T(8,128)(2,1)}, bf16[8,64,128]{2,1,0:T(8,128)(2,1)S(1)}, u32[]{:S(2)}, u32[]{:S(2)}) collective-permute-start(bf16[8,64,128]{2,1,0:T(8,128)(2,1)} %get-tuple-element.42), channel_id=1, source_target_pairs={{0,6},{2,4},{4,2},{6,0},{8,14},{10,12},{12,10},{14,8},{16,22},{18,... | collective-permute-start | bytes 393224 | tf_op jit(solution)/shard_map/ppermute | solution.py:448
  89.8 12.1 %collective-permute-start.8 = (bf16[8,64,128]{2,1,0:T(8,128)(2,1)}, bf16[8,64,128]{2,1,0:T(8,128)(2,1)S(1)}, u32[]{:S(2)}, u32[]{:S(2)}) collective-permute-start(bf16[8,64,128]{2,1,0:T(8,128)(2,1)} %get-tuple-element.43), channel_id=1, source_target_pairs={{0,8},{2,10},{4,12},{6,14},{8,0},{10,2},{12,4},{14,6},{16,24},{18,... | collective-permute-start | bytes 393224 | tf_op jit(solution)/shard_map/ppermute | solution.py:448
  101.2 6.1 %collective-permute-start.9 = (bf16[8,64,128]{2,1,0:T(8,128)(2,1)}, bf16[8,64,128]{2,1,0:T(8,128)(2,1)S(1)}, u32[]{:S(2)}, u32[]{:S(2)}) collective-permute-start(bf16[8,64,128]{2,1,0:T(8,128)(2,1)} %get-tuple-element.44), channel_id=1, source_target_pairs={{0,10},{2,8},{4,14},{6,12},{8,2},{10,0},{12,6},{14,4},{16,26},{18,... | collective-permute-start | bytes 393224 | tf_op jit(solution)/shard_map/ppermute | solution.py:448
  101.9 8.6 %collective-permute-start.10 = (bf16[8,64,128]{2,1,0:T(8,128)(2,1)S(1)}, bf16[8,64,128]{2,1,0:T(8,128)(2,1)S(1)}, u32[]{:S(2)}, u32[]{:S(2)}) collective-permute-start(bf16[8,64,128]{2,1,0:T(8,128)(2,1)S(1)} %copy-done.33), channel_id=1, source_target_pairs={{0,12},{2,14},{4,8},{6,10},{8,4},{10,6},{12,0},{14,2},{16,28},{18,... | collective-permute-start | bytes 393224 | tf_op jit(solution)/shard_map/ppermute | solution.py:448
  107.3 8.1 %collective-permute-start.11 = (bf16[8,64,128]{2,1,0:T(8,128)(2,1)S(1)}, bf16[8,64,128]{2,1,0:T(8,128)(2,1)S(1)}, u32[]{:S(2)}, u32[]{:S(2)}) collective-permute-start(bf16[8,64,128]{2,1,0:T(8,128)(2,1)S(1)} %copy-done.32), channel_id=1, source_target_pairs={{0,14},{2,12},{4,10},{6,8},{8,6},{10,4},{12,2},{14,0},{16,30},{18,... | collective-permute-start | bytes 393224 | tf_op jit(solution)/shard_map/ppermute | solution.py:448
  108.8 12.6 %collective-permute-start.12 = (bf16[8,64,128]{2,1,0:T(8,128)(2,1)S(1)}, bf16[8,64,128]{2,1,0:T(8,128)(2,1)S(1)}, u32[]{:S(2)}, u32[]{:S(2)}) collective-permute-start(bf16[8,64,128]{2,1,0:T(8,128)(2,1)S(1)} %copy-done.31), channel_id=1, source_target_pairs={{0,16},{2,18},{4,20},{6,22},{8,24},{10,26},{12,28},{14,30},{16,0},... | collective-permute-start | bytes 393224 | tf_op jit(solution)/shard_map/ppermute | solution.py:448
  110.5 18.3 %collective-permute-start.13 = (bf16[8,64,128]{2,1,0:T(8,128)(2,1)S(1)}, bf16[8,64,128]{2,1,0:T(8,128)(2,1)S(1)}, u32[]{:S(2)}, u32[]{:S(2)}) collective-permute-start(bf16[8,64,128]{2,1,0:T(8,128)(2,1)S(1)} %copy-done.30), channel_id=1, source_target_pairs={{0,18},{2,16},{4,22},{6,20},{8,26},{10,24},{12,30},{14,28},{16,2},... | collective-permute-start | bytes 393224 | tf_op jit(solution)/shard_map/ppermute | solution.py:448
  115.4 17.1 %collective-permute-start.14 = (bf16[8,64,128]{2,1,0:T(8,128)(2,1)S(1)}, bf16[8,64,128]{2,1,0:T(8,128)(2,1)S(1)}, u32[]{:S(2)}, u32[]{:S(2)}) collective-permute-start(bf16[8,64,128]{2,1,0:T(8,128)(2,1)S(1)} %copy-done.29), channel_id=1, source_target_pairs={{0,20},{2,22},{4,16},{6,18},{8,28},{10,30},{12,24},{14,26},{16,4},... | collective-permute-start | bytes 393224 | tf_op jit(solution)/shard_map/ppermute | solution.py:448
  121.4 14.0 %collective-permute-start.15 = (bf16[8,64,128]{2,1,0:T(8,128)(2,1)S(1)}, bf16[8,64,128]{2,1,0:T(8,128)(2,1)S(1)}, u32[]{:S(2)}, u32[]{:S(2)}) collective-permute-start(bf16[8,64,128]{2,1,0:T(8,128)(2,1)S(1)} %copy-done.28), channel_id=1, source_target_pairs={{0,22},{2,20},{4,18},{6,16},{8,30},{10,28},{12,26},{14,24},{16,6},... | collective-permute-start | bytes 393224 | tf_op jit(solution)/shard_map/ppermute | solution.py:448
  126.4 44.6 %collective-permute-start.4 = (bf16[8,2,16,2048]{3,2,1,0:T(8,128)(2,1)}, bf16[8,2,16,2048]{3,2,1,0:T(8,128)(2,1)}, u32[]{:S(2)}, u32[]{:S(2)}) collective-permute-start(bf16[8,2,16,2048]{3,2,1,0:T(8,128)(2,1)} %get-tuple-element.73), channel_id=1, source_target_pairs={{0,4},{2,6},{4,0},{6,2},{8,12},{10,14},{12,8},{14,10},{16,20},{18,... | collective-permute-start | bytes 3145736 | tf_op jit(solution)/shard_map/ppermute | solution.py:448
  128.8 15.9 %collective-permute-start.16 = (bf16[8,64,128]{2,1,0:T(8,128)(2,1)S(1)}, bf16[8,64,128]{2,1,0:T(8,128)(2,1)S(1)}, u32[]{:S(2)}, u32[]{:S(2)}) collective-permute-start(bf16[8,64,128]{2,1,0:T(8,128)(2,1)S(1)} %copy-done.27), channel_id=1, source_target_pairs={{0,24},{2,26},{4,28},{6,30},{8,16},{10,18},{12,20},{14,22},{16,8},... | collective-permute-start | bytes 393224 | tf_op jit(solution)/shard_map/ppermute | solution.py:448
  132.6 15.1 %collective-permute-start.17 = (bf16[8,64,128]{2,1,0:T(8,128)(2,1)S(1)}, bf16[8,64,128]{2,1,0:T(8,128)(2,1)S(1)}, u32[]{:S(2)}, u32[]{:S(2)}) collective-permute-start(bf16[8,64,128]{2,1,0:T(8,128)(2,1)S(1)} %copy-done.26), channel_id=1, source_target_pairs={{0,26},{2,24},{4,30},{6,28},{8,18},{10,16},{12,22},{14,20},{16,10}... | collective-permute-start | bytes 393224 | tf_op jit(solution)/shard_map/ppermute | solution.py:448
  135.4 16.7 %collective-permute-start.18 = (bf16[8,64,128]{2,1,0:T(8,128)(2,1)S(1)}, bf16[8,64,128]{2,1,0:T(8,128)(2,1)S(1)}, u32[]{:S(2)}, u32[]{:S(2)}) collective-permute-start(bf16[8,64,128]{2,1,0:T(8,128)(2,1)S(1)} %copy-done.25), channel_id=1, source_target_pairs={{0,28},{2,30},{4,24},{6,26},{8,20},{10,22},{12,16},{14,18},{16,12}... | collective-permute-start | bytes 393224 | tf_op jit(solution)/shard_map/ppermute | solution.py:448
  138.5 15.2 %collective-permute-start.19 = (bf16[8,64,128]{2,1,0:T(8,128)(2,1)S(1)}, bf16[8,64,128]{2,1,0:T(8,128)(2,1)S(1)}, u32[]{:S(2)}, u32[]{:S(2)}) collective-permute-start(bf16[8,64,128]{2,1,0:T(8,128)(2,1)S(1)} %copy-done.24), channel_id=1, source_target_pairs={{0,30},{2,28},{4,26},{6,24},{8,22},{10,20},{12,18},{14,16},{16,14}... | collective-permute-start | bytes 393224 | tf_op jit(solution)/shard_map/ppermute | solution.py:448
  154.4 15.3 %collective-permute-start.24 = (bf16[1024,256]{1,0:T(8,128)(2,1)S(1)}, bf16[1024,256]{1,0:T(8,128)(2,1)}, u32[]{:S(2)}, u32[]{:S(2)}) collective-permute-start(bf16[1024,256]{1,0:T(8,128)(2,1)S(1)} %get-tuple-element.57), channel_id=1, source_target_pairs={{8,16},{10,18},{12,20},{14,22},{9,17},{11,19},{13,21},{15,23}} | collective-permute-start | bytes 1572872 | tf_op jit(solution)/shard_map/ppermute | solution.py:458
  158.6 60.4 %collective-permute-start.22 = (bf16[2048,256]{1,0:T(8,128)(2,1)}, bf16[2048,256]{1,0:T(8,128)(2,1)}, u32[]{:S(2)}, u32[]{:S(2)}) collective-permute-start(bf16[2048,256]{1,0:T(8,128)(2,1)} %collective-permute-done.20.refs_1_), channel_id=1, source_target_pairs={{16,24},{18,26},{20,28},{22,30},{17,25},{19,27},{21,29},{23,31}} | collective-permute-start | bytes 3145736 | tf_op jit(solution)/shard_map/ppermute | solution.py:458
  160.3 64.8 %collective-permute-start.23 = (bf16[2048,256]{1,0:T(8,128)(2,1)}, bf16[2048,256]{1,0:T(8,128)(2,1)}, u32[]{:S(2)}, u32[]{:S(2)}) collective-permute-start(bf16[2048,256]{1,0:T(8,128)(2,1)} %collective-permute-done.21.refs_2_), channel_id=1, source_target_pairs={{8,0},{10,2},{12,4},{14,6},{9,1},{11,3},{13,5},{15,7}} | collective-permute-start | bytes 3145736 | tf_op jit(solution)/shard_map/ppermute | solution.py:458
  162.7 15.6 %collective-permute-start.25 = (bf16[1024,256]{1,0:T(8,128)(2,1)}, bf16[1024,256]{1,0:T(8,128)(2,1)}, u32[]{:S(2)}, u32[]{:S(2)}) collective-permute-start(bf16[1024,256]{1,0:T(8,128)(2,1)} %get-tuple-element.58), channel_id=1, source_target_pairs={{8,16},{10,18},{12,20},{14,22},{9,17},{11,19},{13,21},{15,23}} | collective-permute-start | bytes 1572872 | tf_op jit(solution)/shard_map/ppermute | solution.py:458
  169.7 12.1 %collective-permute-start.26 = (bf16[1024,256]{1,0:T(8,128)(2,1)}, bf16[1024,256]{1,0:T(8,128)(2,1)}, u32[]{:S(2)}, u32[]{:S(2)}) collective-permute-start(bf16[1024,256]{1,0:T(8,128)(2,1)} %get-tuple-element.59), channel_id=1, source_target_pairs={{16,8},{18,10},{20,12},{22,14},{17,9},{19,11},{21,13},{23,15}} | collective-permute-start | bytes 1572872 | tf_op jit(solution)/shard_map/ppermute | solution.py:458
  171.0 16.4 %collective-permute-start.27 = (bf16[1024,256]{1,0:T(8,128)(2,1)}, bf16[1024,256]{1,0:T(8,128)(2,1)}, u32[]{:S(2)}, u32[]{:S(2)}) collective-permute-start(bf16[1024,256]{1,0:T(8,128)(2,1)} %get-tuple-element.60), channel_id=1, source_target_pairs={{16,8},{18,10},{20,12},{22,14},{17,9},{19,11},{21,13},{23,15}} | collective-permute-start | bytes 1572872 | tf_op jit(solution)/shard_map/ppermute | solution.py:458
  178.2 48.2 %collective-permute-start.28 = (bf16[1024,256]{1,0:T(8,128)(2,1)}, bf16[1024,256]{1,0:T(8,128)(2,1)}, u32[]{:S(2)}, u32[]{:S(2)}) collective-permute-start(bf16[1024,256]{1,0:T(8,128)(2,1)} %collective-permute-done.24.refs_5_), channel_id=1, source_target_pairs={{16,24},{18,26},{20,28},{22,30},{17,25},{19,27},{21,29},{23,31}} | collective-permute-start | bytes 1572872 | tf_op jit(solution)/shard_map/ppermute | solution.py:458
  181.7 46.2 %collective-permute-start.29 = (bf16[1024,256]{1,0:T(8,128)(2,1)}, bf16[1024,256]{1,0:T(8,128)(2,1)}, u32[]{:S(2)}, u32[]{:S(2)}) collective-permute-start(bf16[1024,256]{1,0:T(8,128)(2,1)} %collective-permute-done.25.refs_6_), channel_id=1, source_target_pairs={{16,24},{18,26},{20,28},{22,30},{17,25},{19,27},{21,29},{23,31}} | collective-permute-start | bytes 1572872 | tf_op jit(solution)/shard_map/ppermute | solution.py:458
  187.4 41.3 %collective-permute-start.30 = (bf16[1024,256]{1,0:T(8,128)(2,1)}, bf16[1024,256]{1,0:T(8,128)(2,1)}, u32[]{:S(2)}, u32[]{:S(2)}) collective-permute-start(bf16[1024,256]{1,0:T(8,128)(2,1)} %collective-permute-done.26.refs_7_), channel_id=1, source_target_pairs={{8,0},{10,2},{12,4},{14,6},{9,1},{11,3},{13,5},{15,7}} | collective-permute-start | bytes 1572872 | tf_op jit(solution)/shard_map/ppermute | solution.py:458
  219.0 18.8 %collective-permute-start.37 = (bf16[128,2048]{1,0:T(8,128)(2,1)S(1)}, bf16[128,2048]{1,0:T(8,128)(2,1)S(1)}, u32[]{:S(2)}, u32[]{:S(2)}) collective-permute-start(bf16[128,2048]{1,0:T(8,128)(2,1)S(1)} %get-tuple-element.55.refs_0_), channel_id=1, source_target_pairs={{0,4},{2,6},{4,0},{6,2},{8,12},{10,14},{12,8},{14,10},{16,20},{18,... | collective-permute-start | bytes 1572872 | tf_op jit(solution)/shard_map/ppermute | solution.py:448
  225.1 14.8 %collective-permute-start.34 = (bf16[128,2048]{1,0:T(8,128)(2,1)S(1)}, bf16[128,2048]{1,0:T(8,128)(2,1)S(1)}, u32[]{:S(2)}, u32[]{:S(2)}) collective-permute-start(bf16[128,2048]{1,0:T(8,128)(2,1)S(1)} %get-tuple-element.56.refs_1_), channel_id=1, source_target_pairs={{0,2},{2,0},{4,6},{6,4},{8,10},{10,8},{12,14},{14,12},{16,18},{18,... | collective-permute-start | bytes 1572872 | tf_op jit(solution)/shard_map/ppermute | solution.py:448
  226.5 14.8 %collective-permute-start.31 = (bf16[1024,256]{1,0:T(8,128)(2,1)}, bf16[1024,256]{1,0:T(8,128)(2,1)S(1)}, u32[]{:S(2)}, u32[]{:S(2)}) collective-permute-start(bf16[1024,256]{1,0:T(8,128)(2,1)} %collective-permute-done.27.refs_8_), channel_id=1, source_target_pairs={{8,0},{10,2},{12,4},{14,6},{9,1},{11,3},{13,5},{15,7}} | collective-permute-start | bytes 1572872 | tf_op jit(solution)/shard_map/ppermute | solution.py:458
  228.0 21.4 %collective-permute-start.33 = (bf16[128,2048]{1,0:T(8,128)(2,1)S(1)}, bf16[128,2048]{1,0:T(8,128)(2,1)S(1)}, u32[]{:S(2)}, u32[]{:S(2)}) collective-permute-start(bf16[128,2048]{1,0:T(8,128)(2,1)S(1)} %get-tuple-element.55.refs_0_), channel_id=1, source_target_pairs={{0,2},{2,0},{4,6},{6,4},{8,10},{10,8},{12,14},{14,12},{16,18},{18,... | collective-permute-start | bytes 1572872 | tf_op jit(solution)/shard_map/ppermute | solution.py:448
  228.7 24.7 %collective-permute-start.38 = (bf16[128,2048]{1,0:T(8,128)(2,1)S(1)}, bf16[128,2048]{1,0:T(8,128)(2,1)S(1)}, u32[]{:S(2)}, u32[]{:S(2)}) collective-permute-start(bf16[128,2048]{1,0:T(8,128)(2,1)S(1)} %get-tuple-element.56.refs_1_), channel_id=1, source_target_pairs={{0,4},{2,6},{4,0},{6,2},{8,12},{10,14},{12,8},{14,10},{16,20},{18,... | collective-permute-start | bytes 1572872 | tf_op jit(solution)/shard_map/ppermute | solution.py:448
  237.8 17.2 %collective-permute-start.41 = (bf16[128,2048]{1,0:T(8,128)(2,1)S(1)}, bf16[128,2048]{1,0:T(8,128)(2,1)S(1)}, u32[]{:S(2)}, u32[]{:S(2)}) collective-permute-start(bf16[128,2048]{1,0:T(8,128)(2,1)S(1)} %collective-permute-done.37.refs_0_), channel_id=1, source_target_pairs={{0,2},{2,0},{4,6},{6,4},{8,10},{10,8},{12,14},{14,12},{16,18},{18,... | collective-permute-start | bytes 1572872 | tf_op jit(solution)/shard_map/ppermute | solution.py:448
  239.9 15.1 %collective-permute-start.42 = (bf16[128,2048]{1,0:T(8,128)(2,1)S(1)}, bf16[128,2048]{1,0:T(8,128)(2,1)S(1)}, u32[]{:S(2)}, u32[]{:S(2)}) collective-permute-start(bf16[128,2048]{1,0:T(8,128)(2,1)S(1)} %collective-permute-done.34.refs_1_), channel_id=1, source_target_pairs={{0,4},{2,6},{4,0},{6,2},{8,12},{10,14},{12,8},{14,10},{16,20},{18,... | collective-permute-start | bytes 1572872 | tf_op jit(solution)/shard_map/ppermute | solution.py:448
  250.7 5.9 %collective-permute-start.35 = (bf16[256,512]{1,0:T(8,128)(2,1)S(1)}, bf16[256,512]{1,0:T(8,128)(2,1)S(1)}, u32[]{:S(2)}, u32[]{:S(2)}) collective-permute-start(bf16[256,512]{1,0:T(8,128)(2,1)S(1)} %bitcast.21), channel_id=1, source_target_pairs={{0,1},{1,0},{2,3},{3,2},{4,5},{5,4},{6,7},{7,6},{8,9},{9,8},{10,11... | collective-permute-start | bytes 786440 | tf_op jit(solution)/shard_map/ppermute | solution.py:534
  252.8 7.6 %collective-permute-start.32 = (bf16[256,512]{1,0:T(8,128)(2,1)S(1)}, bf16[256,512]{1,0:T(8,128)(2,1)S(1)}, u32[]{:S(2)}, u32[]{:S(2)}) collective-permute-start(bf16[256,512]{1,0:T(8,128)(2,1)S(1)} %bitcast.20), channel_id=1, source_target_pairs={{0,1},{1,0},{2,3},{3,2},{4,5},{5,4},{6,7},{7,6},{8,9},{9,8},{10,11... | collective-permute-start | bytes 786440 | tf_op jit(solution)/shard_map/ppermute | solution.py:534
  254.6 3.7 %collective-permute-start.39 = (bf16[256,512]{1,0:T(8,128)(2,1)S(1)}, bf16[256,512]{1,0:T(8,128)(2,1)S(1)}, u32[]{:S(2)}, u32[]{:S(2)}) collective-permute-start(bf16[256,512]{1,0:T(8,128)(2,1)S(1)} %bitcast.22), channel_id=1, source_target_pairs={{0,1},{1,0},{2,3},{3,2},{4,5},{5,4},{6,7},{7,6},{8,9},{9,8},{10,11... | collective-permute-start | bytes 786440 | tf_op jit(solution)/shard_map/ppermute | solution.py:534
  256.3 2.6 collective-permute-start.43
  256.6 9.2 %collective-permute-start.36 = (bf16[256,512]{1,0:T(8,128)(2,1)S(1)}, bf16[256,512]{1,0:T(8,128)(2,1)S(1)}, u32[]{:S(2)}, u32[]{:S(2)}) collective-permute-start(bf16[256,512]{1,0:T(8,128)(2,1)S(1)} %add_convert_fusion.2), channel_id=1, source_target_pairs={{0,2},{2,0},{4,6},{6,4},{8,10},{10,8},{12,14},{14,12},{16,18},{18,... | collective-permute-start | bytes 786440 | tf_op jit(solution)/shard_map/ppermute | solution.py:448
  258.4 13.9 %collective-permute-start.40 = (bf16[256,512]{1,0:T(8,128)(2,1)S(1)}, bf16[256,512]{1,0:T(8,128)(2,1)S(1)}, u32[]{:S(2)}, u32[]{:S(2)}) collective-permute-start(bf16[256,512]{1,0:T(8,128)(2,1)S(1)} %add_convert_fusion.1), channel_id=1, source_target_pairs={{0,4},{2,6},{4,0},{6,2},{8,12},{10,14},{12,8},{14,10},{16,20},{18,... | collective-permute-start | bytes 786440 | tf_op jit(solution)/shard_map/ppermute | solution.py:448
  258.9 13.4 %collective-permute-start.44 = (bf16[256,512]{1,0:T(8,128)(2,1)S(1)}, bf16[256,512]{1,0:T(8,128)(2,1)S(1)}, u32[]{:S(2)}, u32[]{:S(2)}) collective-permute-start(bf16[256,512]{1,0:T(8,128)(2,1)S(1)} %add_convert_fusion), channel_id=1, source_target_pairs={{0,6},{2,4},{4,2},{6,0},{8,14},{10,12},{12,10},{14,8},{16,22},{18,... | collective-permute-start | bytes 786440 | tf_op jit(solution)/shard_map/ppermute | solution.py:448
  (32 other events, 629.2 us)

commit v4 on v3

--- a/solution.py
+++ b/solution.py
@@ -120,77 +120,71 @@
     )(asked, place, source)
 
 
-def fence_kernel(in_ref, out_ref):
-    def move(i, carry):
-        out_ref[i] = in_ref[i]
-        return carry
-
-    lax.fori_loop(0, in_ref.shape[0], move, 0)
-
-
-def fence(table):
-    return pl.pallas_call(
-        fence_kernel,
-        out_shape=jax.ShapeDtypeStruct(table.shape, table.dtype),
-        in_specs=[SMEM],
-        out_specs=SMEM,
-        name="fence",
-    )(table)
-
-
 def nt_dot(a, b):
     return lax.dot_general(a, b, (((1,), (1,)), ((), ())), preferred_element_type=jnp.float32)
 
 
+def near_kernel(groups, step_heads, q_ref, land_ref, lk_ref, lv_ref, acc_ref, stat_ref):
+    rows = q_ref.shape[0]
+    size = q_ref.shape[1] // step_heads
+    scaling = 1.0 / math.sqrt(size)
+    row = lax.broadcasted_iota(jnp.int32, (rows, BLOCK), 0)
+    column = lax.broadcasted_iota(jnp.int32, (rows, BLOCK), 1)
+    causal = lax.rem(row, BLOCK) >= column
+    spans = [slice(g * BLOCK, (g + 1) * BLOCK) for g in range(groups)]
+    pieces, _, land_rows, _ = land_ref.shape
+    for hh in range(step_heads):
+        cols = slice(hh * size, (hh + 1) * size)
+        land_k = land_ref[:, 0, :, cols].reshape(pieces * land_rows, size)
+        land_v = land_ref[:, 1, :, cols].reshape(pieces * land_rows, size)
+        s_land = nt_dot(q_ref[:, cols], land_k) * scaling
+        s_local = jnp.concatenate([nt_dot(q_ref[g, cols], lk_ref[g, cols]) for g in spans], axis=0)
+        s_local = jnp.where(causal, s_local * scaling, -jnp.inf)
+        top = jnp.maximum(
+            jnp.max(s_land, axis=1, keepdims=True), jnp.max(s_local, axis=1, keepdims=True)
+        )
+        w_land = jnp.exp(s_land - top)
+        w_local = jnp.exp(s_local - top)
+        stat_ref[hh, :, 0:1] = top
+        stat_ref[hh, :, 1:2] = jnp.sum(w_land, axis=1, keepdims=True) + jnp.sum(
+            w_local, axis=1, keepdims=True
+        )
+        w_local = w_local.astype(jnp.bfloat16)
+        acc_ref[:, cols] = jnp.dot(
+            w_land.astype(jnp.bfloat16), land_v, preferred_element_type=jnp.float32
+        ) + jnp.concatenate(
+            [
+                jnp.dot(w_local[g], lv_ref[g, cols], preferred_element_type=jnp.float32)
+                for g in spans
+            ],
+            axis=0,
+        )
+
+
 def score_kernel(
-    groups, heads, picks, step_heads, cell_ref, q_ref, land_ref, lk_ref, lv_ref, fk_ref,
-    weight_ref, acc_ref,
+    groups, heads, picks, step_heads, cell_ref, q_ref, fk_ref, near_ref, stat_ref, weight_ref,
+    acc_ref,
 ):
     size = q_ref.shape[1] // step_heads
     scaling = 1.0 / math.sqrt(size)
     first_head = pl.program_id(0) * step_heads
-    row = lax.broadcasted_iota(jnp.int32, (BLOCK, BLOCK), 0)
-    column = lax.broadcasted_iota(jnp.int32, (BLOCK, BLOCK), 1)
-    causal = row >= column
-    pieces, _, land_rows, _ = land_ref.shape
     chosen = picks * BLOCK
     for hh in range(step_heads):
         cols = slice(hh * size, (hh + 1) * size)
-        land_k = land_ref[:, 0, :, cols].reshape(pieces * land_rows, size)
-        land_v = land_ref[:, 1, :, cols].reshape(pieces * land_rows, size)
+        scores = []
         for g in range(groups):
-            rows = slice(g * BLOCK, (g + 1) * BLOCK)
-            q = q_ref[rows, cols]
             base = (g * heads + first_head + hh) * picks
             keys = jnp.concatenate([fk_ref[cell_ref[base + p]] for p in range(picks)], axis=0)
-            s_land = nt_dot(q, land_k) * scaling
-            s_chosen = nt_dot(q, keys) * scaling
-            s_local = jnp.where(causal, nt_dot(q, lk_ref[rows, cols]) * scaling, -jnp.inf)
-            top = jnp.maximum(
-                jnp.maximum(
-                    jnp.max(s_land, axis=1, keepdims=True),
-                    jnp.max(s_chosen, axis=1, keepdims=True),
-                ),
-                jnp.max(s_local, axis=1, keepdims=True),
-            )
-            w_land = jnp.exp(s_land - top)
-            w_chosen = jnp.exp(s_chosen - top)
-            w_local = jnp.exp(s_local - top)
-            total = (
-                jnp.sum(w_land, axis=1, keepdims=True)
-                + jnp.sum(w_chosen, axis=1, keepdims=True)
-                + jnp.sum(w_local, axis=1, keepdims=True)
-            )
-            inverse = 1.0 / total
-            part = jnp.dot(
-                w_land.astype(jnp.bfloat16), land_v, preferred_element_type=jnp.float32
-            ) + jnp.dot(
-                w_local.astype(jnp.bfloat16), lv_ref[rows, cols], preferred_element_type=jnp.float32
-            )
-            acc_ref[rows, cols] = part * inverse
-            weight_ref[rows, hh * chosen : (hh + 1) * chosen] = (w_chosen * inverse).astype(
-                jnp.bfloat16
-            )
+            scores.append(nt_dot(q_ref[g * BLOCK : (g + 1) * BLOCK, cols], keys))
+        scores = jnp.concatenate(scores, axis=0) * scaling
+        near_top = stat_ref[hh, :, 0:1]
+        top = jnp.maximum(near_top, jnp.max(scores, axis=1, keepdims=True))
+        weights = jnp.exp(scores - top)
+        factor = jnp.exp(near_top - top)
+        total = stat_ref[hh, :, 1:2] * factor + jnp.sum(weights, axis=1, keepdims=True)
+        inverse = 1.0 / total
+        weight_ref[:, hh * chosen : (hh + 1) * chosen] = (weights * inverse).astype(jnp.bfloat16)
+        acc_ref[:, cols] = near_ref[:, cols] * (factor * inverse)
 
 
 def value_kernel(groups, heads, picks, step_heads, devices, cell_ref, weight_ref, acc_ref, *refs):
@@ -228,7 +222,46 @@
             ).astype(jnp.bfloat16)
 
 
-def attention_scores(cell, queries, land, span_keys, span_values, fetched_keys, dims):
+def in_hbm(value):
+    return pltpu.with_memory_space_constraint(value, pltpu.HBM)
+
+
+def attention_near(queries, land, span_keys, span_values, dims):
+    groups, heads, _ = dims
+    rows, width = queries.shape
+    size = width // heads
+    step = math.gcd(heads, 4)
+    wide = step * size
+    by_head = lambda i: (0, i)
+    keys = land.shape[0] * land.shape[2] + BLOCK
+    return pl.pallas_call(
+        functools.partial(near_kernel, groups, step),
+        grid=(heads // step,),
+        in_specs=[
+            pl.BlockSpec((rows, wide), by_head),
+            pl.BlockSpec(land.shape[:3] + (wide,), lambda i: (0, 0, 0, i)),
+            pl.BlockSpec((rows, wide), by_head),
+            pl.BlockSpec((rows, wide), by_head),
+        ],
+        out_specs=[
+            pl.BlockSpec((rows, wide), by_head),
+            pl.BlockSpec((step, rows, 2), lambda i: (i, 0, 0)),
+        ],
+        out_shape=[
+            jax.ShapeDtypeStruct((rows, width), jnp.float32),
+            jax.ShapeDtypeStruct((heads, rows, 2), jnp.float32),
+        ],
+        compiler_params=pltpu.CompilerParams(vmem_limit_bytes=LIMIT),
+        cost_estimate=pl.CostEstimate(
+            flops=16 * rows * keys * width,
+            bytes_accessed=16 * rows * width,
+            transcendentals=rows * keys * heads,
+        ),
+        name="attention_near",
+    )(in_hbm(queries), in_hbm(land), in_hbm(span_keys), in_hbm(span_values))
+
+
+def attention_scores(cell, queries, fetched_keys, near, stats, dims):
     groups, heads, picks = dims
     rows, width = queries.shape
     size = width // heads
@@ -236,7 +269,6 @@
     wide = step * size
     chosen = picks * BLOCK
     by_head = lambda i, c: (0, i)
-    keys = land.shape[0] * land.shape[2] + chosen + BLOCK
     return pl.pallas_call(
         functools.partial(score_kernel, groups, heads, picks, step),
         grid_spec=pltpu.PrefetchScalarGridSpec(
@@ -244,10 +276,9 @@
             grid=(heads // step,),
             in_specs=[
                 pl.BlockSpec((rows, wide), by_head),
-                pl.BlockSpec(land.shape[:3] + (wide,), lambda i, c: (0, 0, 0, i)),
+                pl.BlockSpec(fetched_keys.shape, lambda i, c: (0, 0, 0)),
                 pl.BlockSpec((rows, wide), by_head),
-                pl.BlockSpec((rows, wide), by_head),
-                pl.BlockSpec(fetched_keys.shape, lambda i, c: (0, 0, 0)),
+                pl.BlockSpec((step, rows, 2), lambda i, c: (i, 0, 0)),
             ],
             out_specs=[
                 pl.BlockSpec((rows, step * chosen), by_head),
@@ -255,17 +286,17 @@
             ],
         ),
         out_shape=[
-            jax.ShapeDtypeStruct((rows, heads * chosen), jnp.bfloat16),
-            jax.ShapeDtypeStruct((rows, width), jnp.float32),
+            pltpu.VMEM((rows, heads * chosen), jnp.bfloat16),
+            pltpu.VMEM((rows, width), jnp.float32),
         ],
         compiler_params=pltpu.CompilerParams(vmem_limit_bytes=LIMIT),
         cost_estimate=pl.CostEstimate(
-            flops=16 * rows * keys * width,
+            flops=8 * rows * chosen * width,
             bytes_accessed=16 * rows * width,
-            transcendentals=rows * keys * heads,
+            transcendentals=rows * chosen * heads,
         ),
         name="attention_scores",
-    )(cell, queries, land, span_keys, span_values, fetched_keys)
+    )(cell, in_hbm(queries), fetched_keys, in_hbm(near), in_hbm(stats))
 
 
 def attention_values(cell, weights, part, fetched_values, dims):
@@ -491,20 +522,14 @@
     fetched_keys = got.reshape(-1, BLOCK, size)
     sent = spread_blocks(asked_for, place, cache_values, heads, devices)
     fetched_values = [sent[0]] + [across(sent[m], m) for m in range(1, devices)]
-    cell = fence(cell)
     most = asked.shape[1]
     partner_cell = (cell // most ^ index) * most + cell % most
 
     dims = (groups, heads, picks)
-    weights, part = attention_scores(
-        cell, queries, land, span_keys, span_values, fetched_keys, dims
-    )
+    near, stats = attention_near(queries, land, span_keys, span_values, dims)
+    weights, part = attention_scores(cell, queries, fetched_keys, near, stats, dims)
     attended = attention_values(partner_cell, weights, part, fetched_values, dims)
 
-    if slow_count > 3:
-        low_parts, high_parts, _ = lax.optimization_barrier(
-            (low_parts, high_parts, fetched_values)
-        )
     for hop in range(2, slow_count):
         top = last - 1 if hop == 2 else last
         if hop > top:
@@ -528,7 +553,7 @@
 
     b_all = pick(place, blocks, slow_count, head_devices)
     tiles = {}
-    for mask in [*masks, 0]:
+    for mask in [*reversed(masks), 0]:
         mine, send = project(pieces[mask], b_all, share)
         received = [
             lax.ppermute(

time: 277 us -> 269 us (0.971)
  local copies, waits for them, and re-layouts: 22 us -> 15 us
  Pallas kernels: 45.4 us -> 42.3 us
  waiting for transfers between devices: 112 us -> 115 us
    pallas_call x1, Pallas kernels: 18.9 us -> 10.9 us  [attention_scores(): pl.pallas_call(functools.partial(score_kernel, groups, heads, picks, step...]
    pallas_call x1, Pallas kernels: 2.87 us -> 7.58 us  [attention_near(): pl.pallas_call(functools.partial(near_kernel, groups, step), grid=(heads...]
    unnamed x71 -> x69, local copies, waits for them, and re-layouts: 12.4 us -> 9.47 us
  transfers between devices with their start and end apart: 46 -> 46, of which waited for: 22 -> 18; matrix products, arithmetic and copies ran while one was open for 4% -> 3% of each run, Pallas kernels for 14% -> 13%
where the time goes in v4:
time: 269 us; the launch traced here: 268 us
  waiting for transfers between devices  115 us (43%)
  starting transfers between devices  78.9 us (29%)
  Pallas kernels  42.3 us (16%)
  local copies, waits for them, and re-layouts  15 us (6%)
  blocking collectives  13 us (5%)
  other arithmetic  3.7 us (1%)
    ppermute x26, waiting for transfers between devices, across(): return lax.ppermute(value, 'ctx', [(i, i ^ mask) for i in range(devices)])  63.7 us
    ppermute x26, starting transfers between devices, across(): return lax.ppermute(value, 'ctx', [(i, i ^ mask) for i in range(devices)])  40.9 us
    ppermute x3, waiting for transfers between devices, local(): land_parts.append(lax.ppermute(land, 'ctx', pairs))  39.5 us
    ppermute x12, starting transfers between devices, along(): return lax.ppermute(value, 'ctx', pairs)  27.3 us
    all_to_all x1, blocking collectives, local(): lax.all_to_all(asked, 'ctx', split_axis=0, concat_axis=0, tiled=True)  13 us
    ppermute x12, waiting for transfers between devices, along(): return lax.ppermute(value, 'ctx', pairs)  11.5 us
    pallas_call x1, Pallas kernels, attention_scores(): pl.pallas_call(functools.partial(score_kernel, groups, heads, picks, step...  10.9 us
    unnamed x69, local copies, waits for them, and re-layouts  9.47 us
  transfers between devices with their start and end apart: 46, of which 18 were waited for; matrix products, arithmetic and copies ran while one was open for 3% of the time, Pallas kernels for 13%

profile of v4, /device:TPU:8, one launch (start us, length us, event | category | flops | bytes accessed | tf_op | source)
XLA Modules:
  0.0 268.1 jit_solution(6014448468266888796)
XLA Ops:
  2.2 13.0 %all_to_all.14 = s32[16,1,8]{2,1,0:T(1,128)S(1)} all-to-all(s32[16,1,8]{2,1,0:T(1,128)S(1)} %bitcast.29), channel_id=1, replica_groups=mesh['ctx'=16,'head'=2] {'ctx'}, dimensions={0} | all-to-all | bytes 1024 | tf_op jit(solution)/shard_map/all_to_all | solution.py:493
  17.0 4.2 %gather_blocks.1 = bf16[128,64,128]{2,1,0:T(8,128)(2,1)} custom-call(s32[128]{0:T(128)} %reshape.35.asked_ref, bf16[1024,2048]{1,0:T(8,128)(2,1)} %source_ref.2), custom_call_target="tpu_custom_call" | custom-call | flops 67108864 | bytes 4194304 | tf_op jit(solution)/shard_map/gather_blocks/pallas_call | solution.py:72
  21.1 5.2 %all-to-all-start.1 = ((bf16[16,8,64,128]{3,2,1,0:T(8,128)(2,1)}), bf16[16,8,64,128]{3,2,1,0:T(8,128)(2,1)S(1)}, u32[]{:S(2)}, u32[]{:S(2)}) async-start(bf16[16,8,64,128]{3,2,1,0:T(8,128)(2,1)} %bitcast.24), calls=%async_computation.1 | async-start | bytes 4194304 | tf_op jit(solution)/shard_map/all_to_all | solution.py:521
  26.4 1.5 collective-permute-start
  29.0 1.9 collective-permute-start.2
  30.8 2.0 collective-permute-start.20
  32.9 4.8 %collective-permute-start.21 = (bf16[2048,256]{1,0:T(8,128)(2,1)}, bf16[2048,256]{1,0:T(8,128)(2,1)}, u32[]{:S(2)}, u32[]{:S(2)}) collective-permute-start(bf16[2048,256]{1,0:T(8,128)(2,1)} %refs_0_.1), channel_id=1, source_target_pairs={{8,0},{10,2},{12,4},{14,6},{16,8},{18,10},{20,12},{22,14},{24,16},... | collective-permute-start | bytes 3145736 | tf_op jit(solution)/shard_map/ppermute | solution.py:489
  39.0 3.9 %spread_blocks.1 = (bf16[8,64,128]{2,1,0:T(8,128)(2,1)}, bf16[8,64,128]{2,1,0:T(8,128)(2,1)}, bf16[8,64,128]{2,1,0:T(8,128)(2,1)}, bf16[8,64,128]{2,1,0:T(8,128)...) custom-call(s32[128]{0:T(128)} %reshape.35.asked_ref, ...), custom_call_target="tpu_custom_call" | custom-call | flops 67108864 | bytes 4194304 | tf_op jit(solution)/shard_map/spread_blocks/pallas_call | solution.py:108
  43.0 38.0 %collective-permute-done = bf16[1,2,16,2048]{3,2,1,0:T(8,128)(2,1)S(1)} collective-permute-done((bf16[1,2,16,2048]{3,2,1,0:T(8,128)(2,1)S(1)}, bf16[1,2,16,2048]{3,2,1,0:T(8,128)(2,1)S(1)}, u32[]{:S(2)}, u32[]{:S(2)}) %collective-permute-start) | collective-permute-done | bytes 131104 | tf_op jit(solution)/shard_map/ppermute | solution.py:515
  84.3 1.5 collective-permute-start.3
  87.3 1.8 collective-permute-start.7
  89.9 11.3 %collective-permute-done.7.refs_3_ = bf16[8,64,128]{2,1,0:T(8,128)(2,1)S(1)} collective-permute-done((bf16[8,64,128]{2,1,0:T(8,128)(2,1)}, bf16[8,64,128]{2,1,0:T(8,128)(2,1)S(1)}, u32[]{:S(2)}, u32[]{:S(2)}) %collective-permute-start.7) | collective-permute-done | bytes 131104 | tf_op jit(solution)/shard_map/ppermute | solution.py:479
  101.2 2.8 %collective-permute-start.10 = (bf16[8,64,128]{2,1,0:T(8,128)(2,1)}, bf16[8,64,128]{2,1,0:T(8,128)(2,1)S(1)}, u32[]{:S(2)}, u32[]{:S(2)}) collective-permute-start(bf16[8,64,128]{2,1,0:T(8,128)(2,1)} %get-tuple-element.45), channel_id=1, source_target_pairs={{0,12},{2,14},{4,8},{6,10},{8,4},{10,6},{12,0},{14,2},{16,28},{18,... | collective-permute-start | bytes 393224 | tf_op jit(solution)/shard_map/ppermute | solution.py:479
  104.7 2.5 collective-permute-done.9.refs_5_
  107.9 2.3 collective-permute-done.10.refs_6_
  110.2 2.4 collective-permute-start.12
  115.9 5.5 %collective-permute-done.12.refs_8_ = bf16[8,64,128]{2,1,0:T(8,128)(2,1)S(1)} collective-permute-done((bf16[8,64,128]{2,1,0:T(8,128)(2,1)S(1)}, bf16[8,64,128]{2,1,0:T(8,128)(2,1)S(1)}, u32[]{:S(2)}, u32[]{:S(2)}) %collective-permute-start.12) | collective-permute-done | bytes 131104 | tf_op jit(solution)/shard_map/ppermute | solution.py:479
  121.4 3.5 %collective-permute-start.14 = (bf16[8,64,128]{2,1,0:T(8,128)(2,1)S(1)}, bf16[8,64,128]{2,1,0:T(8,128)(2,1)S(1)}, u32[]{:S(2)}, u32[]{:S(2)}) collective-permute-start(bf16[8,64,128]{2,1,0:T(8,128)(2,1)S(1)} %copy-done.29), channel_id=1, source_target_pairs={{0,20},{2,22},{4,16},{6,18},{8,28},{10,30},{12,24},{14,26},{16,4},... | collective-permute-start | bytes 393224 | tf_op jit(solution)/shard_map/ppermute | solution.py:479
  124.9 2.1 collective-permute-done.13.refs_9_
  127.0 4.4 %collective-permute-start.15 = (bf16[8,64,128]{2,1,0:T(8,128)(2,1)S(1)}, bf16[8,64,128]{2,1,0:T(8,128)(2,1)S(1)}, u32[]{:S(2)}, u32[]{:S(2)}) collective-permute-start(bf16[8,64,128]{2,1,0:T(8,128)(2,1)S(1)} %copy-done.28), channel_id=1, source_target_pairs={{0,22},{2,20},{4,18},{6,16},{8,30},{10,28},{12,26},{14,24},{16,6},... | collective-permute-start | bytes 393224 | tf_op jit(solution)/shard_map/ppermute | solution.py:479
  133.5 3.9 %collective-permute-start.24 = (bf16[1024,256]{1,0:T(8,128)(2,1)S(1)}, bf16[1024,256]{1,0:T(8,128)(2,1)}, u32[]{:S(2)}, u32[]{:S(2)}) collective-permute-start(bf16[1024,256]{1,0:T(8,128)(2,1)S(1)} %get-tuple-element.70), channel_id=1, source_target_pairs={{8,16},{10,18},{12,20},{14,22},{9,17},{11,19},{13,21},{15,23}} | collective-permute-start | bytes 1572872 | tf_op jit(solution)/shard_map/ppermute | solution.py:489
  137.5 1.7 collective-permute-done.15.refs_11_
  139.2 1.5 collective-permute-start.17
  140.7 2.7 collective-permute-done.16.refs_12_
  143.4 2.9 %collective-permute-start.18 = (bf16[8,64,128]{2,1,0:T(8,128)(2,1)S(1)}, bf16[8,64,128]{2,1,0:T(8,128)(2,1)S(1)}, u32[]{:S(2)}, u32[]{:S(2)}) collective-permute-start(bf16[8,64,128]{2,1,0:T(8,128)(2,1)S(1)} %copy-done.25), channel_id=1, source_target_pairs={{0,28},{2,30},{4,24},{6,26},{8,20},{10,22},{12,16},{14,18},{16,12}... | collective-permute-start | bytes 393224 | tf_op jit(solution)/shard_map/ppermute | solution.py:479
  146.4 14.0 %collective-permute-done.17.refs_13_ = bf16[8,64,128]{2,1,0:T(8,128)(2,1)S(1)} collective-permute-done((bf16[8,64,128]{2,1,0:T(8,128)(2,1)S(1)}, bf16[8,64,128]{2,1,0:T(8,128)(2,1)S(1)}, u32[]{:S(2)}, u32[]{:S(2)}) %collective-permute-start.17) | collective-permute-done | bytes 131104 | tf_op jit(solution)/shard_map/ppermute | solution.py:479
  161.0 3.6 %collective-permute-start.19 = (bf16[8,64,128]{2,1,0:T(8,128)(2,1)S(1)}, bf16[8,64,128]{2,1,0:T(8,128)(2,1)S(1)}, u32[]{:S(2)}, u32[]{:S(2)}) collective-permute-start(bf16[8,64,128]{2,1,0:T(8,128)(2,1)S(1)} %copy-done.24), channel_id=1, source_target_pairs={{0,30},{2,28},{4,26},{6,24},{8,22},{10,20},{12,18},{14,16},{16,14}... | collective-permute-start | bytes 393224 | tf_op jit(solution)/shard_map/ppermute | solution.py:479
  165.3 1.6 collective-permute-start.22
  166.9 2.3 collective-permute-start.23
  170.5 3.5 %collective-permute-start.25 = (bf16[1024,256]{1,0:T(8,128)(2,1)S(1)}, bf16[1024,256]{1,0:T(8,128)(2,1)}, u32[]{:S(2)}, u32[]{:S(2)}) collective-permute-start(bf16[1024,256]{1,0:T(8,128)(2,1)S(1)} %get-tuple-element.69), channel_id=1, source_target_pairs={{8,16},{10,18},{12,20},{14,22},{9,17},{11,19},{13,21},{15,23}} | collective-permute-start | bytes 1572872 | tf_op jit(solution)/shard_map/ppermute | solution.py:489
  176.7 3.2 %collective-permute-done.25.refs_6_ = bf16[1024,256]{1,0:T(8,128)(2,1)} collective-permute-done((bf16[1024,256]{1,0:T(8,128)(2,1)S(1)}, bf16[1024,256]{1,0:T(8,128)(2,1)}, u32[]{:S(2)}, u32[]{:S(2)}) %collective-permute-start.25) | collective-permute-done | bytes 524320 | tf_op jit(solution)/shard_map/ppermute | solution.py:489
  179.8 1.5 collective-permute-start.28
  181.3 8.3 %collective-permute-done.26.refs_7_ = bf16[1024,256]{1,0:T(8,128)(2,1)} collective-permute-done((bf16[1024,256]{1,0:T(8,128)(2,1)S(1)}, bf16[1024,256]{1,0:T(8,128)(2,1)}, u32[]{:S(2)}, u32[]{:S(2)}) %collective-permute-start.26) | collective-permute-done | bytes 524320 | tf_op jit(solution)/shard_map/ppermute | solution.py:489
  189.6 1.5 collective-permute-start.29
  191.0 7.6 %attention_near.1 = (f32[256,2048]{1,0:T(8,128)S(1)}, f32[16,256,2]{2,1,0:T(8,128)S(1)}) custom-call(bf16[256,2048]{1,0:T(8,128)(2,1)} %q_ref.3, bf16[16,2,16,2048]{3,2,1,0:T(8,128)(2,1)} %copy-done.23, bf16[256,2048]{1,0:T(8,128)(2,1)} %lk_ref.1, bf16[256,2048]{1,0:T(8,128)(2,1)} %lv_ref.1), custom_call_target="tpu_custom_call" | custom-call | flops 2684354560 | bytes 8388608 | tf_op jit(solution)/shard_map/attention_near/pallas_call | solution.py:237
  202.1 2.1 collective-permute-start.30
  204.3 10.9 %attention_scores.1 = (bf16[256,4096]{1,0:T(8,128)(2,1)S(1)}, f32[256,2048]{1,0:T(8,128)S(1)}) custom-call(s32[256]{0:T(256)S(1)} %get-tuple-element.66.cell_ref, bf16[256,2048]{1,0:T(8,128)(2,1)} %q_ref.3, bf16[128,64,128]{2,1,0:T(8,128)(2,1)S(1)} %bitcast.19, f32[256,2048]{1,0:T(8,128)} %copy-done, f32[16,256,2]{2,1,0:T(8,128)} %copy-done.1), custom_call_target="tpu_custom_call" | custom-call | flops 1073741824 | bytes 8388608 | tf_op jit(solution)/shard_map/attention_scores/pallas_call | solution.py:272
  215.2 5.3 %attention_values.1 = (bf16[128,2048]{1,0:T(8,128)(2,1)S(1)}, bf16[128,2048]{1,0:T(8,128)(2,1)S(1)}) custom-call(s32[256]{0:T(256)S(1)} %get-tuple-element.65.cell_ref, bf16[256,4096]{1,0:T(8,128)(2,1)S(1)} %get-tuple-element.37.weight_ref, f32[256,2048]{1,0:T(8,128)S(1)} %get-tuple-element.38.acc_ref, bf16[8,64,128]{2,1,0:T(8,128)(2,1)S(1)} %copy-done.3, ...), custom_call_target="tpu_custom_call" | custom-call | flops 536870912 | bytes 6291456 | tf_op jit(solution)/shard_map/attention_values/pallas_call | solution.py:313
  220.8 2.7 %collective-permute-start.34 = (bf16[128,2048]{1,0:T(8,128)(2,1)S(1)}, bf16[128,2048]{1,0:T(8,128)(2,1)S(1)}, u32[]{:S(2)}, u32[]{:S(2)}) collective-permute-start(bf16[128,2048]{1,0:T(8,128)(2,1)S(1)} %get-tuple-element.56.refs_1_), channel_id=1, source_target_pairs={{0,2},{2,0},{4,6},{6,4},{8,10},{10,8},{12,14},{14,12},{16,18},{18,... | collective-permute-start | bytes 1572872 | tf_op jit(solution)/shard_map/ppermute | solution.py:479
  223.4 1.5 collective-permute-start.31
  226.3 8.0 %collective-permute-done.37.refs_0_ = bf16[128,2048]{1,0:T(8,128)(2,1)S(1)} collective-permute-done((bf16[128,2048]{1,0:T(8,128)(2,1)S(1)}, bf16[128,2048]{1,0:T(8,128)(2,1)S(1)}, u32[]{:S(2)}, u32[]{:S(2)}) %collective-permute-start.37) | collective-permute-done | bytes 524320 | tf_op jit(solution)/shard_map/ppermute | solution.py:479
  234.3 1.9 collective-permute-start.41
  236.2 2.0 collective-permute-start.42
  239.0 2.7 %pick.1.refs_2_ = bf16[4,2048,256]{2,1,0:T(8,128)(2,1)S(1)} custom-call(s32[4]{0:T(128)S(1)} %copy-done.12, bf16[2048,256]{1,0:T(8,128)(2,1)} %refs_0_.1, bf16[2048,256]{1,0:T(8,128)(2,1)} %collective-permute-done.20.refs_1_, bf16[2048,256]{1,0:T(8,128)(2,1)} %collective-permute-done.21.refs_2_, bf16[2048,256]{1,0:T(8,128)(2,1)} %collective-permute-done.22.refs_3_, ...), custom_call_target="tpu_custom_call" | custom-call | flops 134217728 | bytes 8388608 | tf_op jit(solution)/shard_map/pick/pallas_call | solution.py:367
  249.1 1.8 collective-permute-start.36
  253.0 5.4 %collective-permute-done.36.refs_1_ = bf16[256,512]{1,0:T(8,128)(2,1)S(1)} collective-permute-done((bf16[256,512]{1,0:T(8,128)(2,1)S(1)}, bf16[256,512]{1,0:T(8,128)(2,1)S(1)}, u32[]{:S(2)}, u32[]{:S(2)}) %collective-permute-start.36) | collective-permute-done | bytes 262176 | tf_op jit(solution)/shard_map/ppermute | solution.py:479
  258.4 6.5 %collective-permute-done.40.refs_2_ = bf16[256,512]{1,0:T(8,128)(2,1)S(1)} collective-permute-done((bf16[256,512]{1,0:T(8,128)(2,1)S(1)}, bf16[256,512]{1,0:T(8,128)(2,1)S(1)}, u32[]{:S(2)}, u32[]{:S(2)}) %collective-permute-start.40) | collective-permute-done | bytes 262176 | tf_op jit(solution)/shard_map/ppermute | solution.py:479
  265.6 2.5 assemble.1
  (153 shorter events, 39.8 us)
Async XLA Ops:
  21.1 183.1 %all-to-all-start.1 = ((bf16[16,8,64,128]{3,2,1,0:T(8,128)(2,1)}), bf16[16,8,64,128]{3,2,1,0:T(8,128)(2,1)S(1)}, u32[]{:S(2)}, u32[]{:S(2)}) async-start(bf16[16,8,64,128]{3,2,1,0:T(8,128)(2,1)} %bitcast.24), calls=%async_computation.1 | async-start | bytes 4194304 | tf_op jit(solution)/shard_map/all_to_all | solution.py:521
  26.4 54.7 %collective-permute-start = (bf16[1,2,16,2048]{3,2,1,0:T(8,128)(2,1)S(1)}, bf16[1,2,16,2048]{3,2,1,0:T(8,128)(2,1)S(1)}, u32[]{:S(2)}, u32[]{:S(2)}) collective-permute-start(bf16[1,2,16,2048]{3,2,1,0:T(8,128)(2,1)S(1)} %maximum_bitcast_fusion), channel_id=1, source_target_pairs={{0,8},{2,10},{4,12},{6,14},{8,16},{10,18},{12,20},{14,22},{16,24},... | collective-permute-start | bytes 393224 | tf_op jit(solution)/shard_map/ppermute | solution.py:515
  27.9 56.0 %collective-permute-start.1 = (bf16[1,2,16,2048]{3,2,1,0:T(8,128)(2,1)S(1)}, bf16[1,2,16,2048]{3,2,1,0:T(8,128)(2,1)S(1)}, u32[]{:S(2)}, u32[]{:S(2)}) collective-permute-start(bf16[1,2,16,2048]{3,2,1,0:T(8,128)(2,1)S(1)} %maximum_bitcast_fusion), channel_id=1, source_target_pairs={{0,16},{2,18},{4,20},{6,22},{8,24},{10,26},{12,28},{14,30},{16,0},... | collective-permute-start | bytes 393224 | tf_op jit(solution)/shard_map/ppermute | solution.py:515
  29.0 55.3 %collective-permute-start.2 = (bf16[1,2,16,2048]{3,2,1,0:T(8,128)(2,1)S(1)}, bf16[1,2,16,2048]{3,2,1,0:T(8,128)(2,1)S(1)}, u32[]{:S(2)}, u32[]{:S(2)}) collective-permute-start(bf16[1,2,16,2048]{3,2,1,0:T(8,128)(2,1)S(1)} %maximum_bitcast_fusion), channel_id=1, source_target_pairs={{0,24},{2,26},{4,28},{6,30},{8,0},{10,2},{12,4},{14,6},{16,8},{18,... | collective-permute-start | bytes 393224 | tf_op jit(solution)/shard_map/ppermute | solution.py:515
  30.8 100.6 %collective-permute-start.20 = (bf16[2048,256]{1,0:T(8,128)(2,1)}, bf16[2048,256]{1,0:T(8,128)(2,1)}, u32[]{:S(2)}, u32[]{:S(2)}) collective-permute-start(bf16[2048,256]{1,0:T(8,128)(2,1)} %refs_0_.1), channel_id=1, source_target_pairs={{0,8},{2,10},{4,12},{6,14},{8,16},{10,18},{12,20},{14,22},{16,24},... | collective-permute-start | bytes 3145736 | tf_op jit(solution)/shard_map/ppermute | solution.py:489
  32.9 134.0 %collective-permute-start.21 = (bf16[2048,256]{1,0:T(8,128)(2,1)}, bf16[2048,256]{1,0:T(8,128)(2,1)}, u32[]{:S(2)}, u32[]{:S(2)}) collective-permute-start(bf16[2048,256]{1,0:T(8,128)(2,1)} %refs_0_.1), channel_id=1, source_target_pairs={{8,0},{10,2},{12,4},{14,6},{16,8},{18,10},{20,12},{22,14},{24,16},... | collective-permute-start | bytes 3145736 | tf_op jit(solution)/shard_map/ppermute | solution.py:489
  43.0 84.1 %copy-start.28 = (bf16[8,64,128]{2,1,0:T(8,128)(2,1)S(1)}, bf16[8,64,128]{2,1,0:T(8,128)(2,1)}, u32[]{:S(2)}) copy-start(bf16[8,64,128]{2,1,0:T(8,128)(2,1)} %get-tuple-element.50) | copy-start | bytes 393220
  43.0 88.4 %copy-start.27 = (bf16[8,64,128]{2,1,0:T(8,128)(2,1)S(1)}, bf16[8,64,128]{2,1,0:T(8,128)(2,1)}, u32[]{:S(2)}) copy-start(bf16[8,64,128]{2,1,0:T(8,128)(2,1)} %get-tuple-element.51) | copy-start | bytes 393220
  81.0 6.2 %collective-permute-start.5 = (bf16[8,64,128]{2,1,0:T(8,128)(2,1)}, bf16[8,64,128]{2,1,0:T(8,128)(2,1)S(1)}, u32[]{:S(2)}, u32[]{:S(2)}) collective-permute-start(bf16[8,64,128]{2,1,0:T(8,128)(2,1)} %get-tuple-element.40), channel_id=1, source_target_pairs={{0,2},{2,0},{4,6},{6,4},{8,10},{10,8},{12,14},{14,12},{16,18},{18,... | collective-permute-start | bytes 393224 | tf_op jit(solution)/shard_map/ppermute | solution.py:479
  83.9 5.3 %collective-permute-start.6 = (bf16[8,64,128]{2,1,0:T(8,128)(2,1)}, bf16[8,64,128]{2,1,0:T(8,128)(2,1)S(1)}, u32[]{:S(2)}, u32[]{:S(2)}) collective-permute-start(bf16[8,64,128]{2,1,0:T(8,128)(2,1)} %get-tuple-element.41), channel_id=1, source_target_pairs={{0,4},{2,6},{4,0},{6,2},{8,12},{10,14},{12,8},{14,10},{16,20},{18,... | collective-permute-start | bytes 393224 | tf_op jit(solution)/shard_map/ppermute | solution.py:479
  84.3 28.2 %collective-permute-start.3 = (bf16[4,2,16,2048]{3,2,1,0:T(8,128)(2,1)S(1)}, bf16[4,2,16,2048]{3,2,1,0:T(8,128)(2,1)S(1)}, u32[]{:S(2)}, u32[]{:S(2)}) collective-permute-start(bf16[4,2,16,2048]{3,2,1,0:T(8,128)(2,1)S(1)} %pad_maximum_fusion), channel_id=1, source_target_pairs={{0,2},{2,0},{4,6},{6,4},{8,10},{10,8},{12,14},{14,12},{16,18},{18,... | collective-permute-start | bytes 1572872 | tf_op jit(solution)/shard_map/ppermute | solution.py:479
  87.3 13.9 %collective-permute-start.7 = (bf16[8,64,128]{2,1,0:T(8,128)(2,1)}, bf16[8,64,128]{2,1,0:T(8,128)(2,1)S(1)}, u32[]{:S(2)}, u32[]{:S(2)}) collective-permute-start(bf16[8,64,128]{2,1,0:T(8,128)(2,1)} %get-tuple-element.42), channel_id=1, source_target_pairs={{0,6},{2,4},{4,2},{6,0},{8,14},{10,12},{12,10},{14,8},{16,22},{18,... | collective-permute-start | bytes 393224 | tf_op jit(solution)/shard_map/ppermute | solution.py:479
  89.1 12.1 %collective-permute-start.8 = (bf16[8,64,128]{2,1,0:T(8,128)(2,1)}, bf16[8,64,128]{2,1,0:T(8,128)(2,1)S(1)}, u32[]{:S(2)}, u32[]{:S(2)}) collective-permute-start(bf16[8,64,128]{2,1,0:T(8,128)(2,1)} %get-tuple-element.43), channel_id=1, source_target_pairs={{0,8},{2,10},{4,12},{6,14},{8,0},{10,2},{12,4},{14,6},{16,24},{18,... | collective-permute-start | bytes 393224 | tf_op jit(solution)/shard_map/ppermute | solution.py:479
  101.2 6.1 %collective-permute-start.9 = (bf16[8,64,128]{2,1,0:T(8,128)(2,1)}, bf16[8,64,128]{2,1,0:T(8,128)(2,1)S(1)}, u32[]{:S(2)}, u32[]{:S(2)}) collective-permute-start(bf16[8,64,128]{2,1,0:T(8,128)(2,1)} %get-tuple-element.44), channel_id=1, source_target_pairs={{0,10},{2,8},{4,14},{6,12},{8,2},{10,0},{12,6},{14,4},{16,26},{18,... | collective-permute-start | bytes 393224 | tf_op jit(solution)/shard_map/ppermute | solution.py:479
  101.2 9.0 %collective-permute-start.10 = (bf16[8,64,128]{2,1,0:T(8,128)(2,1)}, bf16[8,64,128]{2,1,0:T(8,128)(2,1)S(1)}, u32[]{:S(2)}, u32[]{:S(2)}) collective-permute-start(bf16[8,64,128]{2,1,0:T(8,128)(2,1)} %get-tuple-element.45), channel_id=1, source_target_pairs={{0,12},{2,14},{4,8},{6,10},{8,4},{10,6},{12,0},{14,2},{16,28},{18,... | collective-permute-start | bytes 393224 | tf_op jit(solution)/shard_map/ppermute | solution.py:479
  107.3 7.3 %collective-permute-start.11 = (bf16[8,64,128]{2,1,0:T(8,128)(2,1)S(1)}, bf16[8,64,128]{2,1,0:T(8,128)(2,1)S(1)}, u32[]{:S(2)}, u32[]{:S(2)}) collective-permute-start(bf16[8,64,128]{2,1,0:T(8,128)(2,1)S(1)} %copy-done.32), channel_id=1, source_target_pairs={{0,14},{2,12},{4,10},{6,8},{8,6},{10,4},{12,2},{14,0},{16,30},{18,... | collective-permute-start | bytes 393224 | tf_op jit(solution)/shard_map/ppermute | solution.py:479
  110.2 11.3 %collective-permute-start.12 = (bf16[8,64,128]{2,1,0:T(8,128)(2,1)S(1)}, bf16[8,64,128]{2,1,0:T(8,128)(2,1)S(1)}, u32[]{:S(2)}, u32[]{:S(2)}) collective-permute-start(bf16[8,64,128]{2,1,0:T(8,128)(2,1)S(1)} %copy-done.31), channel_id=1, source_target_pairs={{0,16},{2,18},{4,20},{6,22},{8,24},{10,26},{12,28},{14,30},{16,0},... | collective-permute-start | bytes 393224 | tf_op jit(solution)/shard_map/ppermute | solution.py:479
  112.6 14.5 %collective-permute-start.13 = (bf16[8,64,128]{2,1,0:T(8,128)(2,1)S(1)}, bf16[8,64,128]{2,1,0:T(8,128)(2,1)S(1)}, u32[]{:S(2)}, u32[]{:S(2)}) collective-permute-start(bf16[8,64,128]{2,1,0:T(8,128)(2,1)S(1)} %copy-done.30), channel_id=1, source_target_pairs={{0,18},{2,16},{4,22},{6,20},{8,26},{10,24},{12,30},{14,28},{16,2},... | collective-permute-start | bytes 393224 | tf_op jit(solution)/shard_map/ppermute | solution.py:479
  114.6 60.7 %collective-permute-start.4 = (bf16[8,2,16,2048]{3,2,1,0:T(8,128)(2,1)}, bf16[8,2,16,2048]{3,2,1,0:T(8,128)(2,1)S(1)}, u32[]{:S(2)}, u32[]{:S(2)}) collective-permute-start(bf16[8,2,16,2048]{3,2,1,0:T(8,128)(2,1)} %get-tuple-element.71), channel_id=1, source_target_pairs={{0,4},{2,6},{4,0},{6,2},{8,12},{10,14},{12,8},{14,10},{16,20},{18,... | collective-permute-start | bytes 3145736 | tf_op jit(solution)/shard_map/ppermute | solution.py:479
  121.4 12.1 %collective-permute-start.14 = (bf16[8,64,128]{2,1,0:T(8,128)(2,1)S(1)}, bf16[8,64,128]{2,1,0:T(8,128)(2,1)S(1)}, u32[]{:S(2)}, u32[]{:S(2)}) collective-permute-start(bf16[8,64,128]{2,1,0:T(8,128)(2,1)S(1)} %copy-done.29), channel_id=1, source_target_pairs={{0,20},{2,22},{4,16},{6,18},{8,28},{10,30},{12,24},{14,26},{16,4},... | collective-permute-start | bytes 393224 | tf_op jit(solution)/shard_map/ppermute | solution.py:479
  127.0 12.2 %collective-permute-start.15 = (bf16[8,64,128]{2,1,0:T(8,128)(2,1)S(1)}, bf16[8,64,128]{2,1,0:T(8,128)(2,1)S(1)}, u32[]{:S(2)}, u32[]{:S(2)}) collective-permute-start(bf16[8,64,128]{2,1,0:T(8,128)(2,1)S(1)} %copy-done.28), channel_id=1, source_target_pairs={{0,22},{2,20},{4,18},{6,16},{8,30},{10,28},{12,26},{14,24},{16,6},... | collective-permute-start | bytes 393224 | tf_op jit(solution)/shard_map/ppermute | solution.py:479
  131.4 12.0 %collective-permute-start.16 = (bf16[8,64,128]{2,1,0:T(8,128)(2,1)S(1)}, bf16[8,64,128]{2,1,0:T(8,128)(2,1)S(1)}, u32[]{:S(2)}, u32[]{:S(2)}) collective-permute-start(bf16[8,64,128]{2,1,0:T(8,128)(2,1)S(1)} %copy-done.27), channel_id=1, source_target_pairs={{0,24},{2,26},{4,28},{6,30},{8,16},{10,18},{12,20},{14,22},{16,8},... | collective-permute-start | bytes 393224 | tf_op jit(solution)/shard_map/ppermute | solution.py:479
  133.5 40.4 %collective-permute-start.24 = (bf16[1024,256]{1,0:T(8,128)(2,1)S(1)}, bf16[1024,256]{1,0:T(8,128)(2,1)}, u32[]{:S(2)}, u32[]{:S(2)}) collective-permute-start(bf16[1024,256]{1,0:T(8,128)(2,1)S(1)} %get-tuple-element.70), channel_id=1, source_target_pairs={{8,16},{10,18},{12,20},{14,22},{9,17},{11,19},{13,21},{15,23}} | collective-permute-start | bytes 1572872 | tf_op jit(solution)/shard_map/ppermute | solution.py:489
  139.2 21.1 %collective-permute-start.17 = (bf16[8,64,128]{2,1,0:T(8,128)(2,1)S(1)}, bf16[8,64,128]{2,1,0:T(8,128)(2,1)S(1)}, u32[]{:S(2)}, u32[]{:S(2)}) collective-permute-start(bf16[8,64,128]{2,1,0:T(8,128)(2,1)S(1)} %copy-done.26), channel_id=1, source_target_pairs={{0,26},{2,24},{4,30},{6,28},{8,18},{10,16},{12,22},{14,20},{16,10}... | collective-permute-start | bytes 393224 | tf_op jit(solution)/shard_map/ppermute | solution.py:479
  143.4 21.2 %collective-permute-start.18 = (bf16[8,64,128]{2,1,0:T(8,128)(2,1)S(1)}, bf16[8,64,128]{2,1,0:T(8,128)(2,1)S(1)}, u32[]{:S(2)}, u32[]{:S(2)}) collective-permute-start(bf16[8,64,128]{2,1,0:T(8,128)(2,1)S(1)} %copy-done.25), channel_id=1, source_target_pairs={{0,28},{2,30},{4,24},{6,26},{8,20},{10,22},{12,16},{14,18},{16,12}... | collective-permute-start | bytes 393224 | tf_op jit(solution)/shard_map/ppermute | solution.py:479
  161.0 9.5 %collective-permute-start.19 = (bf16[8,64,128]{2,1,0:T(8,128)(2,1)S(1)}, bf16[8,64,128]{2,1,0:T(8,128)(2,1)S(1)}, u32[]{:S(2)}, u32[]{:S(2)}) collective-permute-start(bf16[8,64,128]{2,1,0:T(8,128)(2,1)S(1)} %copy-done.24), channel_id=1, source_target_pairs={{0,30},{2,28},{4,26},{6,24},{8,22},{10,20},{12,18},{14,16},{16,14}... | collective-permute-start | bytes 393224 | tf_op jit(solution)/shard_map/ppermute | solution.py:479
  165.3 55.3 %collective-permute-start.22 = (bf16[2048,256]{1,0:T(8,128)(2,1)}, bf16[2048,256]{1,0:T(8,128)(2,1)}, u32[]{:S(2)}, u32[]{:S(2)}) collective-permute-start(bf16[2048,256]{1,0:T(8,128)(2,1)} %collective-permute-done.20.refs_1_), channel_id=1, source_target_pairs={{16,24},{18,26},{20,28},{22,30},{17,25},{19,27},{21,29},{23,31}} | collective-permute-start | bytes 3145736 | tf_op jit(solution)/shard_map/ppermute | solution.py:489
  166.9 53.8 %collective-permute-start.23 = (bf16[2048,256]{1,0:T(8,128)(2,1)}, bf16[2048,256]{1,0:T(8,128)(2,1)}, u32[]{:S(2)}, u32[]{:S(2)}) collective-permute-start(bf16[2048,256]{1,0:T(8,128)(2,1)} %collective-permute-done.21.refs_2_), channel_id=1, source_target_pairs={{8,0},{10,2},{12,4},{14,6},{9,1},{11,3},{13,5},{15,7}} | collective-permute-start | bytes 3145736 | tf_op jit(solution)/shard_map/ppermute | solution.py:489
  170.5 9.3 %collective-permute-start.25 = (bf16[1024,256]{1,0:T(8,128)(2,1)S(1)}, bf16[1024,256]{1,0:T(8,128)(2,1)}, u32[]{:S(2)}, u32[]{:S(2)}) collective-permute-start(bf16[1024,256]{1,0:T(8,128)(2,1)S(1)} %get-tuple-element.69), channel_id=1, source_target_pairs={{8,16},{10,18},{12,20},{14,22},{9,17},{11,19},{13,21},{15,23}} | collective-permute-start | bytes 1572872 | tf_op jit(solution)/shard_map/ppermute | solution.py:489
  173.9 15.6 %collective-permute-start.26 = (bf16[1024,256]{1,0:T(8,128)(2,1)S(1)}, bf16[1024,256]{1,0:T(8,128)(2,1)}, u32[]{:S(2)}, u32[]{:S(2)}) collective-permute-start(bf16[1024,256]{1,0:T(8,128)(2,1)S(1)} %get-tuple-element.68), channel_id=1, source_target_pairs={{16,8},{18,10},{20,12},{22,14},{17,9},{19,11},{21,13},{23,15}} | collective-permute-start | bytes 1572872 | tf_op jit(solution)/shard_map/ppermute | solution.py:489
  175.2 26.1 %collective-permute-start.27 = (bf16[1024,256]{1,0:T(8,128)(2,1)S(1)}, bf16[1024,256]{1,0:T(8,128)(2,1)S(1)}, u32[]{:S(2)}, u32[]{:S(2)}) collective-permute-start(bf16[1024,256]{1,0:T(8,128)(2,1)S(1)} %get-tuple-element.67), channel_id=1, source_target_pairs={{16,8},{18,10},{20,12},{22,14},{17,9},{19,11},{21,13},{23,15}} | collective-permute-start | bytes 1572872 | tf_op jit(solution)/shard_map/ppermute | solution.py:489
  179.8 43.6 %collective-permute-start.28 = (bf16[1024,256]{1,0:T(8,128)(2,1)}, bf16[1024,256]{1,0:T(8,128)(2,1)}, u32[]{:S(2)}, u32[]{:S(2)}) collective-permute-start(bf16[1024,256]{1,0:T(8,128)(2,1)} %collective-permute-done.24.refs_5_), channel_id=1, source_target_pairs={{16,24},{18,26},{20,28},{22,30},{17,25},{19,27},{21,29},{23,31}} | collective-permute-start | bytes 1572872 | tf_op jit(solution)/shard_map/ppermute | solution.py:489
  189.6 35.4 %collective-permute-start.29 = (bf16[1024,256]{1,0:T(8,128)(2,1)}, bf16[1024,256]{1,0:T(8,128)(2,1)}, u32[]{:S(2)}, u32[]{:S(2)}) collective-permute-start(bf16[1024,256]{1,0:T(8,128)(2,1)} %collective-permute-done.25.refs_6_), channel_id=1, source_target_pairs={{16,24},{18,26},{20,28},{22,30},{17,25},{19,27},{21,29},{23,31}} | collective-permute-start | bytes 1572872 | tf_op jit(solution)/shard_map/ppermute | solution.py:489
  202.1 22.9 %collective-permute-start.30 = (bf16[1024,256]{1,0:T(8,128)(2,1)}, bf16[1024,256]{1,0:T(8,128)(2,1)}, u32[]{:S(2)}, u32[]{:S(2)}) collective-permute-start(bf16[1024,256]{1,0:T(8,128)(2,1)} %collective-permute-done.26.refs_7_), channel_id=1, source_target_pairs={{8,0},{10,2},{12,4},{14,6},{9,1},{11,3},{13,5},{15,7}} | collective-permute-start | bytes 1572872 | tf_op jit(solution)/shard_map/ppermute | solution.py:489
  220.6 13.7 %collective-permute-start.37 = (bf16[128,2048]{1,0:T(8,128)(2,1)S(1)}, bf16[128,2048]{1,0:T(8,128)(2,1)S(1)}, u32[]{:S(2)}, u32[]{:S(2)}) collective-permute-start(bf16[128,2048]{1,0:T(8,128)(2,1)S(1)} %get-tuple-element.55.refs_0_), channel_id=1, source_target_pairs={{0,4},{2,6},{4,0},{6,2},{8,12},{10,14},{12,8},{14,10},{16,20},{18,... | collective-permute-start | bytes 1572872 | tf_op jit(solution)/shard_map/ppermute | solution.py:479
  220.8 15.5 %collective-permute-start.34 = (bf16[128,2048]{1,0:T(8,128)(2,1)S(1)}, bf16[128,2048]{1,0:T(8,128)(2,1)S(1)}, u32[]{:S(2)}, u32[]{:S(2)}) collective-permute-start(bf16[128,2048]{1,0:T(8,128)(2,1)S(1)} %get-tuple-element.56.refs_1_), channel_id=1, source_target_pairs={{0,2},{2,0},{4,6},{6,4},{8,10},{10,8},{12,14},{14,12},{16,18},{18,... | collective-permute-start | bytes 1572872 | tf_op jit(solution)/shard_map/ppermute | solution.py:479
  223.4 14.7 %collective-permute-start.31 = (bf16[1024,256]{1,0:T(8,128)(2,1)S(1)}, bf16[1024,256]{1,0:T(8,128)(2,1)S(1)}, u32[]{:S(2)}, u32[]{:S(2)}) collective-permute-start(bf16[1024,256]{1,0:T(8,128)(2,1)S(1)} %copy-done.14), channel_id=1, source_target_pairs={{8,0},{10,2},{12,4},{14,6},{9,1},{11,3},{13,5},{15,7}} | collective-permute-start | bytes 1572872 | tf_op jit(solution)/shard_map/ppermute | solution.py:489
  225.0 16.8 %collective-permute-start.33 = (bf16[128,2048]{1,0:T(8,128)(2,1)S(1)}, bf16[128,2048]{1,0:T(8,128)(2,1)S(1)}, u32[]{:S(2)}, u32[]{:S(2)}) collective-permute-start(bf16[128,2048]{1,0:T(8,128)(2,1)S(1)} %get-tuple-element.55.refs_0_), channel_id=1, source_target_pairs={{0,2},{2,0},{4,6},{6,4},{8,10},{10,8},{12,14},{14,12},{16,18},{18,... | collective-permute-start | bytes 1572872 | tf_op jit(solution)/shard_map/ppermute | solution.py:479
  225.0 20.8 %collective-permute-start.38 = (bf16[128,2048]{1,0:T(8,128)(2,1)S(1)}, bf16[128,2048]{1,0:T(8,128)(2,1)S(1)}, u32[]{:S(2)}, u32[]{:S(2)}) collective-permute-start(bf16[128,2048]{1,0:T(8,128)(2,1)S(1)} %get-tuple-element.56.refs_1_), channel_id=1, source_target_pairs={{0,4},{2,6},{4,0},{6,2},{8,12},{10,14},{12,8},{14,10},{16,20},{18,... | collective-permute-start | bytes 1572872 | tf_op jit(solution)/shard_map/ppermute | solution.py:479
  234.3 13.1 %collective-permute-start.41 = (bf16[128,2048]{1,0:T(8,128)(2,1)S(1)}, bf16[128,2048]{1,0:T(8,128)(2,1)S(1)}, u32[]{:S(2)}, u32[]{:S(2)}) collective-permute-start(bf16[128,2048]{1,0:T(8,128)(2,1)S(1)} %collective-permute-done.37.refs_0_), channel_id=1, source_target_pairs={{0,2},{2,0},{4,6},{6,4},{8,10},{10,8},{12,14},{14,12},{16,18},{18,... | collective-permute-start | bytes 1572872 | tf_op jit(solution)/shard_map/ppermute | solution.py:479
  236.2 11.2 %collective-permute-start.42 = (bf16[128,2048]{1,0:T(8,128)(2,1)S(1)}, bf16[128,2048]{1,0:T(8,128)(2,1)S(1)}, u32[]{:S(2)}, u32[]{:S(2)}) collective-permute-start(bf16[128,2048]{1,0:T(8,128)(2,1)S(1)} %collective-permute-done.34.refs_1_), channel_id=1, source_target_pairs={{0,4},{2,6},{4,0},{6,2},{8,12},{10,14},{12,8},{14,10},{16,20},{18,... | collective-permute-start | bytes 1572872 | tf_op jit(solution)/shard_map/ppermute | solution.py:479
  243.1 5.9 %collective-permute-start.35 = (bf16[256,512]{1,0:T(8,128)(2,1)S(1)}, bf16[256,512]{1,0:T(8,128)(2,1)S(1)}, u32[]{:S(2)}, u32[]{:S(2)}) collective-permute-start(bf16[256,512]{1,0:T(8,128)(2,1)S(1)} %bitcast.21), channel_id=1, source_target_pairs={{0,1},{1,0},{2,3},{3,2},{4,5},{5,4},{6,7},{7,6},{8,9},{9,8},{10,11... | collective-permute-start | bytes 786440 | tf_op jit(solution)/shard_map/ppermute | solution.py:559
  245.3 7.6 %collective-permute-start.32 = (bf16[256,512]{1,0:T(8,128)(2,1)S(1)}, bf16[256,512]{1,0:T(8,128)(2,1)S(1)}, u32[]{:S(2)}, u32[]{:S(2)}) collective-permute-start(bf16[256,512]{1,0:T(8,128)(2,1)S(1)} %bitcast.20), channel_id=1, source_target_pairs={{0,1},{1,0},{2,3},{3,2},{4,5},{5,4},{6,7},{7,6},{8,9},{9,8},{10,11... | collective-permute-start | bytes 786440 | tf_op jit(solution)/shard_map/ppermute | solution.py:559
  247.1 3.8 %collective-permute-start.39 = (bf16[256,512]{1,0:T(8,128)(2,1)S(1)}, bf16[256,512]{1,0:T(8,128)(2,1)S(1)}, u32[]{:S(2)}, u32[]{:S(2)}) collective-permute-start(bf16[256,512]{1,0:T(8,128)(2,1)S(1)} %bitcast.22), channel_id=1, source_target_pairs={{0,1},{1,0},{2,3},{3,2},{4,5},{5,4},{6,7},{7,6},{8,9},{9,8},{10,11... | collective-permute-start | bytes 786440 | tf_op jit(solution)/shard_map/ppermute | solution.py:559
  248.7 2.8 %collective-permute-start.43 = (bf16[256,512]{1,0:T(8,128)(2,1)S(1)}, bf16[256,512]{1,0:T(8,128)(2,1)S(1)}, u32[]{:S(2)}, u32[]{:S(2)}) collective-permute-start(bf16[256,512]{1,0:T(8,128)(2,1)S(1)} %bitcast.23), channel_id=1, source_target_pairs={{0,1},{1,0},{2,3},{3,2},{4,5},{5,4},{6,7},{7,6},{8,9},{9,8},{10,11... | collective-permute-start | bytes 786440 | tf_op jit(solution)/shard_map/ppermute | solution.py:559
  249.1 9.2 %collective-permute-start.36 = (bf16[256,512]{1,0:T(8,128)(2,1)S(1)}, bf16[256,512]{1,0:T(8,128)(2,1)S(1)}, u32[]{:S(2)}, u32[]{:S(2)}) collective-permute-start(bf16[256,512]{1,0:T(8,128)(2,1)S(1)} %add_convert_fusion.2), channel_id=1, source_target_pairs={{0,2},{2,0},{4,6},{6,4},{8,10},{10,8},{12,14},{14,12},{16,18},{18,... | collective-permute-start | bytes 786440 | tf_op jit(solution)/shard_map/ppermute | solution.py:479
  251.0 13.8 %collective-permute-start.40 = (bf16[256,512]{1,0:T(8,128)(2,1)S(1)}, bf16[256,512]{1,0:T(8,128)(2,1)S(1)}, u32[]{:S(2)}, u32[]{:S(2)}) collective-permute-start(bf16[256,512]{1,0:T(8,128)(2,1)S(1)} %add_convert_fusion.1), channel_id=1, source_target_pairs={{0,4},{2,6},{4,0},{6,2},{8,12},{10,14},{12,8},{14,10},{16,20},{18,... | collective-permute-start | bytes 786440 | tf_op jit(solution)/shard_map/ppermute | solution.py:479
  251.5 13.3 %collective-permute-start.44 = (bf16[256,512]{1,0:T(8,128)(2,1)S(1)}, bf16[256,512]{1,0:T(8,128)(2,1)S(1)}, u32[]{:S(2)}, u32[]{:S(2)}) collective-permute-start(bf16[256,512]{1,0:T(8,128)(2,1)S(1)} %add_convert_fusion), channel_id=1, source_target_pairs={{0,6},{2,4},{4,2},{6,0},{8,14},{10,12},{12,10},{14,8},{16,22},{18,... | collective-permute-start | bytes 786440 | tf_op jit(solution)/shard_map/ppermute | solution.py:479
  (31 other events, 688.8 us)
